TPU v7x, 32 devices: a whole 2x2x4 slice. The times are simulated.
32 devices in a mesh: row: 4 (over z), col: 8 (over y, x, core).
Axes of the slice: x: 2, y: 2, z: 4, core: 2. Of those that a mesh axis runs over, the one named last changes fastest.
Arguments:
- layer_in: bfloat16 [2, 4096, 2048], P(None, ('row', 'col')), may hold values from -6 to 6
- earlier_outs: bfloat16 [4, 2, 4096, 2048], P(None, None, ('row', 'col')), may hold values from -6 to 6
- cotangent: bfloat16 [2, 4096, 2048], P(None, ('row', 'col')), may hold values from -6 to 6
- segments: int32 [2, 4096], P(None, 'row'), may hold values from 0 to 4095, as said below
- positions: int32 [2, 4096], P(None, 'row'), may hold values from 0 to 2044, as said below
- w_qkv: bfloat16 [3, 2048, 2048], P(None, 'row', 'col'), may hold values from -0.125 to 0.125
- w_out: bfloat16 [2048, 2048], P('col', 'row'), may hold values from -0.5 to 0.5
- w_up: bfloat16 [2048, 8192], P('row', 'col'), may hold values from -0.125 to 0.125
- w_down: bfloat16 [8192, 2048], P('col', 'row'), may hold values from -0.0625 to 0.0625
- ln_gains: bfloat16 [2, 2048], P(None, 'row'), may hold values from 0.25 to 1.75
- ln_biases: bfloat16 [2, 2048], P(None, 'row'), may hold values from -1.5 to 1.5
- dwa_weights: float32 [5], replicated, may hold values from 0.3 to 1
Outputs:
- out: bfloat16 [2, 4096, 2048], P(None, ('row', 'col'))
- grad_in: float32 [2, 4096, 2048], P(None, ('row', 'col'))
- grad_earlier: float32 [4, 2, 4096, 2048], P(None, None, ('row', 'col'))
- grad_w_qkv: float32 [3, 2048, 2048], P(None, 'row', 'col')
- grad_w_out: float32 [2048, 2048], P('col', 'row')
- grad_w_up: float32 [2048, 8192], P('row', 'col')
- grad_w_down: float32 [8192, 2048], P('col', 'row')
- grad_gains: float32 [2, 2048], P(None, 'row')
- grad_biases: float32 [2, 2048], P(None, 'row')
- grad_dwa: float32 [5], replicated
Inputs may be any that keep to these rules, and one draw needn't show every extreme that they name: `segments`: each aligned run of 1024 tokens of a micro-batch is a sequence whose first and last tokens start documents; a token's number is the index, within its micro-batch, of the first token of its document, so numbers never fall within a sequence. `positions`: 0 at the first token of each document, rising by 1 or 2 from one token to the next within it.
All inputs are finite; a program needn't handle non-finite values.
Results may differ from a plain program's by a relative error of at most 0.014.
Values may be sent and summed in bfloat16 or wider, within the bound.
No kernel may reach another device: no remote copies, remote signals or barrier semaphores. Data moves between devices by JAX's collectives and lax.ppermute only.
A program may use at most 448 MiB of HBM per device.

v0:
```python
import math

import jax
import jax.numpy as jnp
from jax import lax
from jax.sharding import PartitionSpec as P

HEAD = 64
SEQ_MIN = 1024
SEQ_DEV = 64


EPSILON = 1e-05
NEG_FILL = -1e30
F32 = jnp.float32
B16 = jnp.bfloat16


def gelu_exact(values):
    return jax.nn.gelu(values, approximate=False)


def gelu_back(pre_act, grad_hidden):
    return jax.vjp(gelu_exact, pre_act)[1](grad_hidden)[0]


def normalize(values):
    centre = values - jnp.mean(values, axis=-1, keepdims=True)
    spread = lax.rsqrt(jnp.mean(centre * centre, axis=-1, keepdims=True) + EPSILON)
    return (centre * spread, spread)


def norm_back(grad_normed, scaled, spread, ln_gain):
    shaped = grad_normed * ln_gain
    return spread * (
        shaped
        - jnp.mean(shaped, axis=-1, keepdims=True)
        - scaled * jnp.mean(shaped * scaled, axis=-1, keepdims=True)
    )


def rotary_tables(places):
    half_size = HEAD // 2
    inverse = 10000.0 ** (-(jnp.arange(half_size, dtype=F32) * 2.0) / HEAD)
    angles = places.astype(F32)[:, None] * inverse[None, :]
    return (jnp.cos(angles)[:, None, :], jnp.sin(angles)[:, None, :])


def rotate(values, cos_part, sin_part):
    half_size = values.shape[-1] // 2
    lead_half = values[..., :half_size]
    tail_half = values[..., half_size:]
    return jnp.concatenate(
        [lead_half * cos_part - tail_half * sin_part, tail_half * cos_part + lead_half * sin_part],
        axis=-1,
    )


def rotate_back(grads, cos_part, sin_part):
    half_size = grads.shape[-1] // 2
    lead_half = grads[..., :half_size]
    tail_half = grads[..., half_size:]
    return jnp.concatenate(
        [lead_half * cos_part + tail_half * sin_part, tail_half * cos_part - lead_half * sin_part],
        axis=-1,
    )


def split_blocks(values, block_count, block_rows):
    shaped = values.reshape((values.shape[0], block_count, block_rows) + values.shape[2:])
    return jnp.moveaxis(shaped, 1, 0)


def join_blocks(values):
    moved = jnp.moveaxis(values, 0, 1)
    return moved.reshape((moved.shape[0], moved.shape[1] * moved.shape[2]) + moved.shape[3:])


def block_scores(query_blk, seg_blk, start, key_vecs, seg_ids, score_scale):
    block_rows = query_blk.shape[1]
    raw = (
        jnp.einsum("nqhe,nkhe->nhqk", query_blk, key_vecs, preferred_element_type=F32) * score_scale
    )
    query_pos = start + jnp.arange(block_rows, dtype=jnp.int32)
    key_pos = jnp.arange(key_vecs.shape[1], dtype=jnp.int32)
    doc_mask = (seg_blk[:, :, None] == seg_ids[:, None, :]) & (
        key_pos[None, None, :] <= query_pos[None, :, None]
    )
    return jnp.where(doc_mask[:, None], raw, NEG_FILL)


def body(
    layer_in,
    earlier_outs,
    cotangent,
    segments,
    positions,
    w_qkv,
    w_out,
    w_up,
    w_down,
    ln_gains,
    ln_biases,
    dwa_weights,
):
    micro_count, tok_dev, model_width = layer_in.shape
    prior_count = earlier_outs.shape[0]
    col_count = lax.axis_size("col")
    row_count = lax.axis_size("row")
    seq_len = max(SEQ_MIN, SEQ_DEV * col_count)
    group_rows = tok_dev * col_count
    seq_count = group_rows // seq_len
    heads_here = w_qkv.shape[2] // HEAD
    score_scale = HEAD ** (-0.5)
    head_shape = (group_rows, heads_here, HEAD)
    seq_shape = (seq_count, seq_len, heads_here, HEAD)
    block_rows = math.gcd(512, seq_len)
    block_count = seq_len // block_rows
    starts = jnp.arange(block_count, dtype=jnp.int32) * block_rows
    qkv_full, out_full, up_full, down_full, gain_full, bias_full = (
        lax.all_gather(w_qkv, "row", axis=1, tiled=True),
        lax.all_gather(w_out, "row", axis=1, tiled=True),
        lax.all_gather(w_up, "row", axis=0, tiled=True),
        lax.all_gather(w_down, "row", axis=1, tiled=True),
        lax.all_gather(ln_gains, "row", axis=1, tiled=True),
        lax.all_gather(ln_biases, "row", axis=1, tiled=True),
    )
    ln_gain = gain_full.astype(F32)
    ln_bias = bias_full.astype(F32)
    grad_up = jnp.zeros(up_full.shape, F32)
    grad_down = jnp.zeros(down_full.shape, F32)
    grad_qkv = jnp.zeros(qkv_full.shape, F32)
    grad_wout = jnp.zeros(out_full.shape, F32)
    norm_stats = jnp.zeros((4, model_width), F32)
    mix_grads = jnp.zeros((prior_count + 1,), F32)
    outputs = []
    in_grads = []
    earlier_grads = []
    for micro_step in range(micro_count):
        resid_in = layer_in[micro_step].astype(F32)
        scaled1, spread1 = normalize(resid_in)
        normed1 = (scaled1 * ln_gain[0] + ln_bias[0]).astype(B16)
        rows_one = lax.all_gather(normed1, "col", axis=0, tiled=True)
        qkv_proj = jnp.einsum("sd,jdh->jsh", rows_one, qkv_full, preferred_element_type=F32)
        cos_part, sin_part = rotary_tables(positions[micro_step])
        queries = (
            rotate(qkv_proj[0].reshape(head_shape), cos_part, sin_part)
            .astype(B16)
            .reshape(seq_shape)
        )
        key_vecs = (
            rotate(qkv_proj[1].reshape(head_shape), cos_part, sin_part)
            .astype(B16)
            .reshape(seq_shape)
        )
        val_vecs = qkv_proj[2].astype(B16).reshape(seq_shape)
        seg_ids = segments[micro_step].reshape(seq_count, seq_len)
        query_blocks = split_blocks(queries, block_count, block_rows)
        seg_blocks = split_blocks(seg_ids, block_count, block_rows)

        def forward_block(carry, packed):
            query_blk, seg_blk, start = packed
            scores = block_scores(query_blk, seg_blk, start, key_vecs, seg_ids, score_scale)
            row_max = jnp.max(scores, axis=-1, keepdims=True)
            exp_terms = jnp.exp(scores - row_max)
            row_total = jnp.sum(exp_terms, axis=-1, keepdims=True)
            probs = (exp_terms / row_total).astype(B16)
            att_blk = jnp.einsum(
                "nhqk,nkhe->nqhe", probs, val_vecs, preferred_element_type=F32
            ).astype(B16)
            return (carry, (att_blk, row_max + jnp.log(row_total)))

        unused, (att_blocks, log_totals) = lax.scan(
            forward_block, jnp.zeros((), F32), (query_blocks, seg_blocks, starts)
        )
        attended = join_blocks(att_blocks).reshape(group_rows, heads_here * HEAD)
        mixed = lax.psum_scatter(
            jnp.dot(attended, out_full, preferred_element_type=F32),
            "col",
            scatter_dimension=0,
            tiled=True,
        )
        resid = resid_in + mixed
        scaled2, spread2 = normalize(resid)
        normed2 = (scaled2 * ln_gain[1] + ln_bias[1]).astype(B16)
        rows_two = lax.all_gather(normed2, "col", axis=0, tiled=True)
        pre_act = jnp.dot(rows_two, up_full, preferred_element_type=F32)
        hidden = gelu_exact(pre_act).astype(B16)
        branch = lax.psum_scatter(
            jnp.dot(hidden, down_full, preferred_element_type=F32).astype(jnp.bfloat16),
            "col",
            scatter_dimension=0,
            tiled=True,
        ).astype(jnp.float32)
        block_out = resid + branch
        earlier = earlier_outs[:, micro_step].astype(F32)
        mix_sum = dwa_weights[0] * earlier[0]
        for level in range(1, prior_count):
            mix_sum = mix_sum + dwa_weights[level] * earlier[level]
        outputs.append((mix_sum + dwa_weights[prior_count] * block_out).astype(B16))
        grad_y = cotangent[micro_step].astype(F32)
        mix_grads = mix_grads + jnp.concatenate(
            [jnp.sum(grad_y[None] * earlier, axis=(1, 2)), jnp.sum(grad_y * block_out)[None]]
        )
        earlier_grads.append(dwa_weights[:prior_count, None, None] * grad_y[None])
        grad_block = dwa_weights[prior_count] * grad_y
        grad_branch = grad_block.astype(B16)
        grad_rows = lax.all_gather(grad_branch, "col", axis=0, tiled=True)
        grad_hidden = jnp.einsum("sd,fd->sf", grad_rows, down_full, preferred_element_type=F32)
        grad_down = grad_down + jnp.einsum(
            "sf,sd->fd", hidden, grad_rows, preferred_element_type=F32
        )
        grad_pre = gelu_back(pre_act, grad_hidden).astype(B16)
        grad_up = grad_up + jnp.einsum("sd,sf->df", rows_two, grad_pre, preferred_element_type=F32)
        grad_normed2 = lax.psum_scatter(
            jnp.einsum("sf,df->sd", grad_pre, up_full, preferred_element_type=F32),
            "col",
            scatter_dimension=0,
            tiled=True,
        )
        grad_resid = grad_block + norm_back(grad_normed2, scaled2, spread2, ln_gain[1])
        grad_mixed = grad_resid.astype(B16)
        grad_rows_one = lax.all_gather(grad_mixed, "col", axis=0, tiled=True)
        grad_wout = grad_wout + jnp.einsum(
            "sh,sd->hd", attended, grad_rows_one, preferred_element_type=F32
        )
        grad_att = (
            jnp.einsum("sd,hd->sh", grad_rows_one, out_full, preferred_element_type=F32)
            .astype(B16)
            .reshape(seq_shape)
        )
        grad_att_blocks = split_blocks(grad_att, block_count, block_rows)

        def backward_block(carry, packed):
            key_acc, val_acc = carry
            query_blk, grad_att_blk, seg_blk, start, log_total = packed
            fresh_probs = jnp.exp(
                block_scores(query_blk, seg_blk, start, key_vecs, seg_ids, score_scale) - log_total
            )
            probs = fresh_probs.astype(B16)
            val_acc = val_acc + jnp.einsum(
                "nhqk,nqhe->nkhe", probs, grad_att_blk, preferred_element_type=F32
            )
            grad_probs = jnp.einsum(
                "nqhe,nkhe->nhqk", grad_att_blk, val_vecs, preferred_element_type=F32
            )
            row_inner = jnp.sum(fresh_probs * grad_probs, axis=-1, keepdims=True)
            grad_scores = (fresh_probs * (grad_probs - row_inner)).astype(B16)
            query_grad = (
                jnp.einsum("nhqk,nkhe->nqhe", grad_scores, key_vecs, preferred_element_type=F32)
                * score_scale
            )
            key_acc = (
                key_acc
                + jnp.einsum("nhqk,nqhe->nkhe", grad_scores, query_blk, preferred_element_type=F32)
                * score_scale
            )
            return ((key_acc, val_acc), query_grad)

        zero_acc = jnp.zeros(seq_shape, F32)
        (grad_key, grad_val_sum), query_grads = lax.scan(
            backward_block,
            (zero_acc, zero_acc),
            (query_blocks, grad_att_blocks, seg_blocks, starts, log_totals),
        )
        grad_val = grad_val_sum.astype(B16).reshape(group_rows, heads_here * HEAD)
        grad_query = join_blocks(query_grads)
        grad_queries = (
            rotate_back(grad_query.reshape(head_shape), cos_part, sin_part)
            .astype(B16)
            .reshape(group_rows, heads_here * HEAD)
        )
        grad_keys = (
            rotate_back(grad_key.reshape(head_shape), cos_part, sin_part)
            .astype(B16)
            .reshape(group_rows, heads_here * HEAD)
        )
        grad_planes = jnp.stack([grad_queries, grad_keys, grad_val])
        grad_qkv = grad_qkv + jnp.einsum(
            "sd,jsh->jdh", rows_one, grad_planes, preferred_element_type=F32
        )
        grad_normed1 = lax.psum_scatter(
            jnp.einsum("jsh,jdh->sd", grad_planes, qkv_full, preferred_element_type=F32),
            "col",
            scatter_dimension=0,
            tiled=True,
        )
        in_grads.append(grad_resid + norm_back(grad_normed1, scaled1, spread1, ln_gain[0]))
        norm_stats = norm_stats + jnp.stack(
            [
                jnp.sum(grad_normed1 * scaled1, axis=0),
                jnp.sum(grad_normed2 * scaled2, axis=0),
                jnp.sum(grad_normed1, axis=0),
                jnp.sum(grad_normed2, axis=0),
            ]
        )
    grad_qkv, grad_wout, grad_up, grad_down = (
        lax.psum_scatter(grad_qkv, "row", scatter_dimension=1, tiled=True),
        lax.psum_scatter(grad_wout, "row", scatter_dimension=1, tiled=True),
        lax.psum_scatter(grad_up, "row", scatter_dimension=0, tiled=True),
        lax.psum_scatter(grad_down, "row", scatter_dimension=1, tiled=True),
    )
    norm_total, mix_total = lax.psum((norm_stats, mix_grads), ("row", "col"))
    part_width = model_width // row_count
    own_part = lax.dynamic_slice_in_dim(
        norm_total, lax.axis_index("row") * part_width, part_width, 1
    )
    return (
        jnp.stack(outputs),
        jnp.stack(in_grads),
        jnp.stack(earlier_grads, axis=1),
        grad_qkv,
        grad_wout,
        grad_up,
        grad_down,
        own_part[:2],
        own_part[2:],
        mix_total,
    )


def solution(mesh):
    in_specs = (
        P(None, ("row", "col"), None),
        P(None, None, ("row", "col"), None),
        P(None, ("row", "col"), None),
        P(None, "row"),
        P(None, "row"),
        P(None, "row", "col"),
        P("col", "row"),
        P("row", "col"),
        P("col", "row"),
        P(None, "row"),
        P(None, "row"),
        P(),
    )
    out_specs = (
        P(None, ("row", "col"), None),
        P(None, ("row", "col"), None),
        P(None, None, ("row", "col"), None),
        P(None, "row", "col"),
        P("col", "row"),
        P("row", "col"),
        P("col", "row"),
        P(None, "row"),
        P(None, "row"),
        P(),
    )
    return jax.shard_map(body, mesh=mesh, in_specs=in_specs, out_specs=out_specs, check_vma=False)
```

profile of v0, /device:TPU:0, one launch (start us, length us, event | category | flops | bytes accessed | tf_op | source)
XLA Modules:
  0.0 1740.3 jit_solution(16828088820504001090)
XLA Ops:
  9.7 13.8 all_gather.43
  23.5 12.8 all_gather.42
  44.6 31.9 %all-gather.15.cloned.1.call-done = bf16[3,2048,256]{1,2,0:T(8,128)(2,1)} async-done(((bf16[3,512,256]{1,2,0:T(8,128)(2,1)}), bf16[3,2048,256]{1,2,0:T(8,128)(2,1)}) %all-gather.15.cloned.1.call-update) | async-done | bytes 3145744 | tf_op jit(solution)/shard_map/all_gather | solution.py:121
  76.4 37.7 %all-gather.13.cloned.1.call-done = bf16[1024,2048]{1,0:T(8,128)(2,1)} async-done(((bf16[128,2048]{1,0:T(8,128)(2,1)}), bf16[1024,2048]{1,0:T(8,128)(2,1)}) %all-gather.13.cloned.1.call-update) | async-done | bytes 4194320 | tf_op jit(solution)/shard_map/all_gather | solution.py:143
  114.2 6.2 fusion.120
  125.3 19.8 %while.54 = (s32[]{:T(128)}, bf16[2,1,512,4,64]{2,4,3,1,0:T(8,128)(2,1)S(1)}, f32[2,1,4,512,1]{3,2,4,1,0:T(4,128)S(1)}, s32[2,1,512]{2,1,0:T(1,128)S(1)}, s32[1,...) while((s32[]{:T(128)}, ...), condition=%wide.region_5.6_spmd, body=%wide.region_2.5_spmd.sunk | while | flops 563739136 | bytes 28915852 | solution.py:173
  145.8 6.1 fusion.197
  152.1 29.9 %all-gather.25.cloned.1.call-done = bf16[1024,2048]{1,0:T(8,128)(2,1)} async-done(((bf16[128,2048]{1,0:T(8,128)(2,1)}), bf16[1024,2048]{1,0:T(8,128)(2,1)}) %all-gather.25.cloned.1.call-update) | async-done | bytes 4194320 | tf_op jit(solution)/shard_map/all_gather | solution.py:143
  182.1 6.2 fusion.123
  189.4 17.9 %while.55 = (s32[]{:T(128)}, bf16[2,1,512,4,64]{2,4,3,1,0:T(8,128)(2,1)S(1)}, f32[2,1,4,512,1]{3,2,4,1,0:T(4,128)S(1)}, s32[2,1,512]{2,1,0:T(1,128)S(1)}, s32[1,...) while((s32[]{:T(128)}, ...), condition=%wide.region_15.16_spmd, body=%wide.region_12.15_spmd.sunk | while | flops 563739136 | bytes 28915852 | solution.py:173
  208.8 4.8 fusion.199
  214.4 43.0 %reduce-scatter.13.cloned.1.call-done = f32[128,2048]{1,0:T(8,128)} async-done(((f32[1024,2048]{1,0:T(8,128)}), f32[128,2048]{1,0:T(8,128)}) %reduce-scatter.13.cloned.1.call-update) | async-done | bytes 1048592 | tf_op jit(solution)/shard_map/reduce_scatter | solution.py:177
  257.5 74.8 %reduce-scatter.17.cloned.1.call-done = f32[128,2048]{1,0:T(8,128)} async-done(((f32[1024,2048]{1,0:T(8,128)}), f32[128,2048]{1,0:T(8,128)}) %reduce-scatter.17.cloned.1.call-update) | async-done | bytes 1048592 | tf_op jit(solution)/shard_map/reduce_scatter | solution.py:177
  341.0 73.6 %all-gather.21.cloned.1.call-done = bf16[2048,1024]{1,0:T(8,128)(2,1)} async-done(((bf16[512,1024]{1,0:T(8,128)(2,1)}), bf16[2048,1024]{1,0:T(8,128)(2,1)}) %all-gather.21.cloned.1.call-update) | async-done | bytes 4194320 | tf_op jit(solution)/shard_map/all_gather | solution.py:123
  414.6 37.6 %all-gather.27.cloned.1.call-done = bf16[1024,2048]{1,0:T(8,128)(2,1)} async-done(((bf16[128,2048]{1,0:T(8,128)(2,1)}), bf16[1024,2048]{1,0:T(8,128)(2,1)}) %all-gather.27.cloned.1.call-update) | async-done | bytes 4194320 | tf_op jit(solution)/shard_map/all_gather | solution.py:186
  452.2 10.0 fusion.200
  462.2 72.4 %all-gather.23.cloned.1.call-done = bf16[1024,2048]{1,0:T(8,128)(2,1)} async-done(((bf16[1024,512]{1,0:T(8,128)(2,1)}), bf16[1024,2048]{1,0:T(8,128)(2,1)}) %all-gather.23.cloned.1.call-update) | async-done | bytes 4194320 | tf_op jit(solution)/shard_map/all_gather | solution.py:124
  534.6 36.8 %all-gather.33.cloned.1.call-done = bf16[1024,2048]{1,0:T(8,128)(2,1)} async-done(((bf16[128,2048]{1,0:T(8,128)(2,1)}), bf16[1024,2048]{1,0:T(8,128)(2,1)}) %all-gather.33.cloned.1.call-update) | async-done | bytes 4194320 | tf_op jit(solution)/shard_map/all_gather | solution.py:208
  571.4 17.7 %add_convert_fusion = (bf16[1024,1024]{1,0:T(8,128)(2,1)}, f32[1024,1024]{1,0:T(8,128)S(1)}) fusion(f32[1024,1024]{1,0:T(8,128)} %fusion.200, bf16[1024,2048]{1,0:T(8,128)(2,1)} %all-gather.33.cloned.1.call-done, bf16[1024,2048]{1,0:T(8,128)(2,1)} %all-gather.23.cloned.1.call-done), kind=kOutput, calls=%fused_computation.138 | convolution fusion | flops 4370464768 | bytes 18874368 | tf_op jit(solution)/shard_map/sd,fd->sf/dot_general | solution.py:209
  591.5 6.1 convolution_convert_fusion
  598.1 12.4 all-gather.19.cloned.1.call-done
  610.5 10.0 fusion.198
  620.4 29.0 %all-gather.29.cloned.1.call-done = bf16[1024,2048]{1,0:T(8,128)(2,1)} async-done(((bf16[128,2048]{1,0:T(8,128)(2,1)}), bf16[1024,2048]{1,0:T(8,128)(2,1)}) %all-gather.29.cloned.1.call-update) | async-done | bytes 4194320 | tf_op jit(solution)/shard_map/all_gather | solution.py:208
  649.4 17.7 %add_convert_fusion.1 = (bf16[1024,1024]{1,0:T(8,128)(2,1)}, f32[1024,1024]{1,0:T(8,128)S(1)}) fusion(f32[1024,1024]{1,0:T(8,128)} %fusion.198, bf16[1024,2048]{1,0:T(8,128)(2,1)} %all-gather.29.cloned.1.call-done, bf16[1024,2048]{1,0:T(8,128)(2,1)} %all-gather.23.cloned.1.call-done), kind=kOutput, calls=%fused_computation.139 | convolution fusion | flops 4370464768 | bytes 18874368 | tf_op jit(solution)/shard_map/sd,fd->sf/dot_general | solution.py:209
  669.5 6.1 convolution_convert_fusion.1
  675.9 10.8 fusion.201
  686.7 10.6 fusion.202
  697.4 6.5 reduce-scatter.19.cloned.1.call-done
  703.9 54.4 %reduce-scatter.15.cloned.1.call-done = bf16[128,2048]{1,0:T(8,128)(2,1)} async-done(((bf16[1024,2048]{1,0:T(8,128)(2,1)}), bf16[128,2048]{1,0:T(8,128)(2,1)}) %reduce-scatter.15.cloned.1.call-update) | async-done | bytes 524304 | tf_op jit(solution)/shard_map/reduce_scatter | solution.py:189
  758.3 75.4 %reduce-scatter.21.cloned.1.call-done = f32[128,2048]{1,0:T(8,128)} async-done(((f32[1024,2048]{1,0:T(8,128)}), f32[128,2048]{1,0:T(8,128)}) %reduce-scatter.21.cloned.1.call-update) | async-done | bytes 1048592 | tf_op jit(solution)/shard_map/reduce_scatter | solution.py:215
  833.7 74.8 %reduce-scatter.25.cloned.1.call-done = f32[128,2048]{1,0:T(8,128)} async-done(((f32[1024,2048]{1,0:T(8,128)}), f32[128,2048]{1,0:T(8,128)}) %reduce-scatter.25.cloned.1.call-update) | async-done | bytes 1048592 | tf_op jit(solution)/shard_map/reduce_scatter | solution.py:215
  908.6 4.0 multiply_reduce_fusion.2
  916.8 35.7 %all-gather.31.cloned.1.call-done = bf16[1024,2048]{1,0:T(8,128)(2,1)} async-done(((bf16[128,2048]{1,0:T(8,128)(2,1)}), bf16[1024,2048]{1,0:T(8,128)(2,1)}) %all-gather.31.cloned.1.call-update) | async-done | bytes 4194320 | tf_op jit(solution)/shard_map/all_gather | solution.py:223
  952.6 3.8 convolution_convert_fusion.3
  961.3 65.9 %while.56 = (s32[]{:T(128)}, f32[1,1024,4,64]{1,3,2,0:T(8,128)S(1)}, f32[1,1024,4,64]{1,3,2,0:T(8,128)}, f32[2,1,512,4,64]{2,0,4,3,1:T(2,128)}, bf16[2,1,512,4,6...) while((s32[]{:T(128)}, ...), condition=%wide.region_25.26_spmd.clone, body=%wide.region_23.25_spmd.clone.sunk | while | flops 1376647680 | bytes 164698496 | solution.py:261
  983.6 10.3 dynamic_update_slice.37
  1010.0 4.7 fusion.307
  1016.7 10.3 dynamic_update_slice.37
  1038.2 4.3 convolution_convert_fusion.2
  1048.9 63.0 %while.57 = (s32[]{:T(128)}, f32[1,1024,4,64]{1,3,2,0:T(8,128)S(1)}, f32[1,1024,4,64]{1,3,2,0:T(8,128)}, f32[2,1,512,4,64]{2,0,4,3,1:T(2,128)}, bf16[2,1,512,4,6...) while((s32[]{:T(128)}, ...), condition=%wide.region_34.35_spmd.clone, body=%wide.region_32.34_spmd.clone.sunk | while | flops 1376647680 | bytes 162601312 | solution.py:261
  1055.4 3.8 multiply_convert_fusion.9
  1069.4 10.4 dynamic_update_slice.38
  1086.3 3.8 multiply_convert_fusion.9
  1094.8 4.7 fusion.320
  1101.5 10.4 dynamic_update_slice.38
  1116.4 6.0 fusion.100
  1122.5 5.7 add_bitcast_fusion
  1128.2 7.7 convolution_bitcast_fusion.1
  1136.0 7.5 convolution_bitcast_fusion
  1143.6 7.3 fusion.204
  1150.9 7.1 convolution_add_fusion.1
  1158.0 7.4 fusion.205
  1165.5 7.2 convolution_add_fusion
  1175.3 4.2 pad_maximum_fusion
  1179.5 4.3 slice_convert_fusion.1
  1192.7 4.5 fusion.173
  1197.2 3.8 fusion.172
  1203.7 35.4 %reduce-scatter.29.cloned.1.call-done = f32[3,512,256]{1,2,0:T(8,128)} async-done(((f32[3,2048,256]{1,2,0:T(8,128)}), f32[3,512,256]{1,2,0:T(8,128)}) %reduce-scatter.29.cloned.1.call-update) | async-done | bytes 1572880 | tf_op jit(solution)/shard_map/reduce_scatter | solution.py:298
  1242.1 72.3 %reduce-scatter.23.cloned.1.call-done = f32[128,2048]{1,0:T(8,128)} async-done(((f32[1024,2048]{1,0:T(8,128)}), f32[128,2048]{1,0:T(8,128)}) %reduce-scatter.23.cloned.1.call-update) | async-done | bytes 1048592 | tf_op jit(solution)/shard_map/reduce_scatter | solution.py:282
  1314.4 75.0 %reduce-scatter.27.cloned.1.call-done = f32[128,2048]{1,0:T(8,128)} async-done(((f32[1024,2048]{1,0:T(8,128)}), f32[128,2048]{1,0:T(8,128)}) %reduce-scatter.27.cloned.1.call-update) | async-done | bytes 1048592 | tf_op jit(solution)/shard_map/reduce_scatter | solution.py:282
  1392.1 42.8 %all-reduce = (f32[4,2048]{1,0:T(4,128)S(1)}, f32[5]{0:T(128)}) all-reduce(f32[4,2048]{1,0:T(4,128)S(1)} %maximum_add_fusion, f32[5]{0:T(128)S(1)} %maximum_add_fusion.1), channel_id=1, replica_groups=mesh['row'=4,'col'=8] {'row','col'}, use_global_device_ids=true, to_apply=%region_50.51 | all-reduce | flops 8197 | bytes 65576 | tf_op jit(solution)/shard_map/psum | solution.py:303
  1439.5 98.5 %reduce-scatter.33.cloned.1.call-done = f32[512,1024]{1,0:T(8,128)} async-done(((f32[2048,1024]{1,0:T(8,128)}), f32[512,1024]{1,0:T(8,128)}) %reduce-scatter.33.cloned.1.call-update) | async-done | bytes 2097168 | tf_op jit(solution)/shard_map/reduce_scatter | solution.py:300
  1538.0 148.3 %reduce-scatter.35.cloned.1.call-done = f32[1024,512]{1,0:T(8,128)} async-done(((f32[1024,2048]{1,0:T(8,128)}), f32[1024,512]{1,0:T(8,128)}) %reduce-scatter.35.cloned.1.call-update) | async-done | bytes 2097168 | tf_op jit(solution)/shard_map/reduce_scatter | solution.py:301
  1686.3 47.0 %reduce-scatter.31.cloned.1.call-done = f32[256,512]{1,0:T(8,128)} async-done(((f32[256,2048]{1,0:T(8,128)}), f32[256,512]{1,0:T(8,128)}) %reduce-scatter.31.cloned.1.call-update) | async-done | bytes 524304 | tf_op jit(solution)/shard_map/reduce_scatter | solution.py:299
  (444 shorter events, 196.6 us)
Async XLA Ops:
  7.2 33.5 %copy-start.10 = (bf16[2,128,2048]{2,1,0:T(8,128)(2,1)S(1)}, bf16[2,128,2048]{2,1,0:T(8,128)(2,1)}, u32[]{:S(2)}) copy-start(bf16[2,128,2048]{2,1,0:T(8,128)(2,1)} %param.20) | copy-start | bytes 3145732
  7.2 36.3 %copy-start.85 = (s32[2,1024]{1,0:T(2,128)S(1)}, s32[2,1024]{1,0:T(2,128)}, u32[]{:S(2)}) copy-start(s32[2,1024]{1,0:T(2,128)} %param.23) | copy-start | bytes 24580
  7.2 36.3 %copy-start.86 = (s32[2,1024]{1,0:T(2,128)S(1)}, s32[2,1024]{1,0:T(2,128)}, u32[]{:S(2)}) copy-start(s32[2,1024]{1,0:T(2,128)} %param.24) | copy-start | bytes 24580
  7.2 69.2 %all-gather.15.cloned.1.call-start = ((), (), s32[]{:S(2)}) async-start(), calls=%async_computation.13 | async-start | bytes 3932160 | tf_op jit(solution)/shard_map/all_gather | solution.py:121
  9.6 104.5 %all-gather.13.cloned.1.call-start = ((), (), s32[]{:S(2)}) async-start(), calls=%async_computation.12 | async-start | bytes 4718592 | tf_op jit(solution)/shard_map/all_gather | solution.py:143
  42.1 103.6 %all-gather.17.cloned.1.call-start = ((), (), s32[]{:S(2)}) async-start(), calls=%async_computation.14 | async-start | bytes 1310720 | tf_op jit(solution)/shard_map/all_gather | solution.py:122
  42.9 139.2 %all-gather.25.cloned.1.call-start = ((), (), s32[]{:S(2)}) async-start(), calls=%async_computation.20 | async-start | bytes 4718592 | tf_op jit(solution)/shard_map/all_gather | solution.py:143
  43.4 214.0 %reduce-scatter.13.cloned.1.call-start = ((), (), s32[]{:S(2)}) async-start(), calls=%async_computation.15 | async-start | bytes 9437184 | tf_op jit(solution)/shard_map/reduce_scatter | solution.py:177
  44.6 76.0 %copy-start.59 = (f32[1024,32]{0,1:T(8,128)}, f32[1024,32]{0,1:T(8,128)S(1)}, u32[]{:S(2)}) copy-start(f32[1024,32]{0,1:T(8,128)S(1)} %get-tuple-element.582) | copy-start | bytes 393220
  44.6 76.0 %copy-start.61 = (f32[1024,32]{0,1:T(8,128)}, f32[1024,32]{0,1:T(8,128)S(1)}, u32[]{:S(2)}) copy-start(f32[1024,32]{0,1:T(8,128)S(1)} %get-tuple-element.583) | copy-start | bytes 393220
  44.6 143.9 %copy-start.55 = (f32[1024,32]{0,1:T(8,128)}, f32[1024,32]{0,1:T(8,128)S(1)}, u32[]{:S(2)}) copy-start(f32[1024,32]{0,1:T(8,128)S(1)} %get-tuple-element.588) | copy-start | bytes 393220
  44.6 143.9 %copy-start.57 = (f32[1024,32]{0,1:T(8,128)}, f32[1024,32]{0,1:T(8,128)S(1)}, u32[]{:S(2)}) copy-start(f32[1024,32]{0,1:T(8,128)S(1)} %get-tuple-element.589) | copy-start | bytes 393220
  145.1 6.8 copy-start.8
  145.1 6.8 copy-start.21
  145.1 6.8 copy-start.65
  145.1 6.8 copy-start.67
  151.9 180.4 %reduce-scatter.17.cloned.1.call-start = ((), (), s32[]{:S(2)}) async-start(), calls=%async_computation.21 | async-start | bytes 9437184 | tf_op jit(solution)/shard_map/reduce_scatter | solution.py:177
  189.4 19.4 %copy-start.34 = (bf16[256,2048]{1,0:T(8,128)(2,1)S(1)}, bf16[256,2048]{1,0:T(8,128)(2,1)}, u32[]{:S(2)}) copy-start(bf16[256,2048]{1,0:T(8,128)(2,1)} %all-gather.17.cloned.1.call-done) | copy-start | bytes 3145732
  213.6 118.7 %copy-start.11 = (bf16[2,128,2048]{2,1,0:T(8,128)(2,1)S(1)}, bf16[2,128,2048]{2,1,0:T(8,128)(2,1)}, u32[]{:S(2)}) copy-start(bf16[2,128,2048]{2,1,0:T(8,128)(2,1)} %param.20) | copy-start | bytes 3145732
  213.6 121.1 %copy-start.71 = (f32[1,2048]{1,0:T(1,128)S(1)}, f32[1,2048]{1,0:T(1,128)}, u32[]{:S(2)}) copy-start(f32[1,2048]{1,0:T(1,128)} %get-tuple-element.578) | copy-start | bytes 24580
  213.6 121.1 %copy-start.78 = (f32[1,2048]{1,0:T(1,128)S(1)}, f32[1,2048]{1,0:T(1,128)}, u32[]{:S(2)}) copy-start(f32[1,2048]{1,0:T(1,128)} %get-tuple-element.580) | copy-start | bytes 24580
  213.7 201.0 %all-gather.21.cloned.1.call-start = ((), (), s32[]{:S(2)}) async-start(), calls=%async_computation.17 | async-start | bytes 5242880 | tf_op jit(solution)/shard_map/all_gather | solution.py:123
  214.4 237.8 %all-gather.27.cloned.1.call-start = ((), (), s32[]{:S(2)}) async-start(), calls=%async_computation.22 | async-start | bytes 4718592 | tf_op jit(solution)/shard_map/all_gather | solution.py:186
  334.1 578.4 %copy-start.13 = (f32[128,2048]{1,0:T(8,128)}, f32[128,2048]{1,0:T(8,128)S(1)}, u32[]{:S(2)}) copy-start(f32[128,2048]{1,0:T(8,128)S(1)} %get-tuple-element.517) | copy-start | bytes 3145732
  334.2 578.4 %copy-start.15 = (f32[128,2048]{1,0:T(8,128)}, f32[128,2048]{1,0:T(8,128)S(1)}, u32[]{:S(2)}) copy-start(f32[128,2048]{1,0:T(8,128)S(1)} %get-tuple-element.561) | copy-start | bytes 3145732
  336.2 198.4 %all-gather.23.cloned.1.call-start = ((), (), s32[]{:S(2)}) async-start(), calls=%async_computation.18 | async-start | bytes 5242880 | tf_op jit(solution)/shard_map/all_gather | solution.py:124
  336.9 234.5 %all-gather.33.cloned.1.call-start = ((), (), s32[]{:S(2)}) async-start(), calls=%async_computation.28 | async-start | bytes 4718592 | tf_op jit(solution)/shard_map/all_gather | solution.py:208
  339.5 271.0 %all-gather.19.cloned.1.call-start = ((), (), s32[]{:S(2)}) async-start(), calls=%async_computation.16 | async-start | bytes 4718592 | tf_op jit(solution)/shard_map/all_gather | solution.py:186
  340.2 309.2 %all-gather.29.cloned.1.call-start = ((), (), s32[]{:S(2)}) async-start(), calls=%async_computation.24 | async-start | bytes 4718592 | tf_op jit(solution)/shard_map/all_gather | solution.py:208
  340.8 363.2 %reduce-scatter.19.cloned.1.call-start = ((), (), s32[]{:S(2)}) async-start(), calls=%async_computation.23 | async-start | bytes 4718592 | tf_op jit(solution)/shard_map/reduce_scatter | solution.py:189
  571.4 17.7 %copy-start.37 = (f32[1024,1024]{1,0:T(8,128)S(1)}, f32[1024,1024]{1,0:T(8,128)}, u32[]{:S(2)}) copy-start(f32[1024,1024]{1,0:T(8,128)} %fusion.200) | copy-start | bytes 12582916
  597.6 160.7 %reduce-scatter.15.cloned.1.call-start = ((), (), s32[]{:S(2)}) async-start(), calls=%async_computation.19 | async-start | bytes 4718592 | tf_op jit(solution)/shard_map/reduce_scatter | solution.py:189
  649.4 17.7 %copy-start.38 = (f32[1024,1024]{1,0:T(8,128)S(1)}, f32[1024,1024]{1,0:T(8,128)}, u32[]{:S(2)}) copy-start(f32[1024,1024]{1,0:T(8,128)} %fusion.198) | copy-start | bytes 12582916
  675.6 158.1 %reduce-scatter.21.cloned.1.call-start = ((), (), s32[]{:S(2)}) async-start(), calls=%async_computation.25 | async-start | bytes 9437184 | tf_op jit(solution)/shard_map/reduce_scatter | solution.py:215
  686.6 221.9 %reduce-scatter.25.cloned.1.call-start = ((), (), s32[]{:S(2)}) async-start(), calls=%async_computation.29 | async-start | bytes 9437184 | tf_op jit(solution)/shard_map/reduce_scatter | solution.py:215
  697.3 255.2 %all-gather.31.cloned.1.call-start = ((), (), s32[]{:S(2)}) async-start(), calls=%async_computation.26 | async-start | bytes 4718592 | tf_op jit(solution)/shard_map/all_gather | solution.py:223
  915.8 122.4 %all-gather.35.cloned.1.call-start = ((), (), s32[]{:S(2)}) async-start(), calls=%async_computation.30 | async-start | bytes 4718592 | tf_op jit(solution)/shard_map/all_gather | solution.py:223
  916.4 322.7 %reduce-scatter.29.cloned.1.call-start = ((), (), s32[]{:S(2)}) async-start(), calls=%async_computation.32 | async-start | bytes 7864320 | tf_op jit(solution)/shard_map/reduce_scatter | solution.py:298
  1042.5 6.4 copy-start.7
  1042.5 6.4 copy-start.18
  1042.5 6.4 copy-start.20
  1042.5 6.4 copy-start.64
  1042.5 6.4 copy-start.70
  1128.2 186.3 %reduce-scatter.23.cloned.1.call-start = ((), (), s32[]{:S(2)}) async-start(), calls=%async_computation.27 | async-start | bytes 9437184 | tf_op jit(solution)/shard_map/reduce_scatter | solution.py:282
  1135.9 253.5 %reduce-scatter.27.cloned.1.call-start = ((), (), s32[]{:S(2)}) async-start(), calls=%async_computation.31 | async-start | bytes 9437184 | tf_op jit(solution)/shard_map/reduce_scatter | solution.py:282
  1143.5 7.3 copy-start.98
  1143.5 394.5 %reduce-scatter.33.cloned.1.call-start = ((), (), s32[]{:S(2)}) async-start(), calls=%async_computation.34 | async-start | bytes 10485760 | tf_op jit(solution)/shard_map/reduce_scatter | solution.py:300
  1143.6 7.3 copy-start.91
  1158.0 7.5 copy-start.46
  1158.0 528.3 %reduce-scatter.35.cloned.1.call-start = ((), (), s32[]{:S(2)}) async-start(), calls=%async_computation.35 | async-start | bytes 10485760 | tf_op jit(solution)/shard_map/reduce_scatter | solution.py:301
  1158.0 7.5 copy-start.92
  1172.7 560.6 %reduce-scatter.31.cloned.1.call-start = ((), (), s32[]{:S(2)}) async-start(), calls=%async_computation.33 | async-start | bytes 2621440 | tf_op jit(solution)/shard_map/reduce_scatter | solution.py:299
  1201.0 188.4 %copy-start.12 = (bf16[2,128,2048]{2,1,0:T(8,128)(2,1)S(1)}, bf16[2,128,2048]{2,1,0:T(8,128)(2,1)}, u32[]{:S(2)}) copy-start(bf16[2,128,2048]{2,1,0:T(8,128)(2,1)} %param.20) | copy-start | bytes 3145732
  1201.1 188.4 %copy-start.73 = (f32[1,2048]{1,0:T(1,128)S(1)}, f32[1,2048]{1,0:T(1,128)}, u32[]{:S(2)}) copy-start(f32[1,2048]{1,0:T(1,128)} %copy-done.72) | copy-start | bytes 24580
  1201.1 188.4 %copy-start.82 = (f32[128]{0:T(128)S(1)}, f32[128]{0:T(128)}, u32[]{:S(2)}) copy-start(f32[128]{0:T(128)} %copy-done.81) | copy-start | bytes 1540
  1201.1 188.4 %copy-start.84 = (f32[128]{0:T(128)S(1)}, f32[128]{0:T(128)}, u32[]{:S(2)}) copy-start(f32[128]{0:T(128)} %copy-done.83) | copy-start | bytes 1540
  1201.1 188.4 %copy-start.88 = (f32[128]{0:T(128)S(1)}, f32[128]{0:T(128)}, u32[]{:S(2)}) copy-start(f32[128]{0:T(128)} %copy-done.87) | copy-start | bytes 1540
  1201.1 188.4 %copy-start.90 = (f32[128]{0:T(128)S(1)}, f32[128]{0:T(128)}, u32[]{:S(2)}) copy-start(f32[128]{0:T(128)} %copy-done.89) | copy-start | bytes 1540
  1201.1 190.9 %copy-start.74 = (f32[2048]{0:T(1024)S(1)}, f32[2048]{0:T(1024)}, u32[]{:S(2)}) copy-start(f32[2048]{0:T(1024)} %get-tuple-element.411) | copy-start | bytes 24580
  1201.1 190.9 %copy-start.75 = (f32[2048]{0:T(1024)S(1)}, f32[2048]{0:T(1024)}, u32[]{:S(2)}) copy-start(f32[2048]{0:T(1024)} %get-tuple-element.414) | copy-start | bytes 24580
  1201.1 190.9 %copy-start.76 = (f32[2048]{0:T(1024)S(1)}, f32[2048]{0:T(1024)}, u32[]{:S(2)}) copy-start(f32[2048]{0:T(1024)} %get-tuple-element.415) | copy-start | bytes 24580
  1201.1 190.9 %copy-start.77 = (f32[2048]{0:T(1024)S(1)}, f32[2048]{0:T(1024)}, u32[]{:S(2)}) copy-start(f32[2048]{0:T(1024)} %get-tuple-element.416) | copy-start | bytes 24580
  1201.1 234.5 %copy-start.39 = (f32[128,2048]{1,0:T(8,128)S(1)}, f32[128,2048]{1,0:T(8,128)}, u32[]{:S(2)}) copy-start(f32[128,2048]{1,0:T(8,128)} %get-tuple-element.509) | copy-start | bytes 3145732
  1201.2 234.5 %copy-start.40 = (f32[128,2048]{1,0:T(8,128)S(1)}, f32[128,2048]{1,0:T(8,128)}, u32[]{:S(2)}) copy-start(f32[128,2048]{1,0:T(8,128)} %get-tuple-element.555) | copy-start | bytes 3145732
  (70 other events, 296.8 us)
Sparse Core Ops, SparseCore 0:
  10.2 66.2 all-gather.14
  78.9 35.2 all-gather.12
  115.7 27.9 all-gather.16
  146.1 35.9 all-gather.24
  185.9 71.4 reduce-scatter.12
  260.8 71.4 reduce-scatter.16
  333.9 80.7 all-gather.20
  417.1 35.0 all-gather.26
  453.8 80.7 all-gather.22
  536.3 35.0 all-gather.32
  573.9 36.5 all-gather.18
  612.8 36.5 all-gather.28
  652.8 51.1 reduce-scatter.18
  707.2 51.1 reduce-scatter.14
  762.2 71.4 reduce-scatter.20
  837.0 71.4 reduce-scatter.24
  915.9 36.5 all-gather.30
  954.3 36.5 all-gather.34
  1128.3 110.7 reduce-scatter.28
  1242.4 71.9 reduce-scatter.22
  1317.9 71.4 reduce-scatter.26
  1392.4 145.5 reduce-scatter.32
  1540.9 145.3 reduce-scatter.34
  1689.0 44.2 reduce-scatter.30
where the time goes:
time: 1750 us; the launch traced here: 1740 us
  waiting for transfers between devices  1210 us (69%)
  matrix products  256 us (15%)
  local copies, waits for them, and re-layouts  96 us (5%)
  other arithmetic  92.9 us (5%)
  blocking collectives  69.4 us (4%)
    reduce_scatter x2, waiting for transfers between devices, body(): lax.psum_scatter(jnp.einsum('sf,df->sd', grad_pre, up_full, preferred_ele...  150 us
    reduce_scatter x1, waiting for transfers between devices, body(): lax.psum_scatter(grad_down, 'row', scatter_dimension=1, tiled=True)  148 us
    reduce_scatter x2, waiting for transfers between devices, body(): lax.psum_scatter(jnp.einsum('jsh,jdh->sd', grad_planes, qkv_full, preferr...  147 us
    reduce_scatter x2, waiting for transfers between devices, body(): lax.psum_scatter(jnp.dot(attended, out_full, preferred_element_type=F32),...  118 us
    reduce_scatter x1, waiting for transfers between devices, body(): lax.psum_scatter(grad_up, 'row', scatter_dimension=0, tiled=True)  98.5 us
    all_gather x1, waiting for transfers between devices, body(): lax.all_gather(w_up, 'row', axis=0, tiled=True)  73.6 us
    all_gather x1, waiting for transfers between devices, body(): lax.all_gather(w_down, 'row', axis=1, tiled=True)  72.4 us
    all_gather x2, waiting for transfers between devices, body(): rows_one = lax.all_gather(normed1, 'col', axis=0, tiled=True)  67.7 us
  transfers between devices with their start and end apart: 24, of which 22 were waited for; matrix products, arithmetic and copies ran while one was open for 19% of the time, Pallas kernels for 0%

commit v1 on v0

v1 whole, which is shorter than its diff:
```python
import functools
import math

import jax
import jax.numpy as jnp
from jax import lax
from jax.experimental import pallas as pl
from jax.experimental.pallas import tpu as pltpu
from jax.sharding import PartitionSpec as P

HEAD = 64
SEQ_MIN = 1024
SEQ_DEV = 64
EPSILON = 1e-05
NEG_FILL = -1e30
F32 = jnp.float32
B16 = jnp.bfloat16
NT = (((1,), (1,)), ((), ()))
NN = (((1,), (0,)), ((), ()))
TN = (((0,), (0,)), ((), ()))
PARAMS = pltpu.CompilerParams(vmem_limit_bytes=48 << 20)


def normalize(values):
    centre = values - jnp.mean(values, axis=-1, keepdims=True)
    spread = lax.rsqrt(jnp.mean(centre * centre, axis=-1, keepdims=True) + EPSILON)
    return (centre * spread, spread)


def norm_back(grad_normed, scaled, spread, ln_gain):
    shaped = grad_normed * ln_gain
    return spread * (
        shaped
        - jnp.mean(shaped, axis=-1, keepdims=True)
        - scaled * jnp.mean(shaped * scaled, axis=-1, keepdims=True)
    )


def rotary_tables(places, width):
    half_size = HEAD // 2
    inverse = 10000.0 ** (-(jnp.arange(half_size, dtype=F32) * 2.0) / HEAD)
    angles = places.astype(F32)[:, None] * inverse[None, :]
    cos_part, sin_part = lax.optimization_barrier((jnp.cos(angles), jnp.sin(angles)))
    return (
        jnp.tile(cos_part, (1, 2 * width // HEAD)),
        jnp.tile(jnp.concatenate([-sin_part, sin_part], axis=1), (1, width // HEAD)),
    )


def swap_halves(values):
    width = values.shape[-1]
    half = HEAD // 2
    if width % 128 == 0:
        lane = lax.broadcasted_iota(jnp.int32, values.shape, 1)
        return jnp.where(
            lane % HEAD < half,
            pltpu.roll(values, width - half, 1),
            pltpu.roll(values, half, 1),
        )
    return jnp.concatenate([values[:, half:], values[:, :half]], axis=-1)


def side_by_side(parts):
    return jnp.concatenate(parts, axis=-1) if len(parts) > 1 else parts[0]


def piece_at(spot_ref, t, piece):
    return pl.ds(pl.multiple_of(spot_ref[t] * piece, piece), piece)


def doc_mask_of(seg_col, seg_row, lo, hi):
    shape = (hi, hi - lo)
    causal = lax.broadcasted_iota(jnp.int32, shape, 0) <= lo + lax.broadcasted_iota(
        jnp.int32, shape, 1
    )
    return (seg_col[:hi] == seg_row[:, lo:hi]) & causal


def attend_forward(
    spot_ref, q_in, k_in, v_in, cos_ref, sin_ref, seg_col, seg_row, q_ref, k_ref, v_ref, att_ref,
    lse_ref, *, piece, blk
):
    rows, width = q_ref.shape
    score_scale = HEAD ** (-0.5)
    for t in range(rows // piece):
        src = piece_at(spot_ref, t, piece)
        dst = slice(t * piece, (t + 1) * piece)
        cos_part, sin_part = cos_ref[dst], sin_ref[dst]
        q_val, k_val = q_in[src].astype(F32), k_in[src].astype(F32)
        q_ref[dst] = (q_val * cos_part + swap_halves(q_val) * sin_part).astype(B16)
        k_ref[dst] = (k_val * cos_part + swap_halves(k_val) * sin_part).astype(B16)
        v_ref[dst] = v_in[src].astype(B16)
    for t in range(rows // blk):
        lo, hi = t * blk, (t + 1) * blk
        mask = doc_mask_of(seg_col, seg_row, lo, hi)
        outs = []
        for h in range(width // HEAD):
            cols = slice(h * HEAD, (h + 1) * HEAD)
            q_blk = q_ref[lo:hi, cols] * B16(score_scale)
            raw = lax.dot_general(k_ref[:hi, cols], q_blk, NT, preferred_element_type=F32)
            raw = jnp.where(mask, raw, NEG_FILL)
            top = jnp.max(raw, axis=0, keepdims=True)
            terms = jnp.exp(raw - top)
            total = jnp.sum(terms, axis=0, keepdims=True)
            probs = (terms * (1.0 / total)).astype(B16)
            outs.append(
                lax.dot_general(probs, v_ref[:hi, cols], TN, preferred_element_type=F32)
            )
            lse_ref[h, :, lo:hi] = jnp.broadcast_to(top + jnp.log(total), (8, blk))
        att = side_by_side(outs).astype(B16)
        for u in range(blk // piece):
            dst = piece_at(spot_ref, t * (blk // piece) + u, piece)
            att_ref[dst] = att[u * piece : (u + 1) * piece]


def attend_backward(
    spot_ref, q_ref, k_ref, v_ref, g_in, lse_ref, cos_ref, sin_ref, seg_col, seg_row, out_ref,
    g_ref, dk_acc, dv_acc, dq_acc, *, piece, blk
):
    rows, width = q_ref.shape
    score_scale = HEAD ** (-0.5)
    for t in range(rows // piece):
        g_ref[t * piece : (t + 1) * piece] = g_in[piece_at(spot_ref, t, piece)]
    for t in reversed(range(rows // blk)):
        lo, hi = t * blk, (t + 1) * blk
        mask = doc_mask_of(seg_col, seg_row, lo, hi)
        dqs, dks, dvs = [], [], []
        for h in range(width // HEAD):
            cols = slice(h * HEAD, (h + 1) * HEAD)
            q_blk, g_blk = q_ref[lo:hi, cols] * B16(score_scale), g_ref[lo:hi, cols]
            raw = lax.dot_general(k_ref[:hi, cols], q_blk, NT, preferred_element_type=F32)
            probs = jnp.exp(jnp.where(mask, raw, NEG_FILL) - lse_ref[h, :1, lo:hi])
            gp = lax.dot_general(v_ref[:hi, cols], g_blk, NT, preferred_element_type=F32)
            inner = jnp.sum(probs * gp, axis=0, keepdims=True)
            gs = (probs * (gp - inner)).astype(B16)
            dvs.append(
                lax.dot_general(probs.astype(B16), g_blk, NN, preferred_element_type=F32)
            )
            dks.append(lax.dot_general(gs, q_blk, NN, preferred_element_type=F32))
            dqs.append(
                lax.dot_general(gs, k_ref[:hi, cols], TN, preferred_element_type=F32)
                * score_scale
            )
        dq_acc[lo:hi] = side_by_side(dqs)
        if hi == rows:
            dk_acc[...] = side_by_side(dks)
            dv_acc[...] = side_by_side(dvs)
        else:
            dk_acc[:hi] += side_by_side(dks)
            dv_acc[:hi] += side_by_side(dvs)
    for t in range(rows // piece):
        dst = piece_at(spot_ref, t, piece)
        src = slice(t * piece, (t + 1) * piece)
        cos_part, sin_part = cos_ref[src], sin_ref[src]
        dq, dk = dq_acc[src], dk_acc[src]
        out_ref[0, dst] = (dq * cos_part - swap_halves(dq) * sin_part).astype(B16)
        out_ref[1, dst] = (dk * cos_part - swap_halves(dk) * sin_part).astype(B16)
        out_ref[2, dst] = dv_acc[src].astype(B16)


def attention_specs(rows, lanes, seq_len):
    width = min(128, lanes)
    return (
        width,
        (lanes // width, rows // seq_len),
        pl.BlockSpec((seq_len, width), lambda i, j, *_: (j, i)),
        pl.BlockSpec((seq_len, width), lambda i, j, *_: (j, 0)),
        pl.BlockSpec((seq_len, 1), lambda i, j, *_: (j, 0)),
        pl.BlockSpec((1, seq_len), lambda i, j, *_: (0, j)),
        pl.BlockSpec((width // HEAD, 8, seq_len), lambda i, j, *_: (i, 0, j)),
    )


def attention(spots, proj, tables, seg_cols, seg_rows, seq_len, piece):
    _, rows, lanes = proj.shape
    width, grid, wide, table, col, row, stat = attention_specs(rows, lanes, seq_len)
    planes = [
        pl.BlockSpec((None, seq_len, width), lambda i, j, *_, n=n: (n, j, i)) for n in range(3)
    ]
    full = jax.ShapeDtypeStruct((rows, lanes), B16)
    return pl.pallas_call(
        functools.partial(attend_forward, piece=piece, blk=min(256, seq_len)),
        out_shape=(full,) * 4 + (jax.ShapeDtypeStruct((lanes // HEAD, 8, rows), F32),),
        grid_spec=pltpu.PrefetchScalarGridSpec(
            num_scalar_prefetch=1,
            grid=grid,
            in_specs=planes + [table, table, col, row],
            out_specs=(wide, wide, wide, wide, stat),
        ),
        compiler_params=PARAMS,
        cost_estimate=pl.CostEstimate(
            flops=16 * rows * seq_len * lanes,
            bytes_accessed=rows * lanes * 24,
            transcendentals=rows * seq_len * lanes // HEAD,
        ),
        name="attend_forward",
    )(spots, proj, proj, proj, *tables, seg_cols, seg_rows)


def attention_back(spots, saved, grad, tables, seg_cols, seg_rows, seq_len, piece):
    q, k, v, lse = saved
    rows, lanes = q.shape
    width, grid, wide, table, col, row, stat = attention_specs(rows, lanes, seq_len)
    return pl.pallas_call(
        functools.partial(attend_backward, piece=piece, blk=min(256, seq_len)),
        out_shape=jax.ShapeDtypeStruct((3, rows, lanes), B16),
        grid_spec=pltpu.PrefetchScalarGridSpec(
            num_scalar_prefetch=1,
            grid=grid,
            in_specs=[wide, wide, wide, wide, stat, table, table, col, row],
            out_specs=pl.BlockSpec((3, seq_len, width), lambda i, j, *_: (0, j, i)),
            scratch_shapes=[pltpu.VMEM((seq_len, width), B16)]
            + [pltpu.VMEM((seq_len, width), F32)] * 3,
        ),
        compiler_params=PARAMS,
        cost_estimate=pl.CostEstimate(
            flops=24 * rows * seq_len * lanes,
            bytes_accessed=rows * lanes * 24,
            transcendentals=rows * seq_len * lanes // HEAD,
        ),
        name="attend_backward",
    )(spots, q, k, v, grad, lse, *tables, seg_cols, seg_rows)


def expand_kernel(x_ref, w_ref, hidden_ref, slope_ref):
    pre = jnp.dot(x_ref[...], w_ref[...], preferred_element_type=F32)
    share = 0.5 * (1.0 + lax.erf(pre * (2.0**-0.5)))
    hidden_ref[...] = (pre * share).astype(B16)
    density = jnp.exp(-0.5 * pre * pre) * ((2.0 * math.pi) ** -0.5)
    slope_ref[...] = (share + pre * density).astype(B16)


def expand(rows_in, weight):
    rows, depth = rows_in.shape
    units = weight.shape[1]
    tile, strip = min(256, units), min(512, rows)
    out = pl.BlockSpec((strip, tile), lambda i, j: (i, j))
    full = jax.ShapeDtypeStruct((rows, units), B16)
    return pl.pallas_call(
        expand_kernel,
        out_shape=(full, full),
        grid=(rows // strip, units // tile),
        in_specs=[
            pl.BlockSpec((strip, depth), lambda i, j: (i, 0)),
            pl.BlockSpec((depth, tile), lambda i, j: (0, j)),
        ],
        out_specs=(out, out),
        compiler_params=PARAMS,
        cost_estimate=pl.CostEstimate(
            flops=2 * rows * depth * units,
            bytes_accessed=2 * (rows * depth + depth * units) + 4 * rows * units,
            transcendentals=2 * rows * units,
        ),
        name="expand",
    )(rows_in, weight)


def row_chunks(refs, size):
    return [
        ref.at[slice(lo, lo + size)] for ref in refs for lo in range(0, ref.shape[-2], size)
    ]


def weight_kernel(*refs, x_count, planes, size, splits):
    xs, ys, out_ref = refs[:x_count], refs[x_count:-1], refs[-1]
    chunks = row_chunks(xs, size)
    for plane in range(planes or 1):
        own = [ref.at[plane] for ref in ys] if planes else ys
        acc = None
        for x_part, y_part in zip(chunks, row_chunks(own, size)):
            term = lax.dot_general(x_part[...], y_part[...], TN, preferred_element_type=F32)
            acc = term if acc is None else acc + term
        acc = acc.astype(B16)
        if planes:
            out_ref[plane] = acc
        elif splits:
            step = acc.shape[1] // splits
            for n in range(splits):
                out_ref[n] = acc[:, n * step : (n + 1) * step]
        else:
            out_ref[...] = acc


def weight_grad(xs, ys, out_shape, out_block, out_index, x_tile, y_tile, planes=0, splits=0):
    x_rows, depth = sum(x.shape[0] for x in xs), xs[0].shape[1]
    width = ys[0].shape[-1]
    size = math.gcd(512, *[x.shape[0] for x in xs], *[y.shape[-2] for y in ys])
    x_specs = [pl.BlockSpec((x.shape[0], x_tile), lambda i, j: (0, i)) for x in xs]
    y_specs = [
        pl.BlockSpec((planes, y.shape[1], y_tile), lambda i, j: (0, 0, j))
        if planes
        else pl.BlockSpec((y.shape[0], y_tile), lambda i, j: (0, j))
        for y in ys
    ]
    return pl.pallas_call(
        functools.partial(
            weight_kernel, x_count=len(xs), planes=planes, size=size, splits=splits
        ),
        out_shape=jax.ShapeDtypeStruct(out_shape, B16),
        grid=(depth // x_tile, width // y_tile),
        in_specs=x_specs + y_specs,
        out_specs=pl.BlockSpec(out_block, out_index),
        compiler_params=PARAMS,
        cost_estimate=pl.CostEstimate(
            flops=2 * x_rows * depth * width * max(1, planes),
            bytes_accessed=2 * (x_rows * (depth + width) + depth * width),
            transcendentals=0,
        ),
        name="weight_grad",
    )(*xs, *ys)


def flip(values, bits):
    count = lax.axis_size("col")
    return lax.ppermute(values, "col", [(i, i ^ bits) for i in range(count)])


def spread(values, direct):
    if not direct:
        return [lax.all_gather(values, "col", axis=0, tiled=True)]
    chips = lax.axis_size("col") // 2
    near = jnp.concatenate([values] + [flip(values, 2 * c) for c in range(1, chips)], axis=0)
    return [near, flip(near, 1)]


def collapse(make, direct):
    if not direct:
        return lax.psum_scatter(
            make(0).astype(B16), "col", scatter_dimension=0, tiled=True
        ).astype(F32)
    chips = lax.axis_size("col") // 2
    got = flip(make(1).astype(B16), 1)
    near = (make(0) + got.astype(F32)).astype(B16)
    size = near.shape[0] // chips
    total = near[:size].astype(F32)
    for c in range(1, chips):
        total = total + flip(near[c * size : (c + 1) * size], 2 * c).astype(F32)
    return total


def row_shift(values, step):
    count = lax.axis_size("row")
    return lax.ppermute(values, "row", [(i, (i + step) % count) for i in range(count)])


def body(
    layer_in,
    earlier_outs,
    cotangent,
    segments,
    positions,
    w_qkv,
    w_out,
    w_up,
    w_down,
    ln_gains,
    ln_biases,
    dwa_weights,
):
    micro_count, tok_dev, model_width = layer_in.shape
    prior_count = earlier_outs.shape[0]
    col_count = lax.axis_size("col")
    row_count = lax.axis_size("row")
    row_me, col_me = lax.axis_index("row"), lax.axis_index("col")
    direct = col_count == 8
    seq_len = max(SEQ_MIN, SEQ_DEV * col_count)
    group_rows = tok_dev * col_count
    lanes = w_qkv.shape[2]
    part_width = model_width // row_count
    units = w_up.shape[1]
    micros = range(micro_count)

    piece_ids = jnp.arange(col_count, dtype=jnp.int32)
    if direct:
        code = piece_ids ^ col_me
        spots = (code & 1) * (col_count // 2) + (code >> 1)
    else:
        spots = piece_ids

    packed = jnp.concatenate([ln_gains, ln_biases], axis=0)
    norm_params = jnp.zeros((row_count,) + packed.shape, B16)
    norm_params = lax.dynamic_update_index_in_dim(norm_params, packed, row_me, 0)
    for step in range(1, row_count):
        norm_params = lax.dynamic_update_index_in_dim(
            norm_params, row_shift(packed, step), (row_me - step) % row_count, 0
        )
    norm_params = jnp.moveaxis(norm_params, 0, 1).reshape(4, model_width).astype(F32)
    ln_gain, ln_bias = norm_params[:2], norm_params[2:]

    qkv_full = lax.all_gather(w_qkv, "row", axis=1, tiled=True)
    out_full = lax.all_gather(w_out, "row", axis=1, tiled=True)
    up_full = lax.all_gather(w_up, "row", axis=0, tiled=True)
    down_full = lax.all_gather(w_down, "row", axis=1, tiled=True)

    tables = [rotary_tables(positions[m], min(128, lanes)) for m in micros]
    seg_cols = [segments[m][:, None] for m in micros]
    seg_rows = [segments[m][None, :] for m in micros]

    resid_in = [layer_in[m].astype(F32) for m in micros]
    first = [normalize(v) for v in resid_in]
    normed1 = [(s * ln_gain[0] + ln_bias[0]).astype(B16) for s, _ in first]
    rows_one = [spread(v, direct) for v in normed1]
    grad_y = [cotangent[m].astype(F32) for m in micros]
    grad_block = [dwa_weights[prior_count] * g for g in grad_y]
    grad_rows = [spread(g.astype(B16), direct) for g in grad_block]
    parts = range(len(rows_one[0]))
    part_rows = group_rows // len(parts)

    def part_of(values, n):
        return values[n * part_rows : (n + 1) * part_rows]

    saved, attended = [], []
    for m in micros:
        proj = jnp.concatenate(
            [
                jnp.einsum("sd,jdh->jsh", v, qkv_full, preferred_element_type=F32)
                for v in rows_one[m]
            ],
            axis=1,
        )
        q, k, v, att, lse = attention(
            spots, proj, tables[m], seg_cols[m], seg_rows[m], seq_len, tok_dev
        )
        saved.append((q, k, v, lse))
        attended.append(att)

    resid, second, rows_two = [], [], []
    for m in micros:
        mixed = collapse(
            lambda n: jnp.dot(part_of(attended[m], n), out_full, preferred_element_type=F32),
            direct,
        )
        resid.append(resid_in[m] + mixed)
        second.append(normalize(resid[m]))
        normed2 = (second[m][0] * ln_gain[1] + ln_bias[1]).astype(B16)
        rows_two.append(spread(normed2, direct))

    hidden, grad_pre, grad_normed2 = [], [], []
    for m in micros:
        pairs = [expand(v, up_full) for v in rows_two[m]]
        hidden.append([a for a, _ in pairs])
        grad_pre.append(
            [
                (
                    slope.astype(F32)
                    * jnp.einsum("sd,fd->sf", g, down_full, preferred_element_type=F32)
                ).astype(B16)
                for (_, slope), g in zip(pairs, grad_rows[m])
            ]
        )
        grad_normed2.append(
            collapse(
                lambda n: jnp.einsum(
                    "sf,df->sd", grad_pre[m][n], up_full, preferred_element_type=F32
                ),
                direct,
            )
        )

    flat = lambda lists: [v for parts_of in lists for v in parts_of]
    total_rows = micro_count * group_rows
    fit = max(128, (8 << 20) // (2 * total_rows))
    x_tile, y_tile = min(256, units), min(model_width, fit)
    splits = y_tile // part_width if y_tile > part_width else 0
    y_blocks = part_width // y_tile if y_tile < part_width else 1
    grad_down = weight_grad(
        flat(hidden),
        flat(grad_rows),
        (row_count, units, part_width),
        (splits, x_tile, part_width) if splits else (None, x_tile, y_tile),
        (lambda i, j: (j, i, 0)) if splits else (lambda i, j: (j // y_blocks, i, j % y_blocks)),
        x_tile,
        y_tile,
        splits=splits,
    )
    grad_down = lax.psum_scatter(grad_down, "row", scatter_dimension=0)
    x_tile, y_tile = min(256, model_width), min(units, fit)
    grad_up = weight_grad(
        flat(rows_two),
        flat(grad_pre),
        (model_width, units),
        (x_tile, y_tile),
        lambda i, j: (i, j),
        x_tile,
        y_tile,
    )
    grad_up = lax.psum_scatter(grad_up, "row", scatter_dimension=0, tiled=True)

    outputs, mix_grads = [], []
    for m in micros:
        branch = collapse(
            lambda n: jnp.dot(hidden[m][n], down_full, preferred_element_type=F32), direct
        )
        block_out = resid[m] + branch
        earlier = earlier_outs[:, m].astype(F32)
        mix_sum = dwa_weights[0] * earlier[0]
        for level in range(1, prior_count):
            mix_sum = mix_sum + dwa_weights[level] * earlier[level]
        outputs.append((mix_sum + dwa_weights[prior_count] * block_out).astype(B16))
        mix_grads.append(
            jnp.concatenate(
                [
                    jnp.sum(grad_y[m][None] * earlier, axis=(1, 2)),
                    jnp.sum(grad_y[m] * block_out)[None],
                ]
            )
        )

    grad_resid, grad_mixed_rows, grad_planes = [], [], []
    for m in micros:
        grad_resid.append(grad_block[m] + norm_back(grad_normed2[m], *second[m], ln_gain[1]))
        grad_mixed_rows.append(spread(grad_resid[m].astype(B16), direct))
        grad_att = jnp.concatenate(
            [
                jnp.einsum("sd,hd->sh", v, out_full, preferred_element_type=F32).astype(B16)
                for v in grad_mixed_rows[m]
            ],
            axis=0,
        )
        grad_planes.append(
            attention_back(
                spots, saved[m], grad_att, tables[m], seg_cols[m], seg_rows[m], seq_len, tok_dev
            )
        )

    grad_wout = weight_grad(
        attended,
        flat(grad_mixed_rows),
        (row_count, lanes, part_width),
        (None, lanes, part_width),
        lambda i, j: (j, i, 0),
        lanes,
        part_width,
    )
    grad_wout = lax.psum_scatter(grad_wout, "row", scatter_dimension=0)
    x_tile = min(256, part_width)
    per_block = part_width // x_tile
    grad_qkv = weight_grad(
        flat(rows_one),
        grad_planes,
        (row_count, 3, part_width, lanes),
        (None, 3, x_tile, lanes),
        lambda i, j: (i // per_block, 0, i % per_block, 0),
        x_tile,
        lanes,
        planes=3,
    )
    grad_qkv = lax.psum_scatter(grad_qkv, "row", scatter_dimension=0)

    in_grads, grad_normed1 = [], []
    for m in micros:
        grad_normed1.append(
            collapse(
                lambda n: jnp.einsum(
                    "jsh,jdh->sd",
                    grad_planes[m][:, n * part_rows : (n + 1) * part_rows],
                    qkv_full,
                    preferred_element_type=F32,
                ),
                direct,
            )
        )
        in_grads.append(grad_resid[m] + norm_back(grad_normed1[m], *first[m], ln_gain[0]))

    stats = jnp.stack(
        [
            sum(jnp.sum(grad_normed1[m] * first[m][0], axis=0) for m in micros),
            sum(jnp.sum(grad_normed2[m] * second[m][0], axis=0) for m in micros),
            sum(jnp.sum(grad_normed1[m], axis=0) for m in micros),
            sum(jnp.sum(grad_normed2[m], axis=0) for m in micros),
        ]
    )
    mix_row = jnp.pad(sum(mix_grads), (0, part_width - prior_count - 1))
    slabs = jnp.concatenate(
        [
            jnp.moveaxis(stats.reshape(4, row_count, part_width), 1, 0),
            jnp.broadcast_to(mix_row, (row_count, 4, part_width)),
        ],
        axis=1,
    )
    slab = lax.dynamic_index_in_dim(slabs, row_me, 0, keepdims=False)
    for step in range(1, row_count):
        leaving = lax.dynamic_index_in_dim(slabs, (row_me + step) % row_count, 0, keepdims=False)
        slab = slab + row_shift(leaving, step)
    bits = 1
    while bits < col_count:
        slab = slab + flip(slab, bits)
        bits *= 2

    grad_earlier = (
        dwa_weights[:prior_count, None, None, None] * cotangent.astype(F32)[None]
    )
    return (
        jnp.stack(outputs),
        jnp.stack(in_grads),
        grad_earlier,
        grad_qkv.astype(F32),
        grad_wout.astype(F32),
        grad_up.astype(F32),
        grad_down.astype(F32),
        slab[:2],
        slab[2:4],
        slab[4, : prior_count + 1],
    )


def solution(mesh):
    in_specs = (
        P(None, ("row", "col"), None),
        P(None, None, ("row", "col"), None),
        P(None, ("row", "col"), None),
        P(None, "row"),
        P(None, "row"),
        P(None, "row", "col"),
        P("col", "row"),
        P("row", "col"),
        P("col", "row"),
        P(None, "row"),
        P(None, "row"),
        P(),
    )
    out_specs = (
        P(None, ("row", "col"), None),
        P(None, ("row", "col"), None),
        P(None, None, ("row", "col"), None),
        P(None, "row", "col"),
        P("col", "row"),
        P("row", "col"),
        P("col", "row"),
        P(None, "row"),
        P(None, "row"),
        P(),
    )
    return jax.shard_map(body, mesh=mesh, in_specs=in_specs, out_specs=out_specs, check_vma=False)
```

time: 1750 us -> 780 us (0.45)
  waiting for transfers between devices: 1210 us -> 371 us
  matrix products: 256 us -> 88.1 us
  Pallas kernels: 0 us -> 115 us
  starting transfers between devices: 2.35 us -> 78 us
  blocking collectives: 69.4 us -> 0 us
  local copies, waits for them, and re-layouts: 96 us -> 34.1 us
  other arithmetic: 92.9 us -> 70.8 us
    reduce_scatter x12 -> x4, waiting for transfers between devices: 806 us -> 48.9 us  [the longest x1 48.9 us: body(): grad_qkv = lax.psum_scatter(grad_qkv, 'row', scatter_dimension=0)]
    all_gather x12 -> x4, waiting for transfers between devices: 397 us -> 27.3 us  [the longest x1 19.1 us: body(): down_full = lax.all_gather(w_down, 'row', axis=1, tiled=True)]
    ppermute x0 -> x73, waiting for transfers between devices: none -> 294 us  [the longest x67 288 us: flip(): return lax.ppermute(values, 'col', [(i, i ^ bits) for i in range(count)])]
    dot_general x52 -> x28, matrix products: 256 us -> 88.1 us  [the longest x4 21.2 us: body(): jnp.dot(hidden[m][n], down_full, preferred_element_type=F32)]
    pallas_call x0 -> x12, Pallas kernels: none -> 115 us  [the longest x4 44.6 us: weight_grad(): pl.pallas_call(functools.partial(weight_kernel, x_count=len(xs), planes=p...]
    ppermute x0 -> x73, starting transfers between devices: none -> 77.7 us  [the longest x67 67.2 us: flip(): return lax.ppermute(values, 'col', [(i, i ^ bits) for i in range(count)])]
    dynamic_update_slice x8 -> x3, local copies, waits for them, and re-layouts: 43.6 us -> 0.04 us  [body(): lax.dynamic_update_index_in_dim(norm_params, row_shift(packed, step), (ro...]
    psum x1 -> x0, blocking collectives: 42.8 us -> none  [body(): norm_total, mix_total = lax.psum((norm_stats, mix_grads), ('row', 'col'))]
  transfers between devices with their start and end apart: 24 -> 81, of which waited for: 22 -> 50; matrix products, arithmetic and copies ran while one was open for 19% -> 21% of each run, Pallas kernels for 0% -> 14%
where the time goes in v1:
time: 780 us; the launch traced here: 772 us
  waiting for transfers between devices  371 us (48%)
  Pallas kernels  115 us (15%)
  matrix products  88.1 us (11%)
  starting transfers between devices  78 us (10%)
  other arithmetic  70.8 us (9%)
  local copies, waits for them, and re-layouts  34.1 us (4%)
  between operations  16.2 us (2%)
    ppermute x67, waiting for transfers between devices, flip(): return lax.ppermute(values, 'col', [(i, i ^ bits) for i in range(count)])  288 us
    ppermute x67, starting transfers between devices, flip(): return lax.ppermute(values, 'col', [(i, i ^ bits) for i in range(count)])  67.2 us
    reduce_scatter x1, waiting for transfers between devices, body(): grad_qkv = lax.psum_scatter(grad_qkv, 'row', scatter_dimension=0)  48.9 us
    pallas_call x4, Pallas kernels, weight_grad(): pl.pallas_call(functools.partial(weight_kernel, x_count=len(xs), planes=p...  44.6 us
    pallas_call x2, Pallas kernels, attention_back(): pl.pallas_call(functools.partial(attend_backward, piece=piece, blk=min(25...  26.4 us
    unnamed x262, local copies, waits for them, and re-layouts  23.5 us
    pallas_call x4, Pallas kernels, expand(): pl.pallas_call(expand_kernel, out_shape=(full, full), grid=(rows // strip...  23.4 us
    dot_general x4, matrix products, body(): jnp.dot(hidden[m][n], down_full, preferred_element_type=F32)  21.2 us
  transfers between devices with their start and end apart: 81, of which 50 were waited for; matrix products, arithmetic and copies ran while one was open for 21% of the time, Pallas kernels for 14%

profile of v1, /device:TPU:0, one launch (start us, length us, event | category | flops | bytes accessed | tf_op | source)
XLA Modules:
  0.0 772.4 jit_solution(1000261961840214812)
XLA Ops:
  23.3 12.2 %collective-permute-done.5 = bf16[128,2048]{1,0:T(8,128)(2,1)S(1)} collective-permute-done((bf16[128,2048]{1,0:T(8,128)(2,1)S(1)}, bf16[128,2048]{1,0:T(8,128)(2,1)S(1)}, u32[]{:S(2)}, u32[]{:S(2)}) %collective-permute-start.5) | collective-permute-done | bytes 524320 | tf_op jit(solution)/shard_map/ppermute | solution.py:315
  35.6 9.2 %collective-permute-done.4 = bf16[128,2048]{1,0:T(8,128)(2,1)S(1)} collective-permute-done((bf16[128,2048]{1,0:T(8,128)(2,1)S(1)}, bf16[128,2048]{1,0:T(8,128)(2,1)S(1)}, u32[]{:S(2)}, u32[]{:S(2)}) %collective-permute-start.4) | collective-permute-done | bytes 524320 | tf_op jit(solution)/shard_map/ppermute | solution.py:315
  56.9 5.2 collective-permute-done.21
  62.1 10.6 %collective-permute-done.20 = bf16[128,2048]{1,0:T(8,128)(2,1)} collective-permute-done((bf16[128,2048]{1,0:T(8,128)(2,1)}, bf16[128,2048]{1,0:T(8,128)(2,1)}, u32[]{:S(2)}, u32[]{:S(2)}) %collective-permute-start.20) | collective-permute-done | bytes 524320 | tf_op jit(solution)/shard_map/ppermute | solution.py:315
  76.0 4.5 fusion.15
  84.2 10.1 %attend_forward.2 = (bf16[1024,256]{1,0:T(8,128)(2,1)S(1)}, bf16[1024,256]{1,0:T(8,128)(2,1)S(1)}, bf16[1024,256]{1,0:T(8,128)(2,1)S(1)}, bf16[1024,256]{1,0:T(8,128)(2,1)S(1)}, f32[4,8,1024]{2,1,0:T(8,128)S(1)}) custom-call(s32[8]{0:T(128)S(1)} %shift-right-arithmetic_add_fusion.spot_ref, f32[3,1024,256]{2,1,0:T(8,128)} %pad_maximum_fusion.q_in.k_in.v_in, ...), custom_call_target="tpu_custom_call" | custom-call | flops 4294967296 | bytes 6291456 | tf_op jit(solution)/shard_map/attend_forward/pallas_call | solution.py:181
  95.9 8.2 %all-gather.7.cloned.1.call-done = bf16[256,2048]{1,0:T(8,128)(2,1)} async-done(((bf16[256,512]{1,0:T(8,128)(2,1)}), bf16[256,2048]{1,0:T(8,128)(2,1)}) %all-gather.7.cloned.1.call-update) | async-done | bytes 1048592 | tf_op jit(solution)/shard_map/all_gather | solution.py:391
  110.9 3.5 fusion.18
  116.5 10.1 %attend_forward.3 = (bf16[1024,256]{1,0:T(8,128)(2,1)S(1)}, bf16[1024,256]{1,0:T(8,128)(2,1)S(1)}, bf16[1024,256]{1,0:T(8,128)(2,1)S(1)}, bf16[1024,256]{1,0:T(8,128)(2,1)S(1)}, f32[4,8,1024]{2,1,0:T(8,128)S(1)}) custom-call(s32[8]{0:T(128)S(1)} %shift-right-arithmetic_add_fusion.spot_ref, f32[3,1024,256]{2,1,0:T(8,128)} %pad_maximum_fusion.1.q_in.k_in.v_in, ...), custom_call_target="tpu_custom_call" | custom-call | flops 4294967296 | bytes 6291456 | tf_op jit(solution)/shard_map/attend_forward/pallas_call | solution.py:181
  143.3 6.7 collective-permute-done.10
  151.5 9.8 %collective-permute-done.9 = bf16[128,2048]{1,0:T(8,128)(2,1)S(1)} collective-permute-done((bf16[128,2048]{1,0:T(8,128)(2,1)S(1)}, bf16[128,2048]{1,0:T(8,128)(2,1)S(1)}, u32[]{:S(2)}, u32[]{:S(2)}) %collective-permute-start.9) | collective-permute-done | bytes 524320 | tf_op jit(solution)/shard_map/ppermute | solution.py:315
  161.3 11.2 %collective-permute-done.26 = bf16[128,2048]{1,0:T(8,128)(2,1)S(1)} collective-permute-done((bf16[128,2048]{1,0:T(8,128)(2,1)S(1)}, bf16[128,2048]{1,0:T(8,128)(2,1)S(1)}, u32[]{:S(2)}, u32[]{:S(2)}) %collective-permute-start.26) | collective-permute-done | bytes 524320 | tf_op jit(solution)/shard_map/ppermute | solution.py:315
  172.5 10.2 %collective-permute-done.25 = bf16[128,2048]{1,0:T(8,128)(2,1)S(1)} collective-permute-done((bf16[128,2048]{1,0:T(8,128)(2,1)S(1)}, bf16[128,2048]{1,0:T(8,128)(2,1)S(1)}, u32[]{:S(2)}, u32[]{:S(2)}) %collective-permute-start.25) | collective-permute-done | bytes 524320 | tf_op jit(solution)/shard_map/ppermute | solution.py:315
  193.5 7.8 %collective-permute-done.13 = bf16[128,2048]{1,0:T(8,128)(2,1)S(1)} collective-permute-done((bf16[128,2048]{1,0:T(8,128)(2,1)S(1)}, bf16[128,2048]{1,0:T(8,128)(2,1)S(1)}, u32[]{:S(2)}, u32[]{:S(2)}) %collective-permute-start.13) | collective-permute-done | bytes 524320 | tf_op jit(solution)/shard_map/ppermute | solution.py:315
  202.9 9.8 %collective-permute-done.12 = bf16[128,2048]{1,0:T(8,128)(2,1)S(1)} collective-permute-done((bf16[128,2048]{1,0:T(8,128)(2,1)S(1)}, bf16[128,2048]{1,0:T(8,128)(2,1)S(1)}, u32[]{:S(2)}, u32[]{:S(2)}) %collective-permute-start.12) | collective-permute-done | bytes 524320 | tf_op jit(solution)/shard_map/ppermute | solution.py:315
  212.9 11.0 %collective-permute-done.37 = bf16[128,2048]{1,0:T(8,128)(2,1)S(1)} collective-permute-done((bf16[128,2048]{1,0:T(8,128)(2,1)S(1)}, bf16[128,2048]{1,0:T(8,128)(2,1)S(1)}, u32[]{:S(2)}, u32[]{:S(2)}) %collective-permute-start.37) | collective-permute-done | bytes 524320 | tf_op jit(solution)/shard_map/ppermute | solution.py:315
  223.9 10.2 %collective-permute-done.36 = bf16[128,2048]{1,0:T(8,128)(2,1)S(1)} collective-permute-done((bf16[128,2048]{1,0:T(8,128)(2,1)S(1)}, bf16[128,2048]{1,0:T(8,128)(2,1)S(1)}, u32[]{:S(2)}, u32[]{:S(2)}) %collective-permute-start.36) | collective-permute-done | bytes 524320 | tf_op jit(solution)/shard_map/ppermute | solution.py:315
  239.4 6.0 expand.5
  247.3 19.1 %all-gather.11.cloned.1.call-done = bf16[1024,2048]{1,0:T(8,128)(2,1)} async-done(((bf16[1024,512]{1,0:T(8,128)(2,1)}), bf16[1024,2048]{1,0:T(8,128)(2,1)}) %all-gather.11.cloned.1.call-update) | async-done | bytes 4194320 | tf_op jit(solution)/shard_map/all_gather | solution.py:393
  266.4 6.3 convolution_convert_fusion.4
  272.8 4.1 multiply_convert_fusion.2.refs_5_
  276.9 3.7 convolution_convert_fusion.1
  281.2 5.6 expand.4
  289.5 4.3 add_convert_fusion.4
  303.1 6.7 collective-permute-done.18
  313.0 8.0 %collective-permute-done.17 = bf16[128,2048]{1,0:T(8,128)(2,1)S(1)} collective-permute-done((bf16[128,2048]{1,0:T(8,128)(2,1)S(1)}, bf16[128,2048]{1,0:T(8,128)(2,1)S(1)}, u32[]{:S(2)}, u32[]{:S(2)}) %collective-permute-start.17) | collective-permute-done | bytes 524320 | tf_op jit(solution)/shard_map/ppermute | solution.py:315
  321.1 11.2 %collective-permute-done.42 = bf16[128,2048]{1,0:T(8,128)(2,1)S(1)} collective-permute-done((bf16[128,2048]{1,0:T(8,128)(2,1)S(1)}, bf16[128,2048]{1,0:T(8,128)(2,1)S(1)}, u32[]{:S(2)}, u32[]{:S(2)}) %collective-permute-start.42) | collective-permute-done | bytes 524320 | tf_op jit(solution)/shard_map/ppermute | solution.py:315
  332.3 10.3 %collective-permute-done.41 = bf16[128,2048]{1,0:T(8,128)(2,1)S(1)} collective-permute-done((bf16[128,2048]{1,0:T(8,128)(2,1)S(1)}, bf16[128,2048]{1,0:T(8,128)(2,1)S(1)}, u32[]{:S(2)}, u32[]{:S(2)}) %collective-permute-start.41) | collective-permute-done | bytes 524320 | tf_op jit(solution)/shard_map/ppermute | solution.py:315
  348.5 12.3 %collective-permute-done.53 = bf16[128,2048]{1,0:T(8,128)(2,1)S(1)} collective-permute-done((bf16[128,2048]{1,0:T(8,128)(2,1)S(1)}, bf16[128,2048]{1,0:T(8,128)(2,1)S(1)}, u32[]{:S(2)}, u32[]{:S(2)}) %collective-permute-start.53) | collective-permute-done | bytes 524320 | tf_op jit(solution)/shard_map/ppermute | solution.py:315
  360.8 10.2 %collective-permute-done.52 = bf16[128,2048]{1,0:T(8,128)(2,1)S(1)} collective-permute-done((bf16[128,2048]{1,0:T(8,128)(2,1)S(1)}, bf16[128,2048]{1,0:T(8,128)(2,1)S(1)}, u32[]{:S(2)}, u32[]{:S(2)}) %collective-permute-start.52) | collective-permute-done | bytes 524320 | tf_op jit(solution)/shard_map/ppermute | solution.py:315
  371.3 6.2 expand.7
  377.6 6.3 convolution_convert_fusion.2
  384.3 4.2 multiply_convert_fusion.refs_7_
  388.6 3.7 convolution_convert_fusion
  392.4 5.6 expand.6
  398.0 4.4 add_convert_fusion.2
  408.5 4.4 add_convert_fusion
  419.7 9.9 %collective-permute-done.33 = bf16[128,2048]{1,0:T(8,128)(2,1)S(1)} collective-permute-done((bf16[128,2048]{1,0:T(8,128)(2,1)S(1)}, bf16[128,2048]{1,0:T(8,128)(2,1)S(1)}, u32[]{:S(2)}, u32[]{:S(2)}) %collective-permute-start.33) | collective-permute-done | bytes 524320 | tf_op jit(solution)/shard_map/ppermute | solution.py:315
  429.6 11.2 %collective-permute-done.58 = bf16[128,2048]{1,0:T(8,128)(2,1)S(1)} collective-permute-done((bf16[128,2048]{1,0:T(8,128)(2,1)S(1)}, bf16[128,2048]{1,0:T(8,128)(2,1)S(1)}, u32[]{:S(2)}, u32[]{:S(2)}) %collective-permute-start.58) | collective-permute-done | bytes 524320 | tf_op jit(solution)/shard_map/ppermute | solution.py:315
  440.8 10.7 %collective-permute-done.57 = bf16[128,2048]{1,0:T(8,128)(2,1)S(1)} collective-permute-done((bf16[128,2048]{1,0:T(8,128)(2,1)S(1)}, bf16[128,2048]{1,0:T(8,128)(2,1)S(1)}, u32[]{:S(2)}, u32[]{:S(2)}) %collective-permute-start.57) | collective-permute-done | bytes 524320 | tf_op jit(solution)/shard_map/ppermute | solution.py:315
  462.6 9.4 %collective-permute-done.45 = bf16[128,2048]{1,0:T(8,128)(2,1)S(1)} collective-permute-done((bf16[128,2048]{1,0:T(8,128)(2,1)S(1)}, bf16[128,2048]{1,0:T(8,128)(2,1)S(1)}, u32[]{:S(2)}, u32[]{:S(2)}) %collective-permute-start.45) | collective-permute-done | bytes 524320 | tf_op jit(solution)/shard_map/ppermute | solution.py:315
  473.4 9.9 %collective-permute-done.44 = bf16[128,2048]{1,0:T(8,128)(2,1)S(1)} collective-permute-done((bf16[128,2048]{1,0:T(8,128)(2,1)S(1)}, bf16[128,2048]{1,0:T(8,128)(2,1)S(1)}, u32[]{:S(2)}, u32[]{:S(2)}) %collective-permute-start.44) | collective-permute-done | bytes 524320 | tf_op jit(solution)/shard_map/ppermute | solution.py:315
  483.6 11.0 %collective-permute-done.61 = bf16[128,2048]{1,0:T(8,128)(2,1)S(1)} collective-permute-done((bf16[128,2048]{1,0:T(8,128)(2,1)S(1)}, bf16[128,2048]{1,0:T(8,128)(2,1)S(1)}, u32[]{:S(2)}, u32[]{:S(2)}) %collective-permute-start.61) | collective-permute-done | bytes 524320 | tf_op jit(solution)/shard_map/ppermute | solution.py:315
  494.6 10.2 %collective-permute-done.60 = bf16[128,2048]{1,0:T(8,128)(2,1)S(1)} collective-permute-done((bf16[128,2048]{1,0:T(8,128)(2,1)S(1)}, bf16[128,2048]{1,0:T(8,128)(2,1)S(1)}, u32[]{:S(2)}, u32[]{:S(2)}) %collective-permute-start.60) | collective-permute-done | bytes 524320 | tf_op jit(solution)/shard_map/ppermute | solution.py:315
  505.2 4.1 collective-permute-done.62.refs_5_
  510.6 6.0 weight_grad.5
  521.6 12.7 %weight_grad.6 = bf16[2048,1024]{1,0:T(8,128)(2,1)} custom-call(bf16[512,2048]{1,0:T(8,128)(2,1)} %copy-done.2, bf16[512,2048]{1,0:T(8,128)(2,1)} %collective-permute-done.14.x_ref.refs_1_, bf16[512,2048]{1,0:T(8,128)(2,1)} %copy-done.3, bf16[512,2048]{1,0:T(8,128)(2,1)} %copy-done.16, bf16[512,1024]{1,0:T(8,128)(2,1)S(1)} %copy-done.44, ...), custom_call_target="tpu_custom_call" | custom-call | flops 8589934592 | bytes 16777216 | tf_op jit(solution)/shard_map/weight_grad/pallas_call | solution.py:295
  539.3 14.7 %weight_grad.7 = bf16[4,1024,512]{2,1,0:T(8,128)(2,1)} custom-call(bf16[512,1024]{1,0:T(8,128)(2,1)S(1)} %copy-done.20, bf16[512,1024]{1,0:T(8,128)(2,1)S(1)} %copy-done.18, bf16[512,1024]{1,0:T(8,128)(2,1)S(1)} %copy-done.24, bf16[512,1024]{1,0:T(8,128)(2,1)S(1)} %copy-done.22, bf16[512,2048]{1,0:T(8,128)(2,1)} %pad_maximum_fusion.6.refs_4_, ...), custom_call_target="tpu_custom_call" | custom-call | flops 8589934592 | bytes 16777216 | tf_op jit(solution)/shard_map/weight_grad/pallas_call | solution.py:295
  557.0 3.7 fusion
  563.5 4.5 broadcast_multiply_fusion
  568.0 5.8 fusion.75
  578.9 13.4 %attend_backward.2.refs_4_ = bf16[3,1024,256]{2,1,0:T(8,128)(2,1)S(1)} custom-call(s32[8]{0:T(128)S(1)} %shift-right-arithmetic_add_fusion.spot_ref, bf16[1024,256]{1,0:T(8,128)(2,1)S(1)} %copy-done.32, bf16[1024,256]{1,0:T(8,128)(2,1)S(1)} %copy-done.34, bf16[1024,256]{1,0:T(8,128)(2,1)S(1)} %copy-done.36, bf16[1024,256]{1,0:T(8,128)(2,1)S(1)} %pad_maximum_fusion.12.g_in, ...), custom_call_target="tpu_custom_call" | custom-call | flops 6442450944 | bytes 6291456 | tf_op jit(solution)/shard_map/attend_backward/pallas_call | solution.py:204
  597.2 13.1 %attend_backward.3.refs_5_ = bf16[3,1024,256]{2,1,0:T(8,128)(2,1)S(1)} custom-call(s32[8]{0:T(128)S(1)} %shift-right-arithmetic_add_fusion.spot_ref, bf16[1024,256]{1,0:T(8,128)(2,1)S(1)} %copy-done.38, bf16[1024,256]{1,0:T(8,128)(2,1)S(1)} %copy-done.40, bf16[1024,256]{1,0:T(8,128)(2,1)S(1)} %copy-done.42, bf16[1024,256]{1,0:T(8,128)(2,1)S(1)} %pad_maximum_fusion.13.g_in, ...), custom_call_target="tpu_custom_call" | custom-call | flops 6442450944 | bytes 6291456 | tf_op jit(solution)/shard_map/attend_backward/pallas_call | solution.py:204
  613.5 11.3 %weight_grad.4 = bf16[4,3,512,256]{3,2,1,0:T(8,128)(2,1)} custom-call(bf16[512,2048]{1,0:T(8,128)(2,1)S(1)} %copy-done.1, bf16[512,2048]{1,0:T(8,128)(2,1)} %collective-permute-done.6.refs_1_, bf16[512,2048]{1,0:T(8,128)(2,1)} %pad_maximum_fusion.4.refs_2_, bf16[512,2048]{1,0:T(8,128)(2,1)} %collective-permute-done.22.refs_3_, ...), custom_call_target="tpu_custom_call" | custom-call | flops 6442450944 | bytes 10485760 | tf_op jit(solution)/shard_map/weight_grad/pallas_call | solution.py:295
  624.8 7.4 fusion.74
  632.2 3.5 fusion.3
  639.4 3.5 fusion.2
  647.0 4.6 collective-permute-done.50
  657.5 5.6 collective-permute-done.49
  663.1 11.1 %collective-permute-done.66 = bf16[128,2048]{1,0:T(8,128)(2,1)} collective-permute-done((bf16[128,2048]{1,0:T(8,128)(2,1)}, bf16[128,2048]{1,0:T(8,128)(2,1)}, u32[]{:S(2)}, u32[]{:S(2)}) %collective-permute-start.66) | collective-permute-done | bytes 524320 | tf_op jit(solution)/shard_map/ppermute | solution.py:315
  674.3 10.6 %collective-permute-done.65 = bf16[128,2048]{1,0:T(8,128)(2,1)} collective-permute-done((bf16[128,2048]{1,0:T(8,128)(2,1)S(1)}, bf16[128,2048]{1,0:T(8,128)(2,1)}, u32[]{:S(2)}, u32[]{:S(2)}) %collective-permute-start.65) | collective-permute-done | bytes 524320 | tf_op jit(solution)/shard_map/ppermute | solution.py:315
  685.0 3.7 fusion.56
  693.1 5.1 collective-permute-done.68
  714.0 48.9 %reduce-scatter.5.cloned.1.call-done = bf16[1,3,512,256]{3,2,1,0:T(8,128)(2,1)} async-done(((bf16[4,3,512,256]{3,2,1,0:T(8,128)(2,1)}), bf16[1,3,512,256]{3,2,1,0:T(8,128)(2,1)}) %reduce-scatter.5.cloned.1.call-update) | async-done | bytes 786448 | tf_op jit(solution)/shard_map/reduce_scatter | solution.py:548
  (512 shorter events, 198.0 us)
Async XLA Ops:
  7.2 68.8 %all-gather.5.cloned.1.call-start = ((), (), s32[]{:S(2)}) async-start(), calls=%async_computation.4 | async-start | bytes 3932160 | tf_op jit(solution)/shard_map/all_gather | solution.py:390
  7.9 96.1 %all-gather.7.cloned.1.call-start = ((), (), s32[]{:S(2)}) async-start(), calls=%async_computation.5 | async-start | bytes 1310720 | tf_op jit(solution)/shard_map/all_gather | solution.py:391
  15.8 223.7 %all-gather.9.cloned.1.call-start = ((), (), s32[]{:S(2)}) async-start(), calls=%async_computation.6 | async-start | bytes 5242880 | tf_op jit(solution)/shard_map/all_gather | solution.py:392
  22.3 22.5 %collective-permute-start.4 = (bf16[128,2048]{1,0:T(8,128)(2,1)S(1)}, bf16[128,2048]{1,0:T(8,128)(2,1)S(1)}, u32[]{:S(2)}, u32[]{:S(2)}) collective-permute-start(bf16[128,2048]{1,0:T(8,128)(2,1)S(1)} %get-tuple-element.118), channel_id=1, source_target_pairs={{0,4},{1,5},{2,6},{3,7},{4,0},{5,1},{6,2},{7,3},{8,12},{9,13},{10,... | collective-permute-start | bytes 1572872 | tf_op jit(solution)/shard_map/ppermute | solution.py:315
  22.8 22.1 %collective-permute-start.3 = (bf16[128,2048]{1,0:T(8,128)(2,1)S(1)}, bf16[128,2048]{1,0:T(8,128)(2,1)S(1)}, u32[]{:S(2)}, u32[]{:S(2)}) collective-permute-start(bf16[128,2048]{1,0:T(8,128)(2,1)S(1)} %get-tuple-element.118), channel_id=1, source_target_pairs={{0,2},{1,3},{2,0},{3,1},{4,6},{5,7},{6,4},{7,5},{8,10},{9,11},{10,... | collective-permute-start | bytes 1572872 | tf_op jit(solution)/shard_map/ppermute | solution.py:315
  45.7 30.2 %collective-permute-start.6 = (bf16[512,2048]{1,0:T(8,128)(2,1)S(1)}, bf16[512,2048]{1,0:T(8,128)(2,1)}, u32[]{:S(2)}, u32[]{:S(2)}) collective-permute-start(bf16[512,2048]{1,0:T(8,128)(2,1)S(1)} %pad_maximum_fusion.2.refs_0_), channel_id=1, source_target_pairs={{0,1},{1,0},{2,3},{3,2},{4,5},{5,4},{6,7},{7,6},{8,9},{9,8},{10,11... | collective-permute-start | bytes 6291464 | tf_op jit(solution)/shard_map/ppermute | solution.py:315
  45.9 220.6 %all-gather.11.cloned.1.call-start = ((), (), s32[]{:S(2)}) async-start(), calls=%async_computation.7 | async-start | bytes 5242880 | tf_op jit(solution)/shard_map/all_gather | solution.py:393
  46.0 16.1 %collective-permute-start.21 = (bf16[128,2048]{1,0:T(8,128)(2,1)}, bf16[128,2048]{1,0:T(8,128)(2,1)}, u32[]{:S(2)}, u32[]{:S(2)}) collective-permute-start(bf16[128,2048]{1,0:T(8,128)(2,1)} %get-tuple-element.119), channel_id=1, source_target_pairs={{0,6},{1,7},{2,4},{3,5},{4,2},{5,3},{6,0},{7,1},{8,14},{9,15},{10,... | collective-permute-start | bytes 1572872 | tf_op jit(solution)/shard_map/ppermute | solution.py:315
  47.7 25.0 %collective-permute-start.20 = (bf16[128,2048]{1,0:T(8,128)(2,1)}, bf16[128,2048]{1,0:T(8,128)(2,1)}, u32[]{:S(2)}, u32[]{:S(2)}) collective-permute-start(bf16[128,2048]{1,0:T(8,128)(2,1)} %get-tuple-element.119), channel_id=1, source_target_pairs={{0,4},{1,5},{2,6},{3,7},{4,0},{5,1},{6,2},{7,3},{8,12},{9,13},{10,... | collective-permute-start | bytes 1572872 | tf_op jit(solution)/shard_map/ppermute | solution.py:315
  49.0 23.8 %collective-permute-start.19 = (bf16[128,2048]{1,0:T(8,128)(2,1)}, bf16[128,2048]{1,0:T(8,128)(2,1)}, u32[]{:S(2)}, u32[]{:S(2)}) collective-permute-start(bf16[128,2048]{1,0:T(8,128)(2,1)} %get-tuple-element.119), channel_id=1, source_target_pairs={{0,2},{1,3},{2,0},{3,1},{4,6},{5,7},{6,4},{7,5},{8,10},{9,11},{10,... | collective-permute-start | bytes 1572872 | tf_op jit(solution)/shard_map/ppermute | solution.py:315
  75.9 31.6 %collective-permute-start.22 = (bf16[512,2048]{1,0:T(8,128)(2,1)}, bf16[512,2048]{1,0:T(8,128)(2,1)}, u32[]{:S(2)}, u32[]{:S(2)}) collective-permute-start(bf16[512,2048]{1,0:T(8,128)(2,1)} %pad_maximum_fusion.4.refs_2_), channel_id=1, source_target_pairs={{0,1},{1,0},{2,3},{3,2},{4,5},{5,4},{6,7},{7,6},{8,9},{9,8},{10,11... | collective-permute-start | bytes 6291464 | tf_op jit(solution)/shard_map/ppermute | solution.py:315
  107.4 24.2 %collective-permute-start.7 = (bf16[512,2048]{1,0:T(8,128)(2,1)}, bf16[512,2048]{1,0:T(8,128)(2,1)}, u32[]{:S(2)}, u32[]{:S(2)}) collective-permute-start(bf16[512,2048]{1,0:T(8,128)(2,1)} %convolution_convert_fusion.5), channel_id=1, source_target_pairs={{0,1},{1,0},{2,3},{3,2},{4,5},{5,4},{6,7},{7,6},{8,9},{9,8},{10,11... | collective-permute-start | bytes 6291464 | tf_op jit(solution)/shard_map/ppermute | solution.py:315
  131.6 524.1 %reduce-scatter.7.cloned.1.call-start = ((), (), s32[]{:S(2)}) async-start(), calls=%async_computation.9 | async-start | bytes 1310720 | tf_op jit(solution)/shard_map/reduce_scatter | solution.py:535
  134.2 15.8 %collective-permute-start.10 = (bf16[128,2048]{1,0:T(8,128)(2,1)S(1)}, bf16[128,2048]{1,0:T(8,128)(2,1)S(1)}, u32[]{:S(2)}, u32[]{:S(2)}) collective-permute-start(bf16[128,2048]{1,0:T(8,128)(2,1)S(1)} %get-tuple-element.110), channel_id=1, source_target_pairs={{0,6},{1,7},{2,4},{3,5},{4,2},{5,3},{6,0},{7,1},{8,14},{9,15},{10,... | collective-permute-start | bytes 1572872 | tf_op jit(solution)/shard_map/ppermute | solution.py:315
  136.7 24.6 %collective-permute-start.9 = (bf16[128,2048]{1,0:T(8,128)(2,1)S(1)}, bf16[128,2048]{1,0:T(8,128)(2,1)S(1)}, u32[]{:S(2)}, u32[]{:S(2)}) collective-permute-start(bf16[128,2048]{1,0:T(8,128)(2,1)S(1)} %get-tuple-element.111), channel_id=1, source_target_pairs={{0,4},{1,5},{2,6},{3,7},{4,0},{5,1},{6,2},{7,3},{8,12},{9,13},{10,... | collective-permute-start | bytes 1572872 | tf_op jit(solution)/shard_map/ppermute | solution.py:315
  137.2 24.1 %collective-permute-start.8 = (bf16[128,2048]{1,0:T(8,128)(2,1)S(1)}, bf16[128,2048]{1,0:T(8,128)(2,1)S(1)}, u32[]{:S(2)}, u32[]{:S(2)}) collective-permute-start(bf16[128,2048]{1,0:T(8,128)(2,1)S(1)} %get-tuple-element.109), channel_id=1, source_target_pairs={{0,2},{1,3},{2,0},{3,1},{4,6},{5,7},{6,4},{7,5},{8,10},{9,11},{10,... | collective-permute-start | bytes 1572872 | tf_op jit(solution)/shard_map/ppermute | solution.py:315
  140.3 32.3 %collective-permute-start.26 = (bf16[128,2048]{1,0:T(8,128)(2,1)S(1)}, bf16[128,2048]{1,0:T(8,128)(2,1)S(1)}, u32[]{:S(2)}, u32[]{:S(2)}) collective-permute-start(bf16[128,2048]{1,0:T(8,128)(2,1)S(1)} %get-tuple-element.116), channel_id=1, source_target_pairs={{0,6},{1,7},{2,4},{3,5},{4,2},{5,3},{6,0},{7,1},{8,14},{9,15},{10,... | collective-permute-start | bytes 1572872 | tf_op jit(solution)/shard_map/ppermute | solution.py:315
  142.8 40.0 %collective-permute-start.25 = (bf16[128,2048]{1,0:T(8,128)(2,1)S(1)}, bf16[128,2048]{1,0:T(8,128)(2,1)S(1)}, u32[]{:S(2)}, u32[]{:S(2)}) collective-permute-start(bf16[128,2048]{1,0:T(8,128)(2,1)S(1)} %get-tuple-element.117), channel_id=1, source_target_pairs={{0,4},{1,5},{2,6},{3,7},{4,0},{5,1},{6,2},{7,3},{8,12},{9,13},{10,... | collective-permute-start | bytes 1572872 | tf_op jit(solution)/shard_map/ppermute | solution.py:315
  150.0 32.8 %collective-permute-start.24 = (bf16[128,2048]{1,0:T(8,128)(2,1)S(1)}, bf16[128,2048]{1,0:T(8,128)(2,1)S(1)}, u32[]{:S(2)}, u32[]{:S(2)}) collective-permute-start(bf16[128,2048]{1,0:T(8,128)(2,1)S(1)} %get-tuple-element.115), channel_id=1, source_target_pairs={{0,2},{1,3},{2,0},{3,1},{4,6},{5,7},{6,4},{7,5},{8,10},{9,11},{10,... | collective-permute-start | bytes 1572872 | tf_op jit(solution)/shard_map/ppermute | solution.py:315
  187.3 25.4 %collective-permute-start.12 = (bf16[128,2048]{1,0:T(8,128)(2,1)S(1)}, bf16[128,2048]{1,0:T(8,128)(2,1)S(1)}, u32[]{:S(2)}, u32[]{:S(2)}) collective-permute-start(bf16[128,2048]{1,0:T(8,128)(2,1)S(1)} %get-tuple-element.138), channel_id=1, source_target_pairs={{0,4},{1,5},{2,6},{3,7},{4,0},{5,1},{6,2},{7,3},{8,12},{9,13},{10,... | collective-permute-start | bytes 1572872 | tf_op jit(solution)/shard_map/ppermute | solution.py:315
  188.6 24.1 %collective-permute-start.11 = (bf16[128,2048]{1,0:T(8,128)(2,1)S(1)}, bf16[128,2048]{1,0:T(8,128)(2,1)S(1)}, u32[]{:S(2)}, u32[]{:S(2)}) collective-permute-start(bf16[128,2048]{1,0:T(8,128)(2,1)S(1)} %get-tuple-element.138), channel_id=1, source_target_pairs={{0,2},{1,3},{2,0},{3,1},{4,6},{5,7},{6,4},{7,5},{8,10},{9,11},{10,... | collective-permute-start | bytes 1572872 | tf_op jit(solution)/shard_map/ppermute | solution.py:315
  190.5 33.4 %collective-permute-start.37 = (bf16[128,2048]{1,0:T(8,128)(2,1)S(1)}, bf16[128,2048]{1,0:T(8,128)(2,1)S(1)}, u32[]{:S(2)}, u32[]{:S(2)}) collective-permute-start(bf16[128,2048]{1,0:T(8,128)(2,1)S(1)} %multiply_convert_fusion.5), channel_id=1, source_target_pairs={{0,6},{1,7},{2,4},{3,5},{4,2},{5,3},{6,0},{7,1},{8,14},{9,15},{10,... | collective-permute-start | bytes 1572872 | tf_op jit(solution)/shard_map/ppermute | solution.py:315
  192.2 41.8 %collective-permute-start.36 = (bf16[128,2048]{1,0:T(8,128)(2,1)S(1)}, bf16[128,2048]{1,0:T(8,128)(2,1)S(1)}, u32[]{:S(2)}, u32[]{:S(2)}) collective-permute-start(bf16[128,2048]{1,0:T(8,128)(2,1)S(1)} %multiply_convert_fusion.5), channel_id=1, source_target_pairs={{0,4},{1,5},{2,6},{3,7},{4,0},{5,1},{6,2},{7,3},{8,12},{9,13},{10,... | collective-permute-start | bytes 1572872 | tf_op jit(solution)/shard_map/ppermute | solution.py:315
  201.4 32.8 %collective-permute-start.35 = (bf16[128,2048]{1,0:T(8,128)(2,1)S(1)}, bf16[128,2048]{1,0:T(8,128)(2,1)S(1)}, u32[]{:S(2)}, u32[]{:S(2)}) collective-permute-start(bf16[128,2048]{1,0:T(8,128)(2,1)S(1)} %multiply_convert_fusion.5), channel_id=1, source_target_pairs={{0,2},{1,3},{2,0},{3,1},{4,6},{5,7},{6,4},{7,5},{8,10},{9,11},{10,... | collective-permute-start | bytes 1572872 | tf_op jit(solution)/shard_map/ppermute | solution.py:315
  212.8 26.6 %collective-permute-start.14 = (bf16[512,2048]{1,0:T(8,128)(2,1)S(1)}, bf16[512,2048]{1,0:T(8,128)(2,1)}, u32[]{:S(2)}, u32[]{:S(2)}) collective-permute-start(bf16[512,2048]{1,0:T(8,128)(2,1)S(1)} %pad_maximum_fusion.3.x_ref.refs_0_), channel_id=1, source_target_pairs={{0,1},{1,0},{2,3},{3,2},{4,5},{5,4},{6,7},{7,6},{8,9},{9,8},{10,11... | collective-permute-start | bytes 6291464 | tf_op jit(solution)/shard_map/ppermute | solution.py:315
  235.8 37.0 %collective-permute-start.38 = (bf16[512,2048]{1,0:T(8,128)(2,1)}, bf16[512,2048]{1,0:T(8,128)(2,1)}, u32[]{:S(2)}, u32[]{:S(2)}) collective-permute-start(bf16[512,2048]{1,0:T(8,128)(2,1)} %pad_maximum_fusion.6.refs_4_), channel_id=1, source_target_pairs={{0,1},{1,0},{2,3},{3,2},{4,5},{5,4},{6,7},{7,6},{8,9},{9,8},{10,11... | collective-permute-start | bytes 6291464 | tf_op jit(solution)/shard_map/ppermute | solution.py:315
  235.9 63.6 %collective-permute-start.29 = (bf16[128,2048]{1,0:T(8,128)(2,1)}, bf16[128,2048]{1,0:T(8,128)(2,1)}, u32[]{:S(2)}, u32[]{:S(2)}) collective-permute-start(bf16[128,2048]{1,0:T(8,128)(2,1)} %get-tuple-element.139), channel_id=1, source_target_pairs={{0,6},{1,7},{2,4},{3,5},{4,2},{5,3},{6,0},{7,1},{8,14},{9,15},{10,... | collective-permute-start | bytes 1572872 | tf_op jit(solution)/shard_map/ppermute | solution.py:315
  237.4 62.8 %collective-permute-start.28 = (bf16[128,2048]{1,0:T(8,128)(2,1)}, bf16[128,2048]{1,0:T(8,128)(2,1)}, u32[]{:S(2)}, u32[]{:S(2)}) collective-permute-start(bf16[128,2048]{1,0:T(8,128)(2,1)} %get-tuple-element.139), channel_id=1, source_target_pairs={{0,4},{1,5},{2,6},{3,7},{4,0},{5,1},{6,2},{7,3},{8,12},{9,13},{10,... | collective-permute-start | bytes 1572872 | tf_op jit(solution)/shard_map/ppermute | solution.py:315
  238.9 63.7 %collective-permute-start.27 = (bf16[128,2048]{1,0:T(8,128)(2,1)}, bf16[128,2048]{1,0:T(8,128)(2,1)}, u32[]{:S(2)}, u32[]{:S(2)}) collective-permute-start(bf16[128,2048]{1,0:T(8,128)(2,1)} %get-tuple-element.139), channel_id=1, source_target_pairs={{0,2},{1,3},{2,0},{3,1},{4,6},{5,7},{6,4},{7,5},{8,10},{9,11},{10,... | collective-permute-start | bytes 1572872 | tf_op jit(solution)/shard_map/ppermute | solution.py:315
  272.7 16.6 %collective-permute-start.15 = (bf16[512,2048]{1,0:T(8,128)(2,1)}, bf16[512,2048]{1,0:T(8,128)(2,1)}, u32[]{:S(2)}, u32[]{:S(2)}) collective-permute-start(bf16[512,2048]{1,0:T(8,128)(2,1)} %convolution_convert_fusion.4), channel_id=1, source_target_pairs={{0,1},{1,0},{2,3},{3,2},{4,5},{5,4},{6,7},{7,6},{8,9},{9,8},{10,11... | collective-permute-start | bytes 6291464 | tf_op jit(solution)/shard_map/ppermute | solution.py:315
  293.9 15.8 %collective-permute-start.18 = (bf16[128,2048]{1,0:T(8,128)(2,1)S(1)}, bf16[128,2048]{1,0:T(8,128)(2,1)S(1)}, u32[]{:S(2)}, u32[]{:S(2)}) collective-permute-start(bf16[128,2048]{1,0:T(8,128)(2,1)S(1)} %get-tuple-element.107), channel_id=1, source_target_pairs={{0,6},{1,7},{2,4},{3,5},{4,2},{5,3},{6,0},{7,1},{8,14},{9,15},{10,... | collective-permute-start | bytes 1572872 | tf_op jit(solution)/shard_map/ppermute | solution.py:315
  296.4 24.6 %collective-permute-start.17 = (bf16[128,2048]{1,0:T(8,128)(2,1)S(1)}, bf16[128,2048]{1,0:T(8,128)(2,1)S(1)}, u32[]{:S(2)}, u32[]{:S(2)}) collective-permute-start(bf16[128,2048]{1,0:T(8,128)(2,1)S(1)} %get-tuple-element.108), channel_id=1, source_target_pairs={{0,4},{1,5},{2,6},{3,7},{4,0},{5,1},{6,2},{7,3},{8,12},{9,13},{10,... | collective-permute-start | bytes 1572872 | tf_op jit(solution)/shard_map/ppermute | solution.py:315
  299.5 21.5 %collective-permute-start.16 = (bf16[128,2048]{1,0:T(8,128)(2,1)S(1)}, bf16[128,2048]{1,0:T(8,128)(2,1)S(1)}, u32[]{:S(2)}, u32[]{:S(2)}) collective-permute-start(bf16[128,2048]{1,0:T(8,128)(2,1)S(1)} %get-tuple-element.106), channel_id=1, source_target_pairs={{0,2},{1,3},{2,0},{3,1},{4,6},{5,7},{6,4},{7,5},{8,10},{9,11},{10,... | collective-permute-start | bytes 1572872 | tf_op jit(solution)/shard_map/ppermute | solution.py:315
  300.2 32.1 %collective-permute-start.42 = (bf16[128,2048]{1,0:T(8,128)(2,1)S(1)}, bf16[128,2048]{1,0:T(8,128)(2,1)S(1)}, u32[]{:S(2)}, u32[]{:S(2)}) collective-permute-start(bf16[128,2048]{1,0:T(8,128)(2,1)S(1)} %get-tuple-element.101), channel_id=1, source_target_pairs={{0,6},{1,7},{2,4},{3,5},{4,2},{5,3},{6,0},{7,1},{8,14},{9,15},{10,... | collective-permute-start | bytes 1572872 | tf_op jit(solution)/shard_map/ppermute | solution.py:315
  302.5 40.0 %collective-permute-start.41 = (bf16[128,2048]{1,0:T(8,128)(2,1)S(1)}, bf16[128,2048]{1,0:T(8,128)(2,1)S(1)}, u32[]{:S(2)}, u32[]{:S(2)}) collective-permute-start(bf16[128,2048]{1,0:T(8,128)(2,1)S(1)} %get-tuple-element.102), channel_id=1, source_target_pairs={{0,4},{1,5},{2,6},{3,7},{4,0},{5,1},{6,2},{7,3},{8,12},{9,13},{10,... | collective-permute-start | bytes 1572872 | tf_op jit(solution)/shard_map/ppermute | solution.py:315
  309.7 32.9 %collective-permute-start.40 = (bf16[128,2048]{1,0:T(8,128)(2,1)S(1)}, bf16[128,2048]{1,0:T(8,128)(2,1)S(1)}, u32[]{:S(2)}, u32[]{:S(2)}) collective-permute-start(bf16[128,2048]{1,0:T(8,128)(2,1)S(1)} %get-tuple-element.100), channel_id=1, source_target_pairs={{0,2},{1,3},{2,0},{3,1},{4,6},{5,7},{6,4},{7,5},{8,10},{9,11},{10,... | collective-permute-start | bytes 1572872 | tf_op jit(solution)/shard_map/ppermute | solution.py:315
  321.0 50.2 %collective-permute-start.30 = (bf16[512,2048]{1,0:T(8,128)(2,1)S(1)}, bf16[512,2048]{1,0:T(8,128)(2,1)S(1)}, u32[]{:S(2)}, u32[]{:S(2)}) collective-permute-start(bf16[512,2048]{1,0:T(8,128)(2,1)S(1)} %pad_maximum_fusion.5.x_ref.refs_2_), channel_id=1, source_target_pairs={{0,1},{1,0},{2,3},{3,2},{4,5},{5,4},{6,7},{7,6},{8,9},{9,8},{10,11... | collective-permute-start | bytes 6291464 | tf_op jit(solution)/shard_map/ppermute | solution.py:315
  345.1 15.7 %collective-permute-start.53 = (bf16[128,2048]{1,0:T(8,128)(2,1)S(1)}, bf16[128,2048]{1,0:T(8,128)(2,1)S(1)}, u32[]{:S(2)}, u32[]{:S(2)}) collective-permute-start(bf16[128,2048]{1,0:T(8,128)(2,1)S(1)} %get-tuple-element.126), channel_id=1, source_target_pairs={{0,6},{1,7},{2,4},{3,5},{4,2},{5,3},{6,0},{7,1},{8,14},{9,15},{10,... | collective-permute-start | bytes 1572872 | tf_op jit(solution)/shard_map/ppermute | solution.py:315
  346.7 24.2 %collective-permute-start.52 = (bf16[128,2048]{1,0:T(8,128)(2,1)S(1)}, bf16[128,2048]{1,0:T(8,128)(2,1)S(1)}, u32[]{:S(2)}, u32[]{:S(2)}) collective-permute-start(bf16[128,2048]{1,0:T(8,128)(2,1)S(1)} %get-tuple-element.126), channel_id=1, source_target_pairs={{0,4},{1,5},{2,6},{3,7},{4,0},{5,1},{6,2},{7,3},{8,12},{9,13},{10,... | collective-permute-start | bytes 1572872 | tf_op jit(solution)/shard_map/ppermute | solution.py:315
  348.0 23.0 %collective-permute-start.51 = (bf16[128,2048]{1,0:T(8,128)(2,1)S(1)}, bf16[128,2048]{1,0:T(8,128)(2,1)S(1)}, u32[]{:S(2)}, u32[]{:S(2)}) collective-permute-start(bf16[128,2048]{1,0:T(8,128)(2,1)S(1)} %get-tuple-element.126), channel_id=1, source_target_pairs={{0,2},{1,3},{2,0},{3,1},{4,6},{5,7},{6,4},{7,5},{8,10},{9,11},{10,... | collective-permute-start | bytes 1572872 | tf_op jit(solution)/shard_map/ppermute | solution.py:315
  392.3 16.1 %collective-permute-start.55 = (bf16[512,2048]{1,0:T(8,128)(2,1)}, bf16[512,2048]{1,0:T(8,128)(2,1)}, u32[]{:S(2)}, u32[]{:S(2)}) collective-permute-start(bf16[512,2048]{1,0:T(8,128)(2,1)} %convolution_convert_fusion), channel_id=1, source_target_pairs={{0,1},{1,0},{2,3},{3,2},{4,5},{5,4},{6,7},{7,6},{8,9},{9,8},{10,11... | collective-permute-start | bytes 6291464 | tf_op jit(solution)/shard_map/ppermute | solution.py:315
  402.5 15.8 %collective-permute-start.34 = (bf16[128,2048]{1,0:T(8,128)(2,1)S(1)}, bf16[128,2048]{1,0:T(8,128)(2,1)S(1)}, u32[]{:S(2)}, u32[]{:S(2)}) collective-permute-start(bf16[128,2048]{1,0:T(8,128)(2,1)S(1)} %get-tuple-element.113), channel_id=1, source_target_pairs={{0,6},{1,7},{2,4},{3,5},{4,2},{5,3},{6,0},{7,1},{8,14},{9,15},{10,... | collective-permute-start | bytes 1572872 | tf_op jit(solution)/shard_map/ppermute | solution.py:315
  404.0 25.6 %collective-permute-start.33 = (bf16[128,2048]{1,0:T(8,128)(2,1)S(1)}, bf16[128,2048]{1,0:T(8,128)(2,1)S(1)}, u32[]{:S(2)}, u32[]{:S(2)}) collective-permute-start(bf16[128,2048]{1,0:T(8,128)(2,1)S(1)} %get-tuple-element.114), channel_id=1, source_target_pairs={{0,4},{1,5},{2,6},{3,7},{4,0},{5,1},{6,2},{7,3},{8,12},{9,13},{10,... | collective-permute-start | bytes 1572872 | tf_op jit(solution)/shard_map/ppermute | solution.py:315
  405.4 24.1 %collective-permute-start.32 = (bf16[128,2048]{1,0:T(8,128)(2,1)S(1)}, bf16[128,2048]{1,0:T(8,128)(2,1)S(1)}, u32[]{:S(2)}, u32[]{:S(2)}) collective-permute-start(bf16[128,2048]{1,0:T(8,128)(2,1)S(1)} %get-tuple-element.112), channel_id=1, source_target_pairs={{0,2},{1,3},{2,0},{3,1},{4,6},{5,7},{6,4},{7,5},{8,10},{9,11},{10,... | collective-permute-start | bytes 1572872 | tf_op jit(solution)/shard_map/ppermute | solution.py:315
  413.0 27.8 %collective-permute-start.58 = (bf16[128,2048]{1,0:T(8,128)(2,1)S(1)}, bf16[128,2048]{1,0:T(8,128)(2,1)S(1)}, u32[]{:S(2)}, u32[]{:S(2)}) collective-permute-start(bf16[128,2048]{1,0:T(8,128)(2,1)S(1)} %get-tuple-element.104), channel_id=1, source_target_pairs={{0,6},{1,7},{2,4},{3,5},{4,2},{5,3},{6,0},{7,1},{8,14},{9,15},{10,... | collective-permute-start | bytes 1572872 | tf_op jit(solution)/shard_map/ppermute | solution.py:315
  414.5 37.0 %collective-permute-start.57 = (bf16[128,2048]{1,0:T(8,128)(2,1)S(1)}, bf16[128,2048]{1,0:T(8,128)(2,1)S(1)}, u32[]{:S(2)}, u32[]{:S(2)}) collective-permute-start(bf16[128,2048]{1,0:T(8,128)(2,1)S(1)} %get-tuple-element.105), channel_id=1, source_target_pairs={{0,4},{1,5},{2,6},{3,7},{4,0},{5,1},{6,2},{7,3},{8,12},{9,13},{10,... | collective-permute-start | bytes 1572872 | tf_op jit(solution)/shard_map/ppermute | solution.py:315
  418.3 33.3 %collective-permute-start.56 = (bf16[128,2048]{1,0:T(8,128)(2,1)S(1)}, bf16[128,2048]{1,0:T(8,128)(2,1)S(1)}, u32[]{:S(2)}, u32[]{:S(2)}) collective-permute-start(bf16[128,2048]{1,0:T(8,128)(2,1)S(1)} %get-tuple-element.103), channel_id=1, source_target_pairs={{0,2},{1,3},{2,0},{3,1},{4,6},{5,7},{6,4},{7,5},{8,10},{9,11},{10,... | collective-permute-start | bytes 1572872 | tf_op jit(solution)/shard_map/ppermute | solution.py:315
  457.8 25.6 %collective-permute-start.44 = (bf16[128,2048]{1,0:T(8,128)(2,1)S(1)}, bf16[128,2048]{1,0:T(8,128)(2,1)S(1)}, u32[]{:S(2)}, u32[]{:S(2)}) collective-permute-start(bf16[128,2048]{1,0:T(8,128)(2,1)S(1)} %get-tuple-element.82), channel_id=1, source_target_pairs={{0,4},{1,5},{2,6},{3,7},{4,0},{5,1},{6,2},{7,3},{8,12},{9,13},{10,... | collective-permute-start | bytes 1572872 | tf_op jit(solution)/shard_map/ppermute | solution.py:315
  459.1 24.2 %collective-permute-start.43 = (bf16[128,2048]{1,0:T(8,128)(2,1)S(1)}, bf16[128,2048]{1,0:T(8,128)(2,1)S(1)}, u32[]{:S(2)}, u32[]{:S(2)}) collective-permute-start(bf16[128,2048]{1,0:T(8,128)(2,1)S(1)} %get-tuple-element.82), channel_id=1, source_target_pairs={{0,2},{1,3},{2,0},{3,1},{4,6},{5,7},{6,4},{7,5},{8,10},{9,11},{10,... | collective-permute-start | bytes 1572872 | tf_op jit(solution)/shard_map/ppermute | solution.py:315
  459.8 34.8 %collective-permute-start.61 = (bf16[128,2048]{1,0:T(8,128)(2,1)S(1)}, bf16[128,2048]{1,0:T(8,128)(2,1)S(1)}, u32[]{:S(2)}, u32[]{:S(2)}) collective-permute-start(bf16[128,2048]{1,0:T(8,128)(2,1)S(1)} %get-tuple-element.122), channel_id=1, source_target_pairs={{0,6},{1,7},{2,4},{3,5},{4,2},{5,3},{6,0},{7,1},{8,14},{9,15},{10,... | collective-permute-start | bytes 1572872 | tf_op jit(solution)/shard_map/ppermute | solution.py:315
  461.2 43.5 %collective-permute-start.60 = (bf16[128,2048]{1,0:T(8,128)(2,1)S(1)}, bf16[128,2048]{1,0:T(8,128)(2,1)S(1)}, u32[]{:S(2)}, u32[]{:S(2)}) collective-permute-start(bf16[128,2048]{1,0:T(8,128)(2,1)S(1)} %get-tuple-element.122), channel_id=1, source_target_pairs={{0,4},{1,5},{2,6},{3,7},{4,0},{5,1},{6,2},{7,3},{8,12},{9,13},{10,... | collective-permute-start | bytes 1572872 | tf_op jit(solution)/shard_map/ppermute | solution.py:315
  472.0 32.8 %collective-permute-start.59 = (bf16[128,2048]{1,0:T(8,128)(2,1)S(1)}, bf16[128,2048]{1,0:T(8,128)(2,1)S(1)}, u32[]{:S(2)}, u32[]{:S(2)}) collective-permute-start(bf16[128,2048]{1,0:T(8,128)(2,1)S(1)} %get-tuple-element.122), channel_id=1, source_target_pairs={{0,2},{1,3},{2,0},{3,1},{4,6},{5,7},{6,4},{7,5},{8,10},{9,11},{10,... | collective-permute-start | bytes 1572872 | tf_op jit(solution)/shard_map/ppermute | solution.py:315
  483.5 21.7 %collective-permute-start.46 = (bf16[512,2048]{1,0:T(8,128)(2,1)S(1)}, bf16[512,2048]{1,0:T(8,128)(2,1)S(1)}, u32[]{:S(2)}, u32[]{:S(2)}) collective-permute-start(bf16[512,2048]{1,0:T(8,128)(2,1)S(1)} %pad_maximum_fusion.7.refs_2_), channel_id=1, source_target_pairs={{0,1},{1,0},{2,3},{3,2},{4,5},{5,4},{6,7},{7,6},{8,9},{9,8},{10,11... | collective-permute-start | bytes 6291464 | tf_op jit(solution)/shard_map/ppermute | solution.py:315
  516.6 191.6 %reduce-scatter.9.cloned.1.call-start = ((), (), s32[]{:S(2)}) async-start(), calls=%async_computation.10 | async-start | bytes 5242880 | tf_op jit(solution)/shard_map/reduce_scatter | solution.py:487
  534.4 176.8 %reduce-scatter.11.cloned.1.call-start = ((), (), s32[]{:S(2)}) async-start(), calls=%async_computation.11 | async-start | bytes 5242880 | tf_op jit(solution)/shard_map/reduce_scatter | solution.py:476
  554.0 209.0 %reduce-scatter.5.cloned.1.call-start = ((), (), s32[]{:S(2)}) async-start(), calls=%async_computation.8 | async-start | bytes 3932160 | tf_op jit(solution)/shard_map/reduce_scatter | solution.py:548
  595.4 36.7 %collective-permute-start.47 = (bf16[512,2048]{1,0:T(8,128)(2,1)}, bf16[512,2048]{1,0:T(8,128)(2,1)}, u32[]{:S(2)}, u32[]{:S(2)}) collective-permute-start(bf16[512,2048]{1,0:T(8,128)(2,1)} %bitcast_convert_fusion.1), channel_id=1, source_target_pairs={{0,1},{1,0},{2,3},{3,2},{4,5},{5,4},{6,7},{7,6},{8,9},{9,8},{10,11... | collective-permute-start | bytes 6291464 | tf_op jit(solution)/shard_map/ppermute | solution.py:315
  613.5 25.9 %collective-permute-start.63 = (bf16[512,2048]{1,0:T(8,128)(2,1)}, bf16[512,2048]{1,0:T(8,128)(2,1)}, u32[]{:S(2)}, u32[]{:S(2)}) collective-permute-start(bf16[512,2048]{1,0:T(8,128)(2,1)} %bitcast_convert_fusion), channel_id=1, source_target_pairs={{0,1},{1,0},{2,3},{3,2},{4,5},{5,4},{6,7},{7,6},{8,9},{9,8},{10,11... | collective-permute-start | bytes 6291464 | tf_op jit(solution)/shard_map/ppermute | solution.py:315
  635.8 15.8 %collective-permute-start.50 = (bf16[128,2048]{1,0:T(8,128)(2,1)S(1)}, bf16[128,2048]{1,0:T(8,128)(2,1)S(1)}, u32[]{:S(2)}, u32[]{:S(2)}) collective-permute-start(bf16[128,2048]{1,0:T(8,128)(2,1)S(1)} %get-tuple-element.98), channel_id=1, source_target_pairs={{0,6},{1,7},{2,4},{3,5},{4,2},{5,3},{6,0},{7,1},{8,14},{9,15},{10,... | collective-permute-start | bytes 1572872 | tf_op jit(solution)/shard_map/ppermute | solution.py:315
  638.1 25.0 %collective-permute-start.49 = (bf16[128,2048]{1,0:T(8,128)(2,1)S(1)}, bf16[128,2048]{1,0:T(8,128)(2,1)}, u32[]{:S(2)}, u32[]{:S(2)}) collective-permute-start(bf16[128,2048]{1,0:T(8,128)(2,1)S(1)} %get-tuple-element.99), channel_id=1, source_target_pairs={{0,4},{1,5},{2,6},{3,7},{4,0},{5,1},{6,2},{7,3},{8,12},{9,13},{10,... | collective-permute-start | bytes 1572872 | tf_op jit(solution)/shard_map/ppermute | solution.py:315
  639.0 24.2 %collective-permute-start.48 = (bf16[128,2048]{1,0:T(8,128)(2,1)S(1)}, bf16[128,2048]{1,0:T(8,128)(2,1)}, u32[]{:S(2)}, u32[]{:S(2)}) collective-permute-start(bf16[128,2048]{1,0:T(8,128)(2,1)S(1)} %get-tuple-element.97), channel_id=1, source_target_pairs={{0,2},{1,3},{2,0},{3,1},{4,6},{5,7},{6,4},{7,5},{8,10},{9,11},{10,... | collective-permute-start | bytes 1572872 | tf_op jit(solution)/shard_map/ppermute | solution.py:315
  643.9 30.4 %collective-permute-start.66 = (bf16[128,2048]{1,0:T(8,128)(2,1)}, bf16[128,2048]{1,0:T(8,128)(2,1)}, u32[]{:S(2)}, u32[]{:S(2)}) collective-permute-start(bf16[128,2048]{1,0:T(8,128)(2,1)} %get-tuple-element.95), channel_id=1, source_target_pairs={{0,6},{1,7},{2,4},{3,5},{4,2},{5,3},{6,0},{7,1},{8,14},{9,15},{10,... | collective-permute-start | bytes 1572872 | tf_op jit(solution)/shard_map/ppermute | solution.py:315
  646.1 38.7 %collective-permute-start.65 = (bf16[128,2048]{1,0:T(8,128)(2,1)S(1)}, bf16[128,2048]{1,0:T(8,128)(2,1)}, u32[]{:S(2)}, u32[]{:S(2)}) collective-permute-start(bf16[128,2048]{1,0:T(8,128)(2,1)S(1)} %get-tuple-element.96), channel_id=1, source_target_pairs={{0,4},{1,5},{2,6},{3,7},{4,0},{5,1},{6,2},{7,3},{8,12},{9,13},{10,... | collective-permute-start | bytes 1572872 | tf_op jit(solution)/shard_map/ppermute | solution.py:315
  651.7 33.3 %collective-permute-start.64 = (bf16[128,2048]{1,0:T(8,128)(2,1)S(1)}, bf16[128,2048]{1,0:T(8,128)(2,1)}, u32[]{:S(2)}, u32[]{:S(2)}) collective-permute-start(bf16[128,2048]{1,0:T(8,128)(2,1)S(1)} %get-tuple-element.94), channel_id=1, source_target_pairs={{0,2},{1,3},{2,0},{3,1},{4,6},{5,7},{6,4},{7,5},{8,10},{9,11},{10,... | collective-permute-start | bytes 1572872 | tf_op jit(solution)/shard_map/ppermute | solution.py:315
  (148 other events, 1707.2 us)
Sparse Core Ops, SparseCore 0:
  9.6 66.1 all-gather.4
  77.4 26.6 all-gather.6
  105.6 80.0 all-gather.8
  187.2 79.2 all-gather.10
  516.7 24.8 reduce-scatter.6
  543.7 75.2 reduce-scatter.8
  621.4 78.3 reduce-scatter.10
  702.0 60.8 reduce-scatter.4

commit v2 on v1

--- a/solution.py
+++ b/solution.py
@@ -261,8 +261,8 @@
     ]
 
 
-def weight_kernel(*refs, x_count, planes, size, splits):
-    xs, ys, out_ref = refs[:x_count], refs[x_count:-1], refs[-1]
+def weight_kernel(*refs, x_count, y_count, planes, size, splits, stacked):
+    xs, ys, out_ref = refs[:x_count], refs[x_count : x_count + y_count], refs[-1]
     chunks = row_chunks(xs, size)
     for plane in range(planes or 1):
         own = [ref.at[plane] for ref in ys] if planes else ys
@@ -273,6 +273,10 @@
         acc = acc.astype(B16)
         if planes:
             out_ref[plane] = acc
+        elif stacked:
+            step = acc.shape[0]
+            for n in range(acc.shape[1] // step):
+                out_ref[n * step : (n + 1) * step] = acc[:, n * step : (n + 1) * step]
         elif splits:
             step = acc.shape[1] // splits
             for n in range(splits):
@@ -281,7 +285,10 @@
             out_ref[...] = acc
 
 
-def weight_grad(xs, ys, out_shape, out_block, out_index, x_tile, y_tile, planes=0, splits=0):
+def weight_grad(
+    xs, ys, out_shape, out_block, out_index, x_tile, y_tile, planes=0, splits=0, stacked=False,
+    base=None
+):
     x_rows, depth = sum(x.shape[0] for x in xs), xs[0].shape[1]
     width = ys[0].shape[-1]
     size = math.gcd(512, *[x.shape[0] for x in xs], *[y.shape[-2] for y in ys])
@@ -292,14 +299,22 @@
         else pl.BlockSpec((y.shape[0], y_tile), lambda i, j: (0, j))
         for y in ys
     ]
+    bases = [] if base is None else [base]
     return pl.pallas_call(
         functools.partial(
-            weight_kernel, x_count=len(xs), planes=planes, size=size, splits=splits
+            weight_kernel,
+            x_count=len(xs),
+            y_count=len(ys),
+            planes=planes,
+            size=size,
+            splits=splits,
+            stacked=stacked,
         ),
         out_shape=jax.ShapeDtypeStruct(out_shape, B16),
         grid=(depth // x_tile, width // y_tile),
-        in_specs=x_specs + y_specs,
+        in_specs=x_specs + y_specs + [pl.BlockSpec(memory_space=pl.ANY) for _ in bases],
         out_specs=pl.BlockSpec(out_block, out_index),
+        input_output_aliases={len(xs) + len(ys): 0} if bases else {},
         compiler_params=PARAMS,
         cost_estimate=pl.CostEstimate(
             flops=2 * x_rows * depth * width * max(1, planes),
@@ -307,7 +322,7 @@
             transcendentals=0,
         ),
         name="weight_grad",
-    )(*xs, *ys)
+    )(*xs, *ys, *bases)
 
 
 def flip(values, bits):
@@ -323,19 +338,29 @@
     return [near, flip(near, 1)]
 
 
-def collapse(make, direct):
+def near_sum(make, direct):
     if not direct:
-        return lax.psum_scatter(
-            make(0).astype(B16), "col", scatter_dimension=0, tiled=True
-        ).astype(F32)
+        return make(0).astype(B16)
+    got = flip(make(1).astype(B16), 1)
+    return (make(0) + got.astype(F32)).astype(B16)
+
+
+def send_sum(near, direct):
+    if not direct:
+        return [lax.psum_scatter(near, "col", scatter_dimension=0, tiled=True)]
     chips = lax.axis_size("col") // 2
-    got = flip(make(1).astype(B16), 1)
-    near = (make(0) + got.astype(F32)).astype(B16)
     size = near.shape[0] // chips
-    total = near[:size].astype(F32)
-    for c in range(1, chips):
-        total = total + flip(near[c * size : (c + 1) * size], 2 * c).astype(F32)
-    return total
+    return [near[:size]] + [
+        flip(near[c * size : (c + 1) * size], 2 * c) for c in range(1, chips)
+    ]
+
+
+def add_up(parts):
+    return sum(v.astype(F32) for v in parts)
+
+
+def after(values, *others):
+    return lax.optimization_barrier((values, others))[0]
 
 
 def row_shift(values, step):
@@ -387,8 +412,15 @@
     norm_params = jnp.moveaxis(norm_params, 0, 1).reshape(4, model_width).astype(F32)
     ln_gain, ln_bias = norm_params[:2], norm_params[2:]
 
-    qkv_full = lax.all_gather(w_qkv, "row", axis=1, tiled=True)
-    out_full = lax.all_gather(w_out, "row", axis=1, tiled=True)
+    pieces = part_width // lanes
+    w_out = jnp.moveaxis(w_out.reshape(lanes, pieces, lanes), 1, 0).reshape(part_width, lanes)
+    four_full = lax.all_gather(
+        jnp.concatenate([w_qkv, w_out[None]], axis=0), "row", axis=1, tiled=True
+    )
+    qkv_full = four_full[:3]
+    out_full = jnp.moveaxis(four_full[3].reshape(-1, lanes, lanes), 0, 1).reshape(
+        lanes, model_width
+    )
     up_full = lax.all_gather(w_up, "row", axis=0, tiled=True)
     down_full = lax.all_gather(w_down, "row", axis=1, tiled=True)
 
@@ -399,22 +431,27 @@
     resid_in = [layer_in[m].astype(F32) for m in micros]
     first = [normalize(v) for v in resid_in]
     normed1 = [(s * ln_gain[0] + ln_bias[0]).astype(B16) for s, _ in first]
-    rows_one = [spread(v, direct) for v in normed1]
     grad_y = [cotangent[m].astype(F32) for m in micros]
     grad_block = [dwa_weights[prior_count] * g for g in grad_y]
-    grad_rows = [spread(g.astype(B16), direct) for g in grad_block]
+    rows_one, grad_rows, last = [], [], None
+    for values, found in ((normed1, rows_one), (grad_block, grad_rows)):
+        for v in values:
+            v = v.astype(B16)
+            found.append(spread(v if last is None or found is rows_one else after(v, last), direct))
+            last = found[-1][0]
     parts = range(len(rows_one[0]))
     part_rows = group_rows // len(parts)
 
     def part_of(values, n):
         return values[n * part_rows : (n + 1) * part_rows]
 
-    saved, attended = [], []
-    for m in micros:
+    saved, attended, mixed, mixed_parts = [], [], [], []
+    for m in micros:
+        rows_m = after(rows_one[m], grad_rows[0][0], mixed[-1:])
         proj = jnp.concatenate(
             [
                 jnp.einsum("sd,jdh->jsh", v, qkv_full, preferred_element_type=F32)
-                for v in rows_one[m]
+                for v in rows_m
             ],
             axis=1,
         )
@@ -423,43 +460,31 @@
         )
         saved.append((q, k, v, lse))
         attended.append(att)
+        att_m = after(att, mixed_parts[-1] if mixed_parts else grad_rows[-1][0])
+        mixed.append(
+            near_sum(
+                lambda n: jnp.dot(part_of(att_m, n), out_full, preferred_element_type=F32), direct
+            )
+        )
+        mixed_parts.append(send_sum(mixed[-1], direct))
 
     resid, second, rows_two = [], [], []
-    for m in micros:
-        mixed = collapse(
-            lambda n: jnp.dot(part_of(attended[m], n), out_full, preferred_element_type=F32),
-            direct,
-        )
-        resid.append(resid_in[m] + mixed)
+    last = []
+    for m in micros:
+        resid.append(resid_in[m] + add_up(after(mixed_parts[m], last)))
         second.append(normalize(resid[m]))
         normed2 = (second[m][0] * ln_gain[1] + ln_bias[1]).astype(B16)
         rows_two.append(spread(normed2, direct))
-
-    hidden, grad_pre, grad_normed2 = [], [], []
-    for m in micros:
-        pairs = [expand(v, up_full) for v in rows_two[m]]
-        hidden.append([a for a, _ in pairs])
-        grad_pre.append(
-            [
-                (
-                    slope.astype(F32)
-                    * jnp.einsum("sd,fd->sf", g, down_full, preferred_element_type=F32)
-                ).astype(B16)
-                for (_, slope), g in zip(pairs, grad_rows[m])
-            ]
-        )
-        grad_normed2.append(
-            collapse(
-                lambda n: jnp.einsum(
-                    "sf,df->sd", grad_pre[m][n], up_full, preferred_element_type=F32
-                ),
-                direct,
-            )
-        )
+        last = normed2
 
     flat = lambda lists: [v for parts_of in lists for v in parts_of]
     total_rows = micro_count * group_rows
     fit = max(128, (8 << 20) // (2 * total_rows))
+    hidden, slopes = [], []
+    for m in micros:
+        pairs = [expand(v, up_full) for v in rows_two[m]]
+        hidden.append([a for a, _ in pairs])
+        slopes.append([a for _, a in pairs])
     x_tile, y_tile = min(256, units), min(model_width, fit)
     splits = y_tile // part_width if y_tile > part_width else 0
     y_blocks = part_width // y_tile if y_tile < part_width else 1
@@ -473,25 +498,128 @@
         y_tile,
         splits=splits,
     )
+    down_full = after(down_full, grad_down)
     grad_down = lax.psum_scatter(grad_down, "row", scatter_dimension=0)
+
+    grad_pre, back_two = [], []
+    for m in micros:
+        rows_m = after(grad_rows[m], back_two[-1]) if back_two else grad_rows[m]
+        grad_pre.append(
+            [
+                (
+                    slope.astype(F32)
+                    * jnp.einsum("sd,fd->sf", g, down_full, preferred_element_type=F32)
+                ).astype(B16)
+                for slope, g in zip(slopes[m], rows_m)
+            ]
+        )
+        back_two.append(
+            near_sum(
+                lambda n: jnp.einsum(
+                    "sf,df->sd", grad_pre[m][n], up_full, preferred_element_type=F32
+                ),
+                direct,
+            )
+        )
+
+    back_parts = [send_sum(v, direct) for v in back_two]
+    grad_normed2, grad_resid, grad_mixed_rows = [], [], []
+    last = back_two[-1]
     x_tile, y_tile = min(256, model_width), min(units, fit)
-    grad_up = weight_grad(
-        flat(rows_two),
-        flat(grad_pre),
-        (model_width, units),
-        (x_tile, y_tile),
-        lambda i, j: (i, j),
+    for m in micros:
+        grad_normed2.append(add_up(after(back_parts[m], last)))
+        grad_resid.append(grad_block[m] + norm_back(grad_normed2[m], *second[m], ln_gain[1]))
+        grad_mixed = grad_resid[m].astype(B16)
+        grad_mixed_rows.append(spread(grad_mixed, direct))
+        if m == 0:
+            grad_up = weight_grad(
+                flat(rows_two),
+                after(flat(grad_pre), grad_mixed),
+                (model_width, units),
+                (x_tile, y_tile),
+                lambda i, j: (i, j),
+                x_tile,
+                y_tile,
+            )
+            last = grad_up
+    grad_up = lax.psum_scatter(grad_up, "row", scatter_dimension=0, tiled=True)
+
+    branch = []
+    for m in micros:
+        hidden_m = after(hidden[m], branch[-1] if branch else grad_mixed)
+        branch.append(
+            near_sum(
+                lambda n: jnp.dot(hidden_m[n], down_full, preferred_element_type=F32), direct
+            )
+        )
+
+    grad_planes = []
+    last = branch[-1]
+    for m in micros:
+        rows_m = after(grad_mixed_rows[m], last)
+        grad_att = jnp.concatenate(
+            [
+                jnp.einsum("sd,hd->sh", v, out_full, preferred_element_type=F32).astype(B16)
+                for v in rows_m
+            ],
+            axis=0,
+        )
+        grad_planes.append(
+            attention_back(
+                spots, saved[m], grad_att, tables[m], seg_cols[m], seg_rows[m], seq_len, tok_dev
+            )
+        )
+        last = grad_planes[-1]
+
+    four_shape = (row_count, 4, part_width, lanes)
+    grad_four = weight_grad(
+        attended,
+        flat(grad_mixed_rows),
+        four_shape,
+        (None, None, part_width, lanes),
+        lambda i, j: (j, 3, 0, 0),
+        lanes,
+        part_width,
+        stacked=True,
+    )
+    x_tile = min(256, part_width)
+    per_block = part_width // x_tile
+    grad_four = weight_grad(
+        flat(rows_one),
+        grad_planes,
+        four_shape,
+        (None, 3, x_tile, lanes),
+        lambda i, j: (i // per_block, 0, i % per_block, 0),
         x_tile,
-        y_tile,
-    )
-    grad_up = lax.psum_scatter(grad_up, "row", scatter_dimension=0, tiled=True)
+        lanes,
+        planes=3,
+        base=grad_four,
+    )
+    last = grad_four
+    grad_four = lax.psum_scatter(grad_four, "row", scatter_dimension=0)
+
+    in_grads, grad_normed1, back_one = [], [], []
+    for m in micros:
+        planes_m = after(grad_planes[m], last)
+        back_one.append(
+            near_sum(
+                lambda n: jnp.einsum(
+                    "jsh,jdh->sd",
+                    planes_m[:, n * part_rows : (n + 1) * part_rows],
+                    qkv_full,
+                    preferred_element_type=F32,
+                ),
+                direct,
+            )
+        )
+        last = back_one[-1]
+    for m in micros:
+        grad_normed1.append(add_up(send_sum(back_one[m], direct)))
+        in_grads.append(grad_resid[m] + norm_back(grad_normed1[m], *first[m], ln_gain[0]))
 
     outputs, mix_grads = [], []
     for m in micros:
-        branch = collapse(
-            lambda n: jnp.dot(hidden[m][n], down_full, preferred_element_type=F32), direct
-        )
-        block_out = resid[m] + branch
+        block_out = resid[m] + add_up(send_sum(branch[m], direct))
         earlier = earlier_outs[:, m].astype(F32)
         mix_sum = dwa_weights[0] * earlier[0]
         for level in range(1, prior_count):
@@ -506,62 +634,6 @@
             )
         )
 
-    grad_resid, grad_mixed_rows, grad_planes = [], [], []
-    for m in micros:
-        grad_resid.append(grad_block[m] + norm_back(grad_normed2[m], *second[m], ln_gain[1]))
-        grad_mixed_rows.append(spread(grad_resid[m].astype(B16), direct))
-        grad_att = jnp.concatenate(
-            [
-                jnp.einsum("sd,hd->sh", v, out_full, preferred_element_type=F32).astype(B16)
-                for v in grad_mixed_rows[m]
-            ],
-            axis=0,
-        )
-        grad_planes.append(
-            attention_back(
-                spots, saved[m], grad_att, tables[m], seg_cols[m], seg_rows[m], seq_len, tok_dev
-            )
-        )
-
-    grad_wout = weight_grad(
-        attended,
-        flat(grad_mixed_rows),
-        (row_count, lanes, part_width),
-        (None, lanes, part_width),
-        lambda i, j: (j, i, 0),
-        lanes,
-        part_width,
-    )
-    grad_wout = lax.psum_scatter(grad_wout, "row", scatter_dimension=0)
-    x_tile = min(256, part_width)
-    per_block = part_width // x_tile
-    grad_qkv = weight_grad(
-        flat(rows_one),
-        grad_planes,
-        (row_count, 3, part_width, lanes),
-        (None, 3, x_tile, lanes),
-        lambda i, j: (i // per_block, 0, i % per_block, 0),
-        x_tile,
-        lanes,
-        planes=3,
-    )
-    grad_qkv = lax.psum_scatter(grad_qkv, "row", scatter_dimension=0)
-
-    in_grads, grad_normed1 = [], []
-    for m in micros:
-        grad_normed1.append(
-            collapse(
-                lambda n: jnp.einsum(
-                    "jsh,jdh->sd",
-                    grad_planes[m][:, n * part_rows : (n + 1) * part_rows],
-                    qkv_full,
-                    preferred_element_type=F32,
-                ),
-                direct,
-            )
-        )
-        in_grads.append(grad_resid[m] + norm_back(grad_normed1[m], *first[m], ln_gain[0]))
-
     stats = jnp.stack(
         [
             sum(jnp.sum(grad_normed1[m] * first[m][0], axis=0) for m in micros),
@@ -594,8 +666,10 @@
         jnp.stack(outputs),
         jnp.stack(in_grads),
         grad_earlier,
-        grad_qkv.astype(F32),
-        grad_wout.astype(F32),
+        grad_four[:3].astype(F32),
+        jnp.moveaxis(grad_four[3].reshape(pieces, lanes, lanes), 0, 1)
+        .reshape(lanes, part_width)
+        .astype(F32),
         grad_up.astype(F32),
         grad_down.astype(F32),
         slab[:2],

time: 780 us -> 674 us (0.86)
  waiting for transfers between devices: 371 us -> 247 us
  local copies, waits for them, and re-layouts: 34.1 us -> 43.6 us
  other arithmetic: 70.8 us -> 79.1 us
    reduce_scatter x2 -> x1, waiting for transfers between devices: 48.9 us -> 0.01 us  [body(): grad_four = lax.psum_scatter(grad_four, 'row', scatter_dimension=0)]
    ppermute x67, waiting for transfers between devices: 288 us -> 245 us  [flip(): return lax.ppermute(values, 'col', [(i, i ^ bits) for i in range(count)])]
    all_gather x1, waiting for transfers between devices: 19.1 us -> 0.01 us  [body(): down_full = lax.all_gather(w_down, 'row', axis=1, tiled=True)]
    slice x8 -> x11, local copies, waits for them, and re-layouts: 1.91 us -> 11.8 us  [the longest x8 8.98 us: send_sum(): near[c * size:(c + 1) * size]]
    all_gather x2 -> x1, waiting for transfers between devices: 8.18 us -> 0.01 us  [body(): lax.all_gather(jnp.concatenate([w_qkv, w_out[None]], axis=0), 'row', axis...]
    unnamed x262 -> x236, local copies, waits for them, and re-layouts: 23.5 us -> 16.8 us
  transfers between devices with their start and end apart: 81 -> 79, of which waited for: 50 -> 36; matrix products, arithmetic and copies ran while one was open for 21% -> 26% of each run, Pallas kernels for 14% -> 16%
where the time goes in v2:
time: 674 us; the launch traced here: 670 us
  waiting for transfers between devices  247 us (37%)
  Pallas kernels  115 us (17%)
  matrix products  94.4 us (14%)
  other arithmetic  79.1 us (12%)
  starting transfers between devices  74.1 us (11%)
  local copies, waits for them, and re-layouts  43.6 us (6%)
  between operations  16.4 us (2%)
    ppermute x67, waiting for transfers between devices, flip(): return lax.ppermute(values, 'col', [(i, i ^ bits) for i in range(count)])  245 us
    ppermute x67, starting transfers between devices, flip(): return lax.ppermute(values, 'col', [(i, i ^ bits) for i in range(count)])  61.8 us
    pallas_call x4, Pallas kernels, weight_grad(): pl.pallas_call(functools.partial(weight_kernel, x_count=len(xs), y_count=...  45.6 us
    pallas_call x2, Pallas kernels, attention_back(): pl.pallas_call(functools.partial(attend_backward, piece=piece, blk=min(25...  25.7 us
    pallas_call x4, Pallas kernels, expand(): pl.pallas_call(expand_kernel, out_shape=(full, full), grid=(rows // strip...  23.8 us
    pallas_call x2, Pallas kernels, attention(): pl.pallas_call(functools.partial(attend_forward, piece=piece, blk=min(256...  19.7 us
    dot_general x4, matrix products, body(): jnp.einsum('sd,fd->sf', g, down_full, preferred_element_type=F32)  17.8 us
    dot_general x4, matrix products, body(): jnp.einsum('jsh,jdh->sd', planes_m[:, n * part_rows:(n + 1) * part_rows],...  17.7 us
  transfers between devices with their start and end apart: 79, of which 36 were waited for; matrix products, arithmetic and copies ran while one was open for 26% of the time, Pallas kernels for 16%

profile of v2, /device:TPU:0, one launch (start us, length us, event | category | flops | bytes accessed | tf_op | source)
XLA Modules:
  0.0 669.6 jit_solution(2264903952840855891)
XLA Ops:
  8.0 3.1 collective-permute-start
  29.1 7.3 %collective-permute-done.7 = bf16[128,2048]{1,0:T(8,128)(2,1)S(1)} collective-permute-done((bf16[128,2048]{1,0:T(8,128)(2,1)S(1)}, bf16[128,2048]{1,0:T(8,128)(2,1)S(1)}, u32[]{:S(2)}, u32[]{:S(2)}) %collective-permute-start.7) | collective-permute-done | bytes 524320 | tf_op jit(solution)/shard_map/ppermute | solution.py:330
  40.8 9.3 %collective-permute-done.8 = bf16[128,2048]{1,0:T(8,128)(2,1)S(1)} collective-permute-done((bf16[128,2048]{1,0:T(8,128)(2,1)S(1)}, bf16[128,2048]{1,0:T(8,128)(2,1)S(1)}, u32[]{:S(2)}, u32[]{:S(2)}) %collective-permute-start.8) | collective-permute-done | bytes 524320 | tf_op jit(solution)/shard_map/ppermute | solution.py:330
  54.3 4.6 collective-permute-done.3
  61.4 11.1 %collective-permute-done.4 = bf16[128,2048]{1,0:T(8,128)(2,1)S(1)} collective-permute-done((bf16[128,2048]{1,0:T(8,128)(2,1)}, bf16[128,2048]{1,0:T(8,128)(2,1)S(1)}, u32[]{:S(2)}, u32[]{:S(2)}) %collective-permute-start.4) | collective-permute-done | bytes 524320 | tf_op jit(solution)/shard_map/ppermute | solution.py:330
  76.0 5.5 collective-permute-done.10
  83.4 9.3 %collective-permute-done.11 = bf16[128,2048]{1,0:T(8,128)(2,1)S(1)} collective-permute-done((bf16[128,2048]{1,0:T(8,128)(2,1)S(1)}, bf16[128,2048]{1,0:T(8,128)(2,1)S(1)}, u32[]{:S(2)}, u32[]{:S(2)}) %collective-permute-start.11) | collective-permute-done | bytes 524320 | tf_op jit(solution)/shard_map/ppermute | solution.py:330
  108.1 9.7 %collective-permute-done.14 = bf16[128,2048]{1,0:T(8,128)(2,1)} collective-permute-done((bf16[128,2048]{1,0:T(8,128)(2,1)S(1)}, bf16[128,2048]{1,0:T(8,128)(2,1)}, u32[]{:S(2)}, u32[]{:S(2)}) %collective-permute-start.14) | collective-permute-done | bytes 524320 | tf_op jit(solution)/shard_map/ppermute | solution.py:330
  120.5 3.9 fusion.16
  124.4 3.4 fusion.19
  129.7 9.9 %attend_forward.2 = (bf16[1024,256]{1,0:T(8,128)(2,1)S(1)}, bf16[1024,256]{1,0:T(8,128)(2,1)S(1)}, bf16[1024,256]{1,0:T(8,128)(2,1)S(1)}, bf16[1024,256]{1,0:T(8,128)(2,1)S(1)}, f32[4,8,1024]{2,1,0:T(8,128)S(1)}) custom-call(s32[8]{0:T(128)S(1)} %shift-right-arithmetic_add_fusion.spot_ref, f32[3,1024,256]{2,1,0:T(8,128)} %pad_maximum_fusion.q_in.k_in.v_in, ...), custom_call_target="tpu_custom_call" | custom-call | flops 4294967296 | bytes 6291456 | tf_op jit(solution)/shard_map/attend_forward/pallas_call | solution.py:181
  148.6 3.0 add_convert_fusion.5
  157.8 3.4 fusion.25
  163.2 9.9 %attend_forward.3 = (bf16[1024,256]{1,0:T(8,128)(2,1)S(1)}, bf16[1024,256]{1,0:T(8,128)(2,1)S(1)}, bf16[1024,256]{1,0:T(8,128)(2,1)S(1)}, bf16[1024,256]{1,0:T(8,128)(2,1)S(1)}, f32[4,8,1024]{2,1,0:T(8,128)S(1)}) custom-call(s32[8]{0:T(128)S(1)} %shift-right-arithmetic_add_fusion.spot_ref, f32[3,1024,256]{2,1,0:T(8,128)} %pad_maximum_fusion.1.q_in.k_in.v_in, ...), custom_call_target="tpu_custom_call" | custom-call | flops 4294967296 | bytes 6291456 | tf_op jit(solution)/shard_map/attend_forward/pallas_call | solution.py:181
  193.2 9.0 %collective-permute-done.26 = bf16[128,2048]{1,0:T(8,128)(2,1)S(1)} collective-permute-done((bf16[128,2048]{1,0:T(8,128)(2,1)S(1)}, bf16[128,2048]{1,0:T(8,128)(2,1)S(1)}, u32[]{:S(2)}, u32[]{:S(2)}) %collective-permute-start.26) | collective-permute-done | bytes 524320 | tf_op jit(solution)/shard_map/ppermute | solution.py:330
  203.6 11.2 %collective-permute-done.27 = bf16[128,2048]{1,0:T(8,128)(2,1)S(1)} collective-permute-done((bf16[128,2048]{1,0:T(8,128)(2,1)S(1)}, bf16[128,2048]{1,0:T(8,128)(2,1)S(1)}, u32[]{:S(2)}, u32[]{:S(2)}) %collective-permute-start.27) | collective-permute-done | bytes 524320 | tf_op jit(solution)/shard_map/ppermute | solution.py:330
  217.7 7.0 %collective-permute-done.20 = bf16[128,2048]{1,0:T(8,128)(2,1)S(1)} collective-permute-done((bf16[128,2048]{1,0:T(8,128)(2,1)S(1)}, bf16[128,2048]{1,0:T(8,128)(2,1)S(1)}, u32[]{:S(2)}, u32[]{:S(2)}) %collective-permute-start.20) | collective-permute-done | bytes 524320 | tf_op jit(solution)/shard_map/ppermute | solution.py:330
  226.1 11.1 %collective-permute-done.21 = bf16[128,2048]{1,0:T(8,128)(2,1)S(1)} collective-permute-done((bf16[128,2048]{1,0:T(8,128)(2,1)S(1)}, bf16[128,2048]{1,0:T(8,128)(2,1)S(1)}, u32[]{:S(2)}, u32[]{:S(2)}) %collective-permute-start.21) | collective-permute-done | bytes 524320 | tf_op jit(solution)/shard_map/ppermute | solution.py:330
  237.6 9.6 %collective-permute-done.29 = bf16[128,2048]{1,0:T(8,128)(2,1)S(1)} collective-permute-done((bf16[128,2048]{1,0:T(8,128)(2,1)S(1)}, bf16[128,2048]{1,0:T(8,128)(2,1)S(1)}, u32[]{:S(2)}, u32[]{:S(2)}) %collective-permute-start.29) | collective-permute-done | bytes 524320 | tf_op jit(solution)/shard_map/ppermute | solution.py:330
  247.2 11.4 %collective-permute-done.30 = bf16[128,2048]{1,0:T(8,128)(2,1)S(1)} collective-permute-done((bf16[128,2048]{1,0:T(8,128)(2,1)S(1)}, bf16[128,2048]{1,0:T(8,128)(2,1)S(1)}, u32[]{:S(2)}, u32[]{:S(2)}) %collective-permute-start.30) | collective-permute-done | bytes 524320 | tf_op jit(solution)/shard_map/ppermute | solution.py:330
  260.7 5.3 expand.4
  266.9 6.3 expand.5
  274.2 5.9 expand.6
  280.1 6.3 expand.7
  287.5 14.6 %weight_grad.4 = bf16[4,1024,512]{2,1,0:T(8,128)(2,1)} custom-call(bf16[512,1024]{1,0:T(8,128)(2,1)S(1)} %get-tuple-element.118.refs_0_, bf16[512,1024]{1,0:T(8,128)(2,1)S(1)} %get-tuple-element.119.refs_1_, bf16[512,1024]{1,0:T(8,128)(2,1)S(1)} %get-tuple-element.120.refs_2_, bf16[512,1024]{1,0:T(8,128)(2,1)S(1)} %get-tuple-element.121.refs_3_, ...), custom_call_target="tpu_custom_call" | custom-call | flops 8589934592 | bytes 16777216 | tf_op jit(solution)/shard_map/weight_grad/pallas_call | solution.py:303
  303.1 5.6 multiply_convert_fusion.2.refs_5_
  311.7 4.0 multiply_convert_fusion.3.refs_4_
  315.8 3.7 add_convert_fusion.3
  319.5 4.0 multiply_convert_fusion.refs_7_
  323.5 3.7 convolution_convert_fusion.2
  333.5 4.2 multiply_convert_fusion.1.refs_6_
  337.8 4.1 add_convert_fusion.2
  341.9 2.9 collective-permute-done.40
  344.8 11.0 %collective-permute-done.41 = bf16[128,2048]{1,0:T(8,128)(2,1)S(1)} collective-permute-done((bf16[128,2048]{1,0:T(8,128)(2,1)S(1)}, bf16[128,2048]{1,0:T(8,128)(2,1)S(1)}, u32[]{:S(2)}, u32[]{:S(2)}) %collective-permute-start.41) | collective-permute-done | bytes 524320 | tf_op jit(solution)/shard_map/ppermute | solution.py:330
  364.3 12.7 %weight_grad.5 = bf16[2048,1024]{1,0:T(8,128)(2,1)} custom-call(bf16[512,2048]{1,0:T(8,128)(2,1)} %copy-done.2, bf16[512,2048]{1,0:T(8,128)(2,1)} %collective-permute-done.23.x_ref.refs_1_, bf16[512,2048]{1,0:T(8,128)(2,1)} %pad_maximum_fusion.5.x_ref.refs_2_, bf16[512,2048]{1,0:T(8,128)(2,1)} %collective-permute-done.33.x_ref.refs_3_, ...), custom_call_target="tpu_custom_call" | custom-call | flops 8589934592 | bytes 16777216 | tf_op jit(solution)/shard_map/weight_grad/pallas_call | solution.py:303
  376.9 9.7 %collective-permute-done.38 = bf16[128,2048]{1,0:T(8,128)(2,1)} collective-permute-done((bf16[128,2048]{1,0:T(8,128)(2,1)}, bf16[128,2048]{1,0:T(8,128)(2,1)}, u32[]{:S(2)}, u32[]{:S(2)}) %collective-permute-start.38) | collective-permute-done | bytes 524320 | tf_op jit(solution)/shard_map/ppermute | solution.py:330
  397.9 10.7 %collective-permute-done.51 = bf16[128,2048]{1,0:T(8,128)(2,1)S(1)} collective-permute-done((bf16[128,2048]{1,0:T(8,128)(2,1)S(1)}, bf16[128,2048]{1,0:T(8,128)(2,1)S(1)}, u32[]{:S(2)}, u32[]{:S(2)}) %collective-permute-start.51) | collective-permute-done | bytes 524320 | tf_op jit(solution)/shard_map/ppermute | solution.py:330
  409.2 10.5 %collective-permute-done.52 = bf16[128,2048]{1,0:T(8,128)(2,1)S(1)} collective-permute-done((bf16[128,2048]{1,0:T(8,128)(2,1)S(1)}, bf16[128,2048]{1,0:T(8,128)(2,1)S(1)}, u32[]{:S(2)}, u32[]{:S(2)}) %collective-permute-start.52) | collective-permute-done | bytes 524320 | tf_op jit(solution)/shard_map/ppermute | solution.py:330
  421.5 9.7 %collective-permute-done.55 = bf16[128,2048]{1,0:T(8,128)(2,1)S(1)} collective-permute-done((bf16[128,2048]{1,0:T(8,128)(2,1)S(1)}, bf16[128,2048]{1,0:T(8,128)(2,1)S(1)}, u32[]{:S(2)}, u32[]{:S(2)}) %collective-permute-start.55) | collective-permute-done | bytes 524320 | tf_op jit(solution)/shard_map/ppermute | solution.py:330
  431.2 11.0 %collective-permute-done.56 = bf16[128,2048]{1,0:T(8,128)(2,1)S(1)} collective-permute-done((bf16[128,2048]{1,0:T(8,128)(2,1)S(1)}, bf16[128,2048]{1,0:T(8,128)(2,1)S(1)}, u32[]{:S(2)}, u32[]{:S(2)}) %collective-permute-start.56) | collective-permute-done | bytes 524320 | tf_op jit(solution)/shard_map/ppermute | solution.py:330
  443.7 3.7 add_convert_fusion.1
  447.4 3.7 convolution_convert_fusion
  454.5 6.9 %weight_grad.6.refs_6_ = bf16[4,4,512,256]{3,2,1,0:T(8,128)(2,1)} custom-call(bf16[1024,256]{1,0:T(8,128)(2,1)S(1)} %get-tuple-element.80.refs_0_, bf16[1024,256]{1,0:T(8,128)(2,1)S(1)} %get-tuple-element.92.refs_1_, bf16[512,2048]{1,0:T(8,128)(2,1)S(1)} %pad_maximum_fusion.6.refs_2_, bf16[512,2048]{1,0:T(8,128)(2,1)} %collective-permute-done.54.refs_3_, ...), custom_call_target="tpu_custom_call" | custom-call | flops 2147483648 | bytes 10485760 | tf_op jit(solution)/shard_map/weight_grad/pallas_call | solution.py:303
  461.4 5.3 add_convert_fusion
  470.1 12.8 %attend_backward.2.refs_4_ = bf16[3,1024,256]{2,1,0:T(8,128)(2,1)S(1)} custom-call(s32[8]{0:T(128)S(1)} %shift-right-arithmetic_add_fusion.spot_ref, bf16[1024,256]{1,0:T(8,128)(2,1)S(1)} %copy-done.33, bf16[1024,256]{1,0:T(8,128)(2,1)S(1)} %copy-done.35, bf16[1024,256]{1,0:T(8,128)(2,1)S(1)} %copy-done.37, bf16[1024,256]{1,0:T(8,128)(2,1)S(1)} %pad_maximum_fusion.11.g_in, ...), custom_call_target="tpu_custom_call" | custom-call | flops 6442450944 | bytes 6291456 | tf_op jit(solution)/shard_map/attend_backward/pallas_call | solution.py:204
  487.8 13.0 %attend_backward.3.refs_5_ = bf16[3,1024,256]{2,1,0:T(8,128)(2,1)S(1)} custom-call(s32[8]{0:T(128)S(1)} %shift-right-arithmetic_add_fusion.spot_ref, bf16[1024,256]{1,0:T(8,128)(2,1)S(1)} %copy-done.39, bf16[1024,256]{1,0:T(8,128)(2,1)S(1)} %copy-done.41, bf16[1024,256]{1,0:T(8,128)(2,1)S(1)} %copy-done.43, bf16[1024,256]{1,0:T(8,128)(2,1)S(1)} %pad_maximum_fusion.12.g_in, ...), custom_call_target="tpu_custom_call" | custom-call | flops 6442450944 | bytes 6291456 | tf_op jit(solution)/shard_map/attend_backward/pallas_call | solution.py:204
  500.8 11.4 %weight_grad.7 = bf16[4,4,512,256]{3,2,1,0:T(8,128)(2,1)} custom-call(bf16[512,2048]{1,0:T(8,128)(2,1)S(1)} %copy-done.1, bf16[512,2048]{1,0:T(8,128)(2,1)} %collective-permute-done.6.refs_1_, bf16[512,2048]{1,0:T(8,128)(2,1)} %pad_maximum_fusion.3.refs_2_, bf16[512,2048]{1,0:T(8,128)(2,1)} %collective-permute-done.24.refs_3_, ...), custom_call_target="tpu_custom_call", output_to_operand_aliasing={{}: (6, {})} | custom-call | flops 6442450944 | bytes 10485760 | tf_op jit(solution)/shard_map/weight_grad/pallas_call | solution.py:303
  512.2 5.2 bitcast_convert_fusion.1
  521.4 6.8 %slice_convert_fusion.1 = (f32[4,1,128,2048]{3,2,1,0:T(8,128)}, f32[4,1,128,2048]{3,2,1,0:T(8,128)}) fusion(bf16[4,2,128,2048]{3,2,1,0:T(8,128)(2,1)} %param.13), kind=kLoop, calls=%fused_computation.45 | loop fusion | flops 2097152 | bytes 12582912 | tf_op jit(solution)/shard_map/convert_element_type | solution.py:623
  528.1 4.5 broadcast_multiply_fusion
  537.4 5.9 fusion.3
  543.3 3.1 bitcast_convert_fusion
  550.2 11.1 %collective-permute-done.45 = bf16[128,2048]{1,0:T(8,128)(2,1)} collective-permute-done((bf16[128,2048]{1,0:T(8,128)(2,1)}, bf16[128,2048]{1,0:T(8,128)(2,1)}, u32[]{:S(2)}, u32[]{:S(2)}) %collective-permute-start.45) | collective-permute-done | bytes 524320 | tf_op jit(solution)/shard_map/ppermute | solution.py:330
  561.3 5.5 fusion.79
  566.8 3.0 bitcast_convert_fusion.2
  571.5 11.8 %collective-permute-done.49 = bf16[128,2048]{1,0:T(8,128)(2,1)} collective-permute-done((bf16[128,2048]{1,0:T(8,128)(2,1)}, bf16[128,2048]{1,0:T(8,128)(2,1)}, u32[]{:S(2)}, u32[]{:S(2)}) %collective-permute-start.49) | collective-permute-done | bytes 524320 | tf_op jit(solution)/shard_map/ppermute | solution.py:330
  583.3 7.1 %fusion.80 = bf16[1,128,2048]{2,1,0:T(8,128)(2,1)S(1)} fusion(f32[]{:T(128)} %bitcast.5, f32[4,1,128,2048]{3,2,1,0:T(8,128)} %get-tuple-element.175, f32[]{:T(128)} %bitcast.3, f32[]{:T(128)} %bitcast.2, f32[]{:T(128)} %bitcast.1, f32[]{:T(128)} %bitcast, f32[128,2048]{1,0:T(8,128)S(1)} %copy-done.49, bf16[128,2048]{1,0:T(8,128)(2,1)} %collective-permute-done.50, ...), kind=kLoop, calls=%fused_computation.157 | loop fusion | flops 4718592 | bytes 7864340 | tf_op jit(solution)/shard_map/stack | solution.py:666
  595.1 3.5 fusion.2
  601.5 4.8 collective-permute-done.60
  607.6 3.7 multiply_reduce_fusion
  613.9 2.9 convert_element_type.432
  618.6 10.4 %collective-permute-done.64 = bf16[128,2048]{1,0:T(8,128)(2,1)} collective-permute-done((bf16[128,2048]{1,0:T(8,128)(2,1)}, bf16[128,2048]{1,0:T(8,128)(2,1)}, u32[]{:S(2)}, u32[]{:S(2)}) %collective-permute-start.64) | collective-permute-done | bytes 524320 | tf_op jit(solution)/shard_map/ppermute | solution.py:330
  629.0 10.3 %collective-permute-done.65 = bf16[128,2048]{1,0:T(8,128)(2,1)} collective-permute-done((bf16[128,2048]{1,0:T(8,128)(2,1)}, bf16[128,2048]{1,0:T(8,128)(2,1)}, u32[]{:S(2)}, u32[]{:S(2)}) %collective-permute-start.65) | collective-permute-done | bytes 524320 | tf_op jit(solution)/shard_map/ppermute | solution.py:330
  639.3 3.5 fusion.60
  (493 shorter events, 194.8 us)
Async XLA Ops:
  7.2 113.3 %all-gather.4.cloned.1.call-start = ((), (), s32[]{:S(2)}) async-start(), calls=%async_computation.3 | async-start | bytes 5242880 | tf_op jit(solution)/shard_map/all_gather | solution.py:417
  8.0 11.7 %collective-permute-start = (bf16[4,512]{1,0:T(4,128)(2,1)S(1)}, bf16[4,512]{1,0:T(4,128)(2,1)S(1)}, u32[]{:S(2)}, u32[]{:S(2)}) collective-permute-start(bf16[4,512]{1,0:T(4,128)(2,1)S(1)} %pad_maximum_fusion.15), channel_id=1, source_target_pairs={{0,8},{8,16},{16,24},{24,0},{1,9},{9,17},{17,25},{25,1},{2,10},{10... | collective-permute-start | bytes 12296 | tf_op jit(solution)/shard_map/ppermute | solution.py:368
  18.2 242.5 %all-gather.6.cloned.1.call-start = ((), (), s32[]{:S(2)}) async-start(), calls=%async_computation.4 | async-start | bytes 5242880 | tf_op jit(solution)/shard_map/all_gather | solution.py:424
  21.6 14.8 %collective-permute-start.7 = (bf16[128,2048]{1,0:T(8,128)(2,1)S(1)}, bf16[128,2048]{1,0:T(8,128)(2,1)S(1)}, u32[]{:S(2)}, u32[]{:S(2)}) collective-permute-start(bf16[128,2048]{1,0:T(8,128)(2,1)S(1)} %get-tuple-element.205), channel_id=1, source_target_pairs={{0,2},{1,3},{2,0},{3,1},{4,6},{5,7},{6,4},{7,5},{8,10},{9,11},{10,... | collective-permute-start | bytes 1572872 | tf_op jit(solution)/shard_map/ppermute | solution.py:330
  24.0 26.1 %collective-permute-start.8 = (bf16[128,2048]{1,0:T(8,128)(2,1)S(1)}, bf16[128,2048]{1,0:T(8,128)(2,1)S(1)}, u32[]{:S(2)}, u32[]{:S(2)}) collective-permute-start(bf16[128,2048]{1,0:T(8,128)(2,1)S(1)} %get-tuple-element.205), channel_id=1, source_target_pairs={{0,4},{1,5},{2,6},{3,7},{4,0},{5,1},{6,2},{7,3},{8,12},{9,13},{10,... | collective-permute-start | bytes 1572872 | tf_op jit(solution)/shard_map/ppermute | solution.py:330
  25.5 24.5 %collective-permute-start.9 = (bf16[128,2048]{1,0:T(8,128)(2,1)S(1)}, bf16[128,2048]{1,0:T(8,128)(2,1)S(1)}, u32[]{:S(2)}, u32[]{:S(2)}) collective-permute-start(bf16[128,2048]{1,0:T(8,128)(2,1)S(1)} %get-tuple-element.205), channel_id=1, source_target_pairs={{0,6},{1,7},{2,4},{3,5},{4,2},{5,3},{6,0},{7,1},{8,14},{9,15},{10,... | collective-permute-start | bytes 1572872 | tf_op jit(solution)/shard_map/ppermute | solution.py:330
  26.0 32.9 %collective-permute-start.3 = (bf16[128,2048]{1,0:T(8,128)(2,1)}, bf16[128,2048]{1,0:T(8,128)(2,1)S(1)}, u32[]{:S(2)}, u32[]{:S(2)}) collective-permute-start(bf16[128,2048]{1,0:T(8,128)(2,1)} %get-tuple-element.204), channel_id=1, source_target_pairs={{0,2},{1,3},{2,0},{3,1},{4,6},{5,7},{6,4},{7,5},{8,10},{9,11},{10,... | collective-permute-start | bytes 1572872 | tf_op jit(solution)/shard_map/ppermute | solution.py:330
  27.6 44.9 %collective-permute-start.4 = (bf16[128,2048]{1,0:T(8,128)(2,1)}, bf16[128,2048]{1,0:T(8,128)(2,1)S(1)}, u32[]{:S(2)}, u32[]{:S(2)}) collective-permute-start(bf16[128,2048]{1,0:T(8,128)(2,1)} %get-tuple-element.204), channel_id=1, source_target_pairs={{0,4},{1,5},{2,6},{3,7},{4,0},{5,1},{6,2},{7,3},{8,12},{9,13},{10,... | collective-permute-start | bytes 1572872 | tf_op jit(solution)/shard_map/ppermute | solution.py:330
  36.4 36.9 %collective-permute-start.5 = (bf16[128,2048]{1,0:T(8,128)(2,1)}, bf16[128,2048]{1,0:T(8,128)(2,1)}, u32[]{:S(2)}, u32[]{:S(2)}) collective-permute-start(bf16[128,2048]{1,0:T(8,128)(2,1)} %get-tuple-element.204), channel_id=1, source_target_pairs={{0,6},{1,7},{2,4},{3,5},{4,2},{5,3},{6,0},{7,1},{8,14},{9,15},{10,... | collective-permute-start | bytes 1572872 | tf_op jit(solution)/shard_map/ppermute | solution.py:330
  51.6 30.0 %collective-permute-start.10 = (bf16[128,2048]{1,0:T(8,128)(2,1)S(1)}, bf16[128,2048]{1,0:T(8,128)(2,1)}, u32[]{:S(2)}, u32[]{:S(2)}) collective-permute-start(bf16[128,2048]{1,0:T(8,128)(2,1)S(1)} %get-tuple-element.73), channel_id=1, source_target_pairs={{0,2},{1,3},{2,0},{3,1},{4,6},{5,7},{6,4},{7,5},{8,10},{9,11},{10,... | collective-permute-start | bytes 1572872 | tf_op jit(solution)/shard_map/ppermute | solution.py:330
  52.8 39.9 %collective-permute-start.11 = (bf16[128,2048]{1,0:T(8,128)(2,1)S(1)}, bf16[128,2048]{1,0:T(8,128)(2,1)S(1)}, u32[]{:S(2)}, u32[]{:S(2)}) collective-permute-start(bf16[128,2048]{1,0:T(8,128)(2,1)S(1)} %get-tuple-element.73), channel_id=1, source_target_pairs={{0,4},{1,5},{2,6},{3,7},{4,0},{5,1},{6,2},{7,3},{8,12},{9,13},{10,... | collective-permute-start | bytes 1572872 | tf_op jit(solution)/shard_map/ppermute | solution.py:330
  58.9 34.7 %collective-permute-start.12 = (bf16[128,2048]{1,0:T(8,128)(2,1)S(1)}, bf16[128,2048]{1,0:T(8,128)(2,1)S(1)}, u32[]{:S(2)}, u32[]{:S(2)}) collective-permute-start(bf16[128,2048]{1,0:T(8,128)(2,1)S(1)} %get-tuple-element.73), channel_id=1, source_target_pairs={{0,6},{1,7},{2,4},{3,5},{4,2},{5,3},{6,0},{7,1},{8,14},{9,15},{10,... | collective-permute-start | bytes 1572872 | tf_op jit(solution)/shard_map/ppermute | solution.py:330
  75.1 45.4 %collective-permute-start.6 = (bf16[512,2048]{1,0:T(8,128)(2,1)S(1)}, bf16[512,2048]{1,0:T(8,128)(2,1)}, u32[]{:S(2)}, u32[]{:S(2)}) collective-permute-start(bf16[512,2048]{1,0:T(8,128)(2,1)S(1)} %pad_maximum_fusion.2.refs_0_), channel_id=1, source_target_pairs={{0,1},{1,0},{2,3},{3,2},{4,5},{5,4},{6,7},{7,6},{8,9},{9,8},{10,11... | collective-permute-start | bytes 6291464 | tf_op jit(solution)/shard_map/ppermute | solution.py:330
  94.4 11.8 %collective-permute-start.13 = (bf16[128,2048]{1,0:T(8,128)(2,1)S(1)}, bf16[128,2048]{1,0:T(8,128)(2,1)}, u32[]{:S(2)}, u32[]{:S(2)}) collective-permute-start(bf16[128,2048]{1,0:T(8,128)(2,1)S(1)} %get-tuple-element.79), channel_id=1, source_target_pairs={{0,2},{1,3},{2,0},{3,1},{4,6},{5,7},{6,4},{7,5},{8,10},{9,11},{10,... | collective-permute-start | bytes 1572872 | tf_op jit(solution)/shard_map/ppermute | solution.py:330
  95.6 22.2 %collective-permute-start.14 = (bf16[128,2048]{1,0:T(8,128)(2,1)S(1)}, bf16[128,2048]{1,0:T(8,128)(2,1)}, u32[]{:S(2)}, u32[]{:S(2)}) collective-permute-start(bf16[128,2048]{1,0:T(8,128)(2,1)S(1)} %get-tuple-element.79), channel_id=1, source_target_pairs={{0,4},{1,5},{2,6},{3,7},{4,0},{5,1},{6,2},{7,3},{8,12},{9,13},{10,... | collective-permute-start | bytes 1572872 | tf_op jit(solution)/shard_map/ppermute | solution.py:330
  103.8 15.8 %collective-permute-start.15 = (bf16[128,2048]{1,0:T(8,128)(2,1)S(1)}, bf16[128,2048]{1,0:T(8,128)(2,1)S(1)}, u32[]{:S(2)}, u32[]{:S(2)}) collective-permute-start(bf16[128,2048]{1,0:T(8,128)(2,1)S(1)} %get-tuple-element.79), channel_id=1, source_target_pairs={{0,6},{1,7},{2,4},{3,5},{4,2},{5,3},{6,0},{7,1},{8,14},{9,15},{10,... | collective-permute-start | bytes 1572872 | tf_op jit(solution)/shard_map/ppermute | solution.py:330
  144.1 159.0 %all-gather.8.cloned.1.call-start = ((), (), s32[]{:S(2)}) async-start(), calls=%async_computation.5 | async-start | bytes 5242880 | tf_op jit(solution)/shard_map/all_gather | solution.py:425
  152.5 23.0 %collective-permute-start.17 = (bf16[128,2048]{1,0:T(8,128)(2,1)S(1)}, bf16[128,2048]{1,0:T(8,128)(2,1)S(1)}, u32[]{:S(2)}, u32[]{:S(2)}) collective-permute-start(bf16[128,2048]{1,0:T(8,128)(2,1)S(1)} %get-tuple-element.202), channel_id=1, source_target_pairs={{0,2},{1,3},{2,0},{3,1},{4,6},{5,7},{6,4},{7,5},{8,10},{9,11},{10,... | collective-permute-start | bytes 1572872 | tf_op jit(solution)/shard_map/ppermute | solution.py:330
  153.2 24.9 %collective-permute-start.18 = (bf16[128,2048]{1,0:T(8,128)(2,1)S(1)}, bf16[128,2048]{1,0:T(8,128)(2,1)S(1)}, u32[]{:S(2)}, u32[]{:S(2)}) collective-permute-start(bf16[128,2048]{1,0:T(8,128)(2,1)S(1)} %get-tuple-element.201), channel_id=1, source_target_pairs={{0,4},{1,5},{2,6},{3,7},{4,0},{5,1},{6,2},{7,3},{8,12},{9,13},{10,... | collective-permute-start | bytes 1572872 | tf_op jit(solution)/shard_map/ppermute | solution.py:330
  153.9 24.2 %collective-permute-start.19 = (bf16[128,2048]{1,0:T(8,128)(2,1)S(1)}, bf16[128,2048]{1,0:T(8,128)(2,1)S(1)}, u32[]{:S(2)}, u32[]{:S(2)}) collective-permute-start(bf16[128,2048]{1,0:T(8,128)(2,1)S(1)} %get-tuple-element.200), channel_id=1, source_target_pairs={{0,6},{1,7},{2,4},{3,5},{4,2},{5,3},{6,0},{7,1},{8,14},{9,15},{10,... | collective-permute-start | bytes 1572872 | tf_op jit(solution)/shard_map/ppermute | solution.py:330
  180.2 386.6 %reduce-scatter.8.cloned.1.call-start = ((), (), s32[]{:S(2)}) async-start(), calls=%async_computation.8 | async-start | bytes 5242880 | tf_op jit(solution)/shard_map/reduce_scatter | solution.py:502
  187.3 14.9 %collective-permute-start.26 = (bf16[128,2048]{1,0:T(8,128)(2,1)S(1)}, bf16[128,2048]{1,0:T(8,128)(2,1)S(1)}, u32[]{:S(2)}, u32[]{:S(2)}) collective-permute-start(bf16[128,2048]{1,0:T(8,128)(2,1)S(1)} %get-tuple-element.198), channel_id=1, source_target_pairs={{0,2},{1,3},{2,0},{3,1},{4,6},{5,7},{6,4},{7,5},{8,10},{9,11},{10,... | collective-permute-start | bytes 1572872 | tf_op jit(solution)/shard_map/ppermute | solution.py:330
  188.8 26.0 %collective-permute-start.27 = (bf16[128,2048]{1,0:T(8,128)(2,1)S(1)}, bf16[128,2048]{1,0:T(8,128)(2,1)S(1)}, u32[]{:S(2)}, u32[]{:S(2)}) collective-permute-start(bf16[128,2048]{1,0:T(8,128)(2,1)S(1)} %get-tuple-element.197), channel_id=1, source_target_pairs={{0,4},{1,5},{2,6},{3,7},{4,0},{5,1},{6,2},{7,3},{8,12},{9,13},{10,... | collective-permute-start | bytes 1572872 | tf_op jit(solution)/shard_map/ppermute | solution.py:330
  189.4 25.4 %collective-permute-start.28 = (bf16[128,2048]{1,0:T(8,128)(2,1)S(1)}, bf16[128,2048]{1,0:T(8,128)(2,1)S(1)}, u32[]{:S(2)}, u32[]{:S(2)}) collective-permute-start(bf16[128,2048]{1,0:T(8,128)(2,1)S(1)} %get-tuple-element.196), channel_id=1, source_target_pairs={{0,6},{1,7},{2,4},{3,5},{4,2},{5,3},{6,0},{7,1},{8,14},{9,15},{10,... | collective-permute-start | bytes 1572872 | tf_op jit(solution)/shard_map/ppermute | solution.py:330
  191.1 33.6 %collective-permute-start.20 = (bf16[128,2048]{1,0:T(8,128)(2,1)S(1)}, bf16[128,2048]{1,0:T(8,128)(2,1)S(1)}, u32[]{:S(2)}, u32[]{:S(2)}) collective-permute-start(bf16[128,2048]{1,0:T(8,128)(2,1)S(1)} %add_convert_fusion.7), channel_id=1, source_target_pairs={{0,2},{1,3},{2,0},{3,1},{4,6},{5,7},{6,4},{7,5},{8,10},{9,11},{10,... | collective-permute-start | bytes 1572872 | tf_op jit(solution)/shard_map/ppermute | solution.py:330
  192.6 44.7 %collective-permute-start.21 = (bf16[128,2048]{1,0:T(8,128)(2,1)S(1)}, bf16[128,2048]{1,0:T(8,128)(2,1)S(1)}, u32[]{:S(2)}, u32[]{:S(2)}) collective-permute-start(bf16[128,2048]{1,0:T(8,128)(2,1)S(1)} %add_convert_fusion.7), channel_id=1, source_target_pairs={{0,4},{1,5},{2,6},{3,7},{4,0},{5,1},{6,2},{7,3},{8,12},{9,13},{10,... | collective-permute-start | bytes 1572872 | tf_op jit(solution)/shard_map/ppermute | solution.py:330
  202.2 35.1 %collective-permute-start.22 = (bf16[128,2048]{1,0:T(8,128)(2,1)S(1)}, bf16[128,2048]{1,0:T(8,128)(2,1)S(1)}, u32[]{:S(2)}, u32[]{:S(2)}) collective-permute-start(bf16[128,2048]{1,0:T(8,128)(2,1)S(1)} %add_convert_fusion.7), channel_id=1, source_target_pairs={{0,6},{1,7},{2,4},{3,5},{4,2},{5,3},{6,0},{7,1},{8,14},{9,15},{10,... | collective-permute-start | bytes 1572872 | tf_op jit(solution)/shard_map/ppermute | solution.py:330
  215.9 31.3 %collective-permute-start.29 = (bf16[128,2048]{1,0:T(8,128)(2,1)S(1)}, bf16[128,2048]{1,0:T(8,128)(2,1)S(1)}, u32[]{:S(2)}, u32[]{:S(2)}) collective-permute-start(bf16[128,2048]{1,0:T(8,128)(2,1)S(1)} %add_convert_fusion.6), channel_id=1, source_target_pairs={{0,2},{1,3},{2,0},{3,1},{4,6},{5,7},{6,4},{7,5},{8,10},{9,11},{10,... | collective-permute-start | bytes 1572872 | tf_op jit(solution)/shard_map/ppermute | solution.py:330
  216.6 42.0 %collective-permute-start.30 = (bf16[128,2048]{1,0:T(8,128)(2,1)S(1)}, bf16[128,2048]{1,0:T(8,128)(2,1)S(1)}, u32[]{:S(2)}, u32[]{:S(2)}) collective-permute-start(bf16[128,2048]{1,0:T(8,128)(2,1)S(1)} %add_convert_fusion.6), channel_id=1, source_target_pairs={{0,4},{1,5},{2,6},{3,7},{4,0},{5,1},{6,2},{7,3},{8,12},{9,13},{10,... | collective-permute-start | bytes 1572872 | tf_op jit(solution)/shard_map/ppermute | solution.py:330
  224.7 33.9 %collective-permute-start.31 = (bf16[128,2048]{1,0:T(8,128)(2,1)S(1)}, bf16[128,2048]{1,0:T(8,128)(2,1)S(1)}, u32[]{:S(2)}, u32[]{:S(2)}) collective-permute-start(bf16[128,2048]{1,0:T(8,128)(2,1)S(1)} %add_convert_fusion.6), channel_id=1, source_target_pairs={{0,6},{1,7},{2,4},{3,5},{4,2},{5,3},{6,0},{7,1},{8,14},{9,15},{10,... | collective-permute-start | bytes 1572872 | tf_op jit(solution)/shard_map/ppermute | solution.py:330
  237.5 29.4 %collective-permute-start.23 = (bf16[512,2048]{1,0:T(8,128)(2,1)S(1)}, bf16[512,2048]{1,0:T(8,128)(2,1)}, u32[]{:S(2)}, u32[]{:S(2)}) collective-permute-start(bf16[512,2048]{1,0:T(8,128)(2,1)S(1)} %pad_maximum_fusion.4.x_ref.refs_0_), channel_id=1, source_target_pairs={{0,1},{1,0},{2,3},{3,2},{4,5},{5,4},{6,7},{7,6},{8,9},{9,8},{10,11... | collective-permute-start | bytes 6291464 | tf_op jit(solution)/shard_map/ppermute | solution.py:330
  260.2 19.9 %collective-permute-start.33 = (bf16[512,2048]{1,0:T(8,128)(2,1)}, bf16[512,2048]{1,0:T(8,128)(2,1)}, u32[]{:S(2)}, u32[]{:S(2)}) collective-permute-start(bf16[512,2048]{1,0:T(8,128)(2,1)} %pad_maximum_fusion.5.x_ref.refs_2_), channel_id=1, source_target_pairs={{0,1},{1,0},{2,3},{3,2},{4,5},{5,4},{6,7},{7,6},{8,9},{9,8},{10,11... | collective-permute-start | bytes 6291464 | tf_op jit(solution)/shard_map/ppermute | solution.py:330
  260.2 27.3 %collective-permute-start.34 = (bf16[512,2048]{1,0:T(8,128)(2,1)}, bf16[512,2048]{1,0:T(8,128)(2,1)}, u32[]{:S(2)}, u32[]{:S(2)}) collective-permute-start(bf16[512,2048]{1,0:T(8,128)(2,1)} %constant_dynamic-update-slice_fusion.refs_4_), channel_id=1, source_target_pairs={{0,1},{1,0},{2,3},{3,2},{4,5},{5,4},{6,7},{7,6},{8,9},{9,8},{10,11... | collective-permute-start | bytes 6291464 | tf_op jit(solution)/shard_map/ppermute | solution.py:330
  260.7 26.8 %collective-permute-start.32 = (bf16[512,2048]{1,0:T(8,128)(2,1)}, bf16[512,2048]{1,0:T(8,128)(2,1)}, u32[]{:S(2)}, u32[]{:S(2)}) collective-permute-start(bf16[512,2048]{1,0:T(8,128)(2,1)} %constant_dynamic-update-slice_fusion.4.refs_6_), channel_id=1, source_target_pairs={{0,1},{1,0},{2,3},{3,2},{4,5},{5,4},{6,7},{7,6},{8,9},{9,8},{10,11... | collective-permute-start | bytes 6291464 | tf_op jit(solution)/shard_map/ppermute | solution.py:330
  327.6 286.3 %reduce-scatter.6.cloned.1.call-start = ((), (), s32[]{:S(2)}) async-start(), calls=%async_computation.7 | async-start | bytes 5242880 | tf_op jit(solution)/shard_map/reduce_scatter | solution.py:545
  330.0 14.9 %collective-permute-start.40 = (bf16[128,2048]{1,0:T(8,128)(2,1)S(1)}, bf16[128,2048]{1,0:T(8,128)(2,1)S(1)}, u32[]{:S(2)}, u32[]{:S(2)}) collective-permute-start(bf16[128,2048]{1,0:T(8,128)(2,1)S(1)} %get-tuple-element.190), channel_id=1, source_target_pairs={{0,2},{1,3},{2,0},{3,1},{4,6},{5,7},{6,4},{7,5},{8,10},{9,11},{10,... | collective-permute-start | bytes 1572872 | tf_op jit(solution)/shard_map/ppermute | solution.py:330
  330.7 25.1 %collective-permute-start.41 = (bf16[128,2048]{1,0:T(8,128)(2,1)S(1)}, bf16[128,2048]{1,0:T(8,128)(2,1)S(1)}, u32[]{:S(2)}, u32[]{:S(2)}) collective-permute-start(bf16[128,2048]{1,0:T(8,128)(2,1)S(1)} %get-tuple-element.189), channel_id=1, source_target_pairs={{0,4},{1,5},{2,6},{3,7},{4,0},{5,1},{6,2},{7,3},{8,12},{9,13},{10,... | collective-permute-start | bytes 1572872 | tf_op jit(solution)/shard_map/ppermute | solution.py:330
  332.1 23.7 %collective-permute-start.42 = (bf16[128,2048]{1,0:T(8,128)(2,1)S(1)}, bf16[128,2048]{1,0:T(8,128)(2,1)S(1)}, u32[]{:S(2)}, u32[]{:S(2)}) collective-permute-start(bf16[128,2048]{1,0:T(8,128)(2,1)S(1)} %get-tuple-element.188), channel_id=1, source_target_pairs={{0,6},{1,7},{2,4},{3,5},{4,2},{5,3},{6,0},{7,1},{8,14},{9,15},{10,... | collective-permute-start | bytes 1572872 | tf_op jit(solution)/shard_map/ppermute | solution.py:330
  360.8 16.2 %collective-permute-start.37 = (bf16[128,2048]{1,0:T(8,128)(2,1)}, bf16[128,2048]{1,0:T(8,128)(2,1)}, u32[]{:S(2)}, u32[]{:S(2)}) collective-permute-start(bf16[128,2048]{1,0:T(8,128)(2,1)} %get-tuple-element.194), channel_id=1, source_target_pairs={{0,2},{1,3},{2,0},{3,1},{4,6},{5,7},{6,4},{7,5},{8,10},{9,11},{10,... | collective-permute-start | bytes 1572872 | tf_op jit(solution)/shard_map/ppermute | solution.py:330
  361.9 24.7 %collective-permute-start.38 = (bf16[128,2048]{1,0:T(8,128)(2,1)}, bf16[128,2048]{1,0:T(8,128)(2,1)}, u32[]{:S(2)}, u32[]{:S(2)}) collective-permute-start(bf16[128,2048]{1,0:T(8,128)(2,1)} %get-tuple-element.193), channel_id=1, source_target_pairs={{0,4},{1,5},{2,6},{3,7},{4,0},{5,1},{6,2},{7,3},{8,12},{9,13},{10,... | collective-permute-start | bytes 1572872 | tf_op jit(solution)/shard_map/ppermute | solution.py:330
  362.8 23.9 %collective-permute-start.39 = (bf16[128,2048]{1,0:T(8,128)(2,1)}, bf16[128,2048]{1,0:T(8,128)(2,1)}, u32[]{:S(2)}, u32[]{:S(2)}) collective-permute-start(bf16[128,2048]{1,0:T(8,128)(2,1)} %get-tuple-element.192), channel_id=1, source_target_pairs={{0,6},{1,7},{2,4},{3,5},{4,2},{5,3},{6,0},{7,1},{8,14},{9,15},{10,... | collective-permute-start | bytes 1572872 | tf_op jit(solution)/shard_map/ppermute | solution.py:330
  393.7 50.0 %collective-permute-start.43 = (bf16[512,2048]{1,0:T(8,128)(2,1)S(1)}, bf16[512,2048]{1,0:T(8,128)(2,1)S(1)}, u32[]{:S(2)}, u32[]{:S(2)}) collective-permute-start(bf16[512,2048]{1,0:T(8,128)(2,1)S(1)} %convolution_convert_fusion.1), channel_id=1, source_target_pairs={{0,1},{1,0},{2,3},{3,2},{4,5},{5,4},{6,7},{7,6},{8,9},{9,8},{10,11... | collective-permute-start | bytes 6291464 | tf_op jit(solution)/shard_map/ppermute | solution.py:330
  393.8 14.9 %collective-permute-start.51 = (bf16[128,2048]{1,0:T(8,128)(2,1)S(1)}, bf16[128,2048]{1,0:T(8,128)(2,1)S(1)}, u32[]{:S(2)}, u32[]{:S(2)}) collective-permute-start(bf16[128,2048]{1,0:T(8,128)(2,1)S(1)} %copy-done.78), channel_id=1, source_target_pairs={{0,2},{1,3},{2,0},{3,1},{4,6},{5,7},{6,4},{7,5},{8,10},{9,11},{10,... | collective-permute-start | bytes 1572872 | tf_op jit(solution)/shard_map/ppermute | solution.py:330
  394.4 25.3 %collective-permute-start.52 = (bf16[128,2048]{1,0:T(8,128)(2,1)S(1)}, bf16[128,2048]{1,0:T(8,128)(2,1)S(1)}, u32[]{:S(2)}, u32[]{:S(2)}) collective-permute-start(bf16[128,2048]{1,0:T(8,128)(2,1)S(1)} %copy-done.78), channel_id=1, source_target_pairs={{0,4},{1,5},{2,6},{3,7},{4,0},{5,1},{6,2},{7,3},{8,12},{9,13},{10,... | collective-permute-start | bytes 1572872 | tf_op jit(solution)/shard_map/ppermute | solution.py:330
  395.6 25.5 %collective-permute-start.53 = (bf16[128,2048]{1,0:T(8,128)(2,1)S(1)}, bf16[128,2048]{1,0:T(8,128)(2,1)S(1)}, u32[]{:S(2)}, u32[]{:S(2)}) collective-permute-start(bf16[128,2048]{1,0:T(8,128)(2,1)S(1)} %copy-done.78), channel_id=1, source_target_pairs={{0,6},{1,7},{2,4},{3,5},{4,2},{5,3},{6,0},{7,1},{8,14},{9,15},{10,... | collective-permute-start | bytes 1572872 | tf_op jit(solution)/shard_map/ppermute | solution.py:330
  397.3 33.8 %collective-permute-start.55 = (bf16[128,2048]{1,0:T(8,128)(2,1)S(1)}, bf16[128,2048]{1,0:T(8,128)(2,1)S(1)}, u32[]{:S(2)}, u32[]{:S(2)}) collective-permute-start(bf16[128,2048]{1,0:T(8,128)(2,1)S(1)} %get-tuple-element.164), channel_id=1, source_target_pairs={{0,2},{1,3},{2,0},{3,1},{4,6},{5,7},{6,4},{7,5},{8,10},{9,11},{10,... | collective-permute-start | bytes 1572872 | tf_op jit(solution)/shard_map/ppermute | solution.py:330
  408.6 33.5 %collective-permute-start.56 = (bf16[128,2048]{1,0:T(8,128)(2,1)S(1)}, bf16[128,2048]{1,0:T(8,128)(2,1)S(1)}, u32[]{:S(2)}, u32[]{:S(2)}) collective-permute-start(bf16[128,2048]{1,0:T(8,128)(2,1)S(1)} %get-tuple-element.164), channel_id=1, source_target_pairs={{0,4},{1,5},{2,6},{3,7},{4,0},{5,1},{6,2},{7,3},{8,12},{9,13},{10,... | collective-permute-start | bytes 1572872 | tf_op jit(solution)/shard_map/ppermute | solution.py:330
  419.8 22.4 %collective-permute-start.57 = (bf16[128,2048]{1,0:T(8,128)(2,1)S(1)}, bf16[128,2048]{1,0:T(8,128)(2,1)S(1)}, u32[]{:S(2)}, u32[]{:S(2)}) collective-permute-start(bf16[128,2048]{1,0:T(8,128)(2,1)S(1)} %get-tuple-element.164), channel_id=1, source_target_pairs={{0,6},{1,7},{2,4},{3,5},{4,2},{5,3},{6,0},{7,1},{8,14},{9,15},{10,... | collective-permute-start | bytes 1572872 | tf_op jit(solution)/shard_map/ppermute | solution.py:330
  421.4 33.1 %collective-permute-start.54 = (bf16[512,2048]{1,0:T(8,128)(2,1)S(1)}, bf16[512,2048]{1,0:T(8,128)(2,1)}, u32[]{:S(2)}, u32[]{:S(2)}) collective-permute-start(bf16[512,2048]{1,0:T(8,128)(2,1)S(1)} %pad_maximum_fusion.6.refs_2_), channel_id=1, source_target_pairs={{0,1},{1,0},{2,3},{3,2},{4,5},{5,4},{6,7},{7,6},{8,9},{9,8},{10,11... | collective-permute-start | bytes 6291464 | tf_op jit(solution)/shard_map/ppermute | solution.py:330
  451.6 207.4 %reduce-scatter.4.cloned.1.call-start = ((), (), s32[]{:S(2)}) async-start(), calls=%async_computation.6 | async-start | bytes 5242880 | tf_op jit(solution)/shard_map/reduce_scatter | solution.py:599
  517.4 20.0 %collective-permute-start.59 = (bf16[512,2048]{1,0:T(8,128)(2,1)}, bf16[512,2048]{1,0:T(8,128)(2,1)}, u32[]{:S(2)}, u32[]{:S(2)}) collective-permute-start(bf16[512,2048]{1,0:T(8,128)(2,1)} %bitcast_convert_fusion.1), channel_id=1, source_target_pairs={{0,1},{1,0},{2,3},{3,2},{4,5},{5,4},{6,7},{7,6},{8,9},{9,8},{10,11... | collective-permute-start | bytes 6291464 | tf_op jit(solution)/shard_map/ppermute | solution.py:330
  533.9 15.2 %collective-permute-start.44 = (bf16[128,2048]{1,0:T(8,128)(2,1)}, bf16[128,2048]{1,0:T(8,128)(2,1)}, u32[]{:S(2)}, u32[]{:S(2)}) collective-permute-start(bf16[128,2048]{1,0:T(8,128)(2,1)} %get-tuple-element.182), channel_id=1, source_target_pairs={{0,2},{1,3},{2,0},{3,1},{4,6},{5,7},{6,4},{7,5},{8,10},{9,11},{10,... | collective-permute-start | bytes 1572872 | tf_op jit(solution)/shard_map/ppermute | solution.py:330
  535.3 26.0 %collective-permute-start.45 = (bf16[128,2048]{1,0:T(8,128)(2,1)}, bf16[128,2048]{1,0:T(8,128)(2,1)}, u32[]{:S(2)}, u32[]{:S(2)}) collective-permute-start(bf16[128,2048]{1,0:T(8,128)(2,1)} %get-tuple-element.184), channel_id=1, source_target_pairs={{0,4},{1,5},{2,6},{3,7},{4,0},{5,1},{6,2},{7,3},{8,12},{9,13},{10,... | collective-permute-start | bytes 1572872 | tf_op jit(solution)/shard_map/ppermute | solution.py:330
  535.9 25.5 %collective-permute-start.46 = (bf16[128,2048]{1,0:T(8,128)(2,1)}, bf16[128,2048]{1,0:T(8,128)(2,1)}, u32[]{:S(2)}, u32[]{:S(2)}) collective-permute-start(bf16[128,2048]{1,0:T(8,128)(2,1)} %get-tuple-element.183), channel_id=1, source_target_pairs={{0,6},{1,7},{2,4},{3,5},{4,2},{5,3},{6,0},{7,1},{8,14},{9,15},{10,... | collective-permute-start | bytes 1572872 | tf_op jit(solution)/shard_map/ppermute | solution.py:330
  546.4 48.6 %collective-permute-start.63 = (bf16[512,2048]{1,0:T(8,128)(2,1)}, bf16[512,2048]{1,0:T(8,128)(2,1)}, u32[]{:S(2)}, u32[]{:S(2)}) collective-permute-start(bf16[512,2048]{1,0:T(8,128)(2,1)} %bitcast_convert_fusion), channel_id=1, source_target_pairs={{0,1},{1,0},{2,3},{3,2},{4,5},{5,4},{6,7},{7,6},{8,9},{9,8},{10,11... | collective-permute-start | bytes 6291464 | tf_op jit(solution)/shard_map/ppermute | solution.py:330
  547.6 23.9 %collective-permute-start.48 = (bf16[128,2048]{1,0:T(8,128)(2,1)}, bf16[128,2048]{1,0:T(8,128)(2,1)}, u32[]{:S(2)}, u32[]{:S(2)}) collective-permute-start(bf16[128,2048]{1,0:T(8,128)(2,1)} %get-tuple-element.185), channel_id=1, source_target_pairs={{0,2},{1,3},{2,0},{3,1},{4,6},{5,7},{6,4},{7,5},{8,10},{9,11},{10,... | collective-permute-start | bytes 1572872 | tf_op jit(solution)/shard_map/ppermute | solution.py:330
  549.1 34.2 %collective-permute-start.49 = (bf16[128,2048]{1,0:T(8,128)(2,1)}, bf16[128,2048]{1,0:T(8,128)(2,1)}, u32[]{:S(2)}, u32[]{:S(2)}) collective-permute-start(bf16[128,2048]{1,0:T(8,128)(2,1)} %get-tuple-element.187), channel_id=1, source_target_pairs={{0,4},{1,5},{2,6},{3,7},{4,0},{5,1},{6,2},{7,3},{8,12},{9,13},{10,... | collective-permute-start | bytes 1572872 | tf_op jit(solution)/shard_map/ppermute | solution.py:330
  561.3 22.0 %collective-permute-start.50 = (bf16[128,2048]{1,0:T(8,128)(2,1)}, bf16[128,2048]{1,0:T(8,128)(2,1)}, u32[]{:S(2)}, u32[]{:S(2)}) collective-permute-start(bf16[128,2048]{1,0:T(8,128)(2,1)} %get-tuple-element.186), channel_id=1, source_target_pairs={{0,6},{1,7},{2,4},{3,5},{4,2},{5,3},{6,0},{7,1},{8,14},{9,15},{10,... | collective-permute-start | bytes 1572872 | tf_op jit(solution)/shard_map/ppermute | solution.py:330
  591.6 14.8 %collective-permute-start.60 = (bf16[128,2048]{1,0:T(8,128)(2,1)S(1)}, bf16[128,2048]{1,0:T(8,128)(2,1)S(1)}, u32[]{:S(2)}, u32[]{:S(2)}) collective-permute-start(bf16[128,2048]{1,0:T(8,128)(2,1)S(1)} %get-tuple-element.179), channel_id=1, source_target_pairs={{0,2},{1,3},{2,0},{3,1},{4,6},{5,7},{6,4},{7,5},{8,10},{9,11},{10,... | collective-permute-start | bytes 1572872 | tf_op jit(solution)/shard_map/ppermute | solution.py:330
  592.2 26.3 %collective-permute-start.61 = (bf16[128,2048]{1,0:T(8,128)(2,1)}, bf16[128,2048]{1,0:T(8,128)(2,1)}, u32[]{:S(2)}, u32[]{:S(2)}) collective-permute-start(bf16[128,2048]{1,0:T(8,128)(2,1)} %get-tuple-element.181), channel_id=1, source_target_pairs={{0,4},{1,5},{2,6},{3,7},{4,0},{5,1},{6,2},{7,3},{8,12},{9,13},{10,... | collective-permute-start | bytes 1572872 | tf_op jit(solution)/shard_map/ppermute | solution.py:330
  593.4 25.1 %collective-permute-start.62 = (bf16[128,2048]{1,0:T(8,128)(2,1)}, bf16[128,2048]{1,0:T(8,128)(2,1)}, u32[]{:S(2)}, u32[]{:S(2)}) collective-permute-start(bf16[128,2048]{1,0:T(8,128)(2,1)} %get-tuple-element.180), channel_id=1, source_target_pairs={{0,6},{1,7},{2,4},{3,5},{4,2},{5,3},{6,0},{7,1},{8,14},{9,15},{10,... | collective-permute-start | bytes 1572872 | tf_op jit(solution)/shard_map/ppermute | solution.py:330
  599.6 29.3 %collective-permute-start.64 = (bf16[128,2048]{1,0:T(8,128)(2,1)}, bf16[128,2048]{1,0:T(8,128)(2,1)}, u32[]{:S(2)}, u32[]{:S(2)}) collective-permute-start(bf16[128,2048]{1,0:T(8,128)(2,1)} %get-tuple-element.176), channel_id=1, source_target_pairs={{0,2},{1,3},{2,0},{3,1},{4,6},{5,7},{6,4},{7,5},{8,10},{9,11},{10,... | collective-permute-start | bytes 1572872 | tf_op jit(solution)/shard_map/ppermute | solution.py:330
  600.3 38.9 %collective-permute-start.65 = (bf16[128,2048]{1,0:T(8,128)(2,1)}, bf16[128,2048]{1,0:T(8,128)(2,1)}, u32[]{:S(2)}, u32[]{:S(2)}) collective-permute-start(bf16[128,2048]{1,0:T(8,128)(2,1)} %get-tuple-element.178), channel_id=1, source_target_pairs={{0,4},{1,5},{2,6},{3,7},{4,0},{5,1},{6,2},{7,3},{8,12},{9,13},{10,... | collective-permute-start | bytes 1572872 | tf_op jit(solution)/shard_map/ppermute | solution.py:330
  606.4 32.9 %collective-permute-start.66 = (bf16[128,2048]{1,0:T(8,128)(2,1)S(1)}, bf16[128,2048]{1,0:T(8,128)(2,1)}, u32[]{:S(2)}, u32[]{:S(2)}) collective-permute-start(bf16[128,2048]{1,0:T(8,128)(2,1)S(1)} %get-tuple-element.177), channel_id=1, source_target_pairs={{0,6},{1,7},{2,4},{3,5},{4,2},{5,3},{6,0},{7,1},{8,14},{9,15},{10,... | collective-permute-start | bytes 1572872 | tf_op jit(solution)/shard_map/ppermute | solution.py:330
  (130 other events, 1089.8 us)
Sparse Core Ops, SparseCore 0:
  18.3 79.0 all-gather.3
  144.2 77.5 all-gather.5
  223.4 79.2 all-gather.7
  327.7 74.4 reduce-scatter.7
  451.7 74.2 reduce-scatter.5
  537.5 74.2 reduce-scatter.3

commit v3 on v2

--- a/solution.py
+++ b/solution.py
@@ -19,6 +19,8 @@
 NN = (((1,), (0,)), ((), ()))
 TN = (((0,), (0,)), ((), ()))
 PARAMS = pltpu.CompilerParams(vmem_limit_bytes=48 << 20)
+SMALL = pltpu.CompilerParams(vmem_limit_bytes=24 << 20)
+TINY = pl.CostEstimate(flops=1000, bytes_accessed=1000, transcendentals=0)
 
 
 def normalize(values):
@@ -188,11 +190,7 @@
             out_specs=(wide, wide, wide, wide, stat),
         ),
         compiler_params=PARAMS,
-        cost_estimate=pl.CostEstimate(
-            flops=16 * rows * seq_len * lanes,
-            bytes_accessed=rows * lanes * 24,
-            transcendentals=rows * seq_len * lanes // HEAD,
-        ),
+        cost_estimate=TINY,
         name="attend_forward",
     )(spots, proj, proj, proj, *tables, seg_cols, seg_rows)
 
@@ -213,11 +211,7 @@
             + [pltpu.VMEM((seq_len, width), F32)] * 3,
         ),
         compiler_params=PARAMS,
-        cost_estimate=pl.CostEstimate(
-            flops=24 * rows * seq_len * lanes,
-            bytes_accessed=rows * lanes * 24,
-            transcendentals=rows * seq_len * lanes // HEAD,
-        ),
+        cost_estimate=TINY,
         name="attend_backward",
     )(spots, q, k, v, grad, lse, *tables, seg_cols, seg_rows)
 
@@ -246,13 +240,158 @@
         ],
         out_specs=(out, out),
         compiler_params=PARAMS,
-        cost_estimate=pl.CostEstimate(
-            flops=2 * rows * depth * units,
-            bytes_accessed=2 * (rows * depth + depth * units) + 4 * rows * units,
-            transcendentals=2 * rows * units,
-        ),
+        cost_estimate=TINY,
         name="expand",
     )(rows_in, weight)
+
+
+def product_kernel(*refs, make, in_count, added, summed):
+    acc = make(*refs[:in_count])
+    if summed:
+        terms = acc * refs[in_count + added][...].astype(F32)
+        refs[-1][...] = jnp.sum(terms, axis=0, keepdims=True)
+        refs = refs[: in_count + added] + refs[in_count + added + 1 : -1]
+    if added:
+        acc = acc + refs[in_count][...].astype(F32)
+    outs = refs[in_count + added :]
+    size = acc.shape[0] // len(outs)
+    for i, out_ref in enumerate(outs):
+        out_ref[...] = acc[i * size : (i + 1) * size].astype(out_ref.dtype)
+
+
+def product(name, make, operands, rows, width, got=None, pieces=1, tile=512, against=None):
+    strip, tile = min(512, rows), min(tile, width)
+    arrays, specs = zip(*[(v, pl.BlockSpec(block, index)) for v, block, index in operands])
+    here = lambda i, j: (i, j)
+    extra = tuple(v for v in (got, against) if v is not None)
+    arrays, specs = arrays + extra, specs + (pl.BlockSpec((strip, tile), here),) * len(extra)
+    shapes = [jax.ShapeDtypeStruct((rows // pieces, width), B16)] * pieces
+    out_specs = [pl.BlockSpec((strip // pieces, tile), here)] * pieces
+    if against is not None:
+        shapes.append(jax.ShapeDtypeStruct((rows // strip, 1, width), F32))
+        out_specs.append(pl.BlockSpec((None, 1, tile), lambda i, j: (i, 0, j)))
+    out = pl.pallas_call(
+        functools.partial(
+            product_kernel,
+            make=make,
+            in_count=len(operands),
+            added=got is not None,
+            summed=against is not None,
+        ),
+        out_shape=shapes,
+        grid=(rows // strip, width // tile),
+        in_specs=list(specs),
+        out_specs=out_specs,
+        compiler_params=SMALL,
+        cost_estimate=TINY,
+        name=name,
+    )(*arrays)
+    return list(out)
+
+
+def times_out(x_ref, w_ref):
+    step = x_ref.shape[1]
+    return side_by_side(
+        [
+            jnp.dot(x_ref[...], w_ref[lo : lo + step], preferred_element_type=F32)
+            for lo in range(0, w_ref.shape[0], step)
+        ]
+    )
+
+
+def times_plain(x_ref, w_ref):
+    return jnp.dot(x_ref[...], w_ref[...], preferred_element_type=F32)
+
+
+def times_turned(x_ref, w_ref):
+    return lax.dot_general(x_ref[...], w_ref[...], NT, preferred_element_type=F32)
+
+
+def times_planes(x_ref, w_ref):
+    return sum(
+        lax.dot_general(x_ref[n], w_ref[n], NT, preferred_element_type=F32)
+        for n in range(x_ref.shape[0])
+    )
+
+
+def scaled_kernel(x_ref, w_ref, slope_ref, out_ref):
+    acc = lax.dot_general(x_ref[...], w_ref[...], NT, preferred_element_type=F32)
+    out_ref[...] = (slope_ref[...].astype(F32) * acc).astype(B16)
+
+
+def scaled_product(rows_in, weight, slope):
+    rows, depth = rows_in.shape
+    units = weight.shape[0]
+    tile, strip = min(256, units), min(512, rows)
+    here = pl.BlockSpec((strip, tile), lambda i, j: (i, j))
+    return pl.pallas_call(
+        scaled_kernel,
+        out_shape=jax.ShapeDtypeStruct((rows, units), B16),
+        grid=(rows // strip, units // tile),
+        in_specs=[
+            pl.BlockSpec((strip, depth), lambda i, j: (i, 0)),
+            pl.BlockSpec((tile, depth), lambda i, j: (j, 0)),
+            here,
+        ],
+        out_specs=here,
+        compiler_params=SMALL,
+        cost_estimate=TINY,
+        name="scaled_product",
+    )(rows_in, weight, slope)
+
+
+def project_kernel(*refs):
+    w_ref, out_ref = refs[-2:]
+    for n, x_ref in enumerate(refs[:-2]):
+        out_ref[n] = jnp.dot(x_ref[...], w_ref[...], preferred_element_type=F32)
+
+
+def project(parts, four):
+    rows, depth = parts[0].shape
+    lanes = four.shape[2]
+    strip = min(512, rows)
+    out = pl.pallas_call(
+        project_kernel,
+        out_shape=jax.ShapeDtypeStruct((3, len(parts), rows, lanes), F32),
+        grid=(rows // strip, 3),
+        in_specs=[pl.BlockSpec((strip, depth), lambda i, j: (i, 0)) for _ in parts]
+        + [pl.BlockSpec((None, depth, lanes), lambda i, j: (j, 0, 0))],
+        out_specs=pl.BlockSpec((None, len(parts), strip, lanes), lambda i, j: (j, 0, i, 0)),
+        compiler_params=SMALL,
+        cost_estimate=TINY,
+        name="project",
+    )(*parts, four)
+    return out.reshape(3, len(parts) * rows, lanes)
+
+
+def unmix_kernel(*refs):
+    w_ref, out_ref = refs[-2:]
+    step = w_ref.shape[1]
+    for n, x_ref in enumerate(refs[:-2]):
+        acc = None
+        for lo in range(0, w_ref.shape[0], step):
+            cols = slice(lo, lo + step)
+            term = lax.dot_general(x_ref[:, cols], w_ref[cols], NT, preferred_element_type=F32)
+            acc = term if acc is None else acc + term
+        out_ref[n] = acc.astype(B16)
+
+
+def unmix(parts, four):
+    rows, depth = parts[0].shape
+    lanes = four.shape[2]
+    strip = min(512, rows)
+    out = pl.pallas_call(
+        unmix_kernel,
+        out_shape=jax.ShapeDtypeStruct((len(parts), rows, lanes), B16),
+        grid=(rows // strip,),
+        in_specs=[pl.BlockSpec((strip, depth), lambda i: (i, 0)) for _ in parts]
+        + [pl.BlockSpec((None, depth, lanes), lambda i: (3, 0, 0))],
+        out_specs=pl.BlockSpec((len(parts), strip, lanes), lambda i: (0, i, 0)),
+        compiler_params=SMALL,
+        cost_estimate=TINY,
+        name="unmix",
+    )(*parts, four)
+    return out.reshape(len(parts) * rows, lanes)
 
 
 def row_chunks(refs, size):
@@ -316,11 +455,7 @@
         out_specs=pl.BlockSpec(out_block, out_index),
         input_output_aliases={len(xs) + len(ys): 0} if bases else {},
         compiler_params=PARAMS,
-        cost_estimate=pl.CostEstimate(
-            flops=2 * x_rows * depth * width * max(1, planes),
-            bytes_accessed=2 * (x_rows * (depth + width) + depth * width),
-            transcendentals=0,
-        ),
+        cost_estimate=TINY,
         name="weight_grad",
     )(*xs, *ys, *bases)
 
@@ -330,29 +465,48 @@
     return lax.ppermute(values, "col", [(i, i ^ bits) for i in range(count)])
 
 
-def spread(values, direct):
+def send_out(values, direct):
     if not direct:
         return [lax.all_gather(values, "col", axis=0, tiled=True)]
     chips = lax.axis_size("col") // 2
-    near = jnp.concatenate([values] + [flip(values, 2 * c) for c in range(1, chips)], axis=0)
-    return [near, flip(near, 1)]
-
-
-def near_sum(make, direct):
+    return [values] + [flip(values, 2 * c) for c in range(1, chips)]
+
+
+def join(pieces, direct):
+    near = jnp.concatenate(pieces, axis=0)
+    return [near, flip(near, 1)] if direct else [near]
+
+
+def spread(values, direct):
+    return join(send_out(values, direct), direct)
+
+
+def near_sum(make, direct, gate=(), later=()):
     if not direct:
-        return make(0).astype(B16)
-    got = flip(make(1).astype(B16), 1)
-    return (make(0) + got.astype(F32)).astype(B16)
+        return make(0, None, 1)
+    got = flip(after(make(1, None, 1)[0], gate), 1)
+    return make(0, after(got, later), lax.axis_size("col") // 2)
 
 
 def send_sum(near, direct):
     if not direct:
-        return [lax.psum_scatter(near, "col", scatter_dimension=0, tiled=True)]
-    chips = lax.axis_size("col") // 2
-    size = near.shape[0] // chips
-    return [near[:size]] + [
-        flip(near[c * size : (c + 1) * size], 2 * c) for c in range(1, chips)
-    ]
+        return [lax.psum_scatter(near[0], "col", scatter_dimension=0, tiled=True)]
+    return near[:1] + [flip(v, 2 * c) for c, v in enumerate(near) if c > 0]
+
+
+def send_both(near, values, direct):
+    if not direct:
+        return send_sum(near, direct) + send_out(values, direct)
+    pairs = [jnp.concatenate([v, w], axis=0) for v, w in zip(near, values)]
+    return pairs[:1] + [flip(v, 2 * c) for c, v in enumerate(pairs) if c > 0]
+
+
+def first_half(pairs, direct):
+    return [v[: v.shape[0] // 2] for v in pairs] if direct else pairs[:1]
+
+
+def last_half(pairs, direct):
+    return [v[v.shape[0] // 2 :] for v in pairs] if direct else pairs[1:]
 
 
 def add_up(parts):
@@ -417,10 +571,6 @@
     four_full = lax.all_gather(
         jnp.concatenate([w_qkv, w_out[None]], axis=0), "row", axis=1, tiled=True
     )
-    qkv_full = four_full[:3]
-    out_full = jnp.moveaxis(four_full[3].reshape(-1, lanes, lanes), 0, 1).reshape(
-        lanes, model_width
-    )
     up_full = lax.all_gather(w_up, "row", axis=0, tiled=True)
     down_full = lax.all_gather(w_down, "row", axis=1, tiled=True)
 
@@ -433,55 +583,65 @@
     normed1 = [(s * ln_gain[0] + ln_bias[0]).astype(B16) for s, _ in first]
     grad_y = [cotangent[m].astype(F32) for m in micros]
     grad_block = [dwa_weights[prior_count] * g for g in grad_y]
-    rows_one, grad_rows, last = [], [], None
-    for values, found in ((normed1, rows_one), (grad_block, grad_rows)):
-        for v in values:
-            v = v.astype(B16)
-            found.append(spread(v if last is None or found is rows_one else after(v, last), direct))
-            last = found[-1][0]
-    parts = range(len(rows_one[0]))
-    part_rows = group_rows // len(parts)
-
-    def part_of(values, n):
-        return values[n * part_rows : (n + 1) * part_rows]
-
-    saved, attended, mixed, mixed_parts = [], [], [], []
+    one_pieces, branch_pieces, last = [], [], []
     for m in micros:
-        rows_m = after(rows_one[m], grad_rows[0][0], mixed[-1:])
-        proj = jnp.concatenate(
-            [
-                jnp.einsum("sd,jdh->jsh", v, qkv_full, preferred_element_type=F32)
-                for v in rows_m
-            ],
-            axis=1,
-        )
+        branch_pieces.append(send_out(after(grad_block[m].astype(B16), last), direct))
+        one_pieces.append(send_out(after(normed1[m], branch_pieces[m]), direct))
+        last = one_pieces[m]
+    grad_rows = [join(v, direct) for v in branch_pieces]
+    rows_one = [join(after(one_pieces[0], branch_pieces[-1]), direct)]
+    rows_one += [join(v, direct) for v in one_pieces[1:]]
+    part_rows = group_rows // (2 if direct else 1)
+    strip, d_tile = min(512, part_rows), min(512, model_width)
+    strips = part_rows // strip
+
+    saved, attended, resid, second, rows_two = [], [], [], [], []
+    mixed, mixed_parts, two_pieces = [], [], []
+
+    def norm_two(m, gate):
+        resid.append(resid_in[m] + add_up(after(mixed_parts[m], gate)))
+        second.append(normalize(resid[m]))
+        normed2 = (second[m][0] * ln_gain[1] + ln_bias[1]).astype(B16)
+        two_pieces.append(send_out(normed2, direct))
+        return normed2
+
+    last = []
+    for m in micros:
+        proj = project(rows_one[m], after(four_full, mixed[-1]) if m else four_full)
         q, k, v, att, lse = attention(
             spots, proj, tables[m], seg_cols[m], seg_rows[m], seq_len, tok_dev
         )
         saved.append((q, k, v, lse))
         attended.append(att)
-        att_m = after(att, mixed_parts[-1] if mixed_parts else grad_rows[-1][0])
+        if m > 0:
+            last = norm_two(m - 1, att)
+        att_m = after(att, last)
         mixed.append(
             near_sum(
-                lambda n: jnp.dot(part_of(att_m, n), out_full, preferred_element_type=F32), direct
+                lambda n, got, pieces: product(
+                    "mix",
+                    times_out,
+                    [
+                        (att_m, (strip, lanes), lambda i, j: (i + n * strips, 0)),
+                        (four_full, (None, d_tile, lanes), lambda i, j: (3, j, 0)),
+                    ],
+                    part_rows,
+                    model_width,
+                    got,
+                    pieces,
+                ),
+                direct,
             )
         )
         mixed_parts.append(send_sum(mixed[-1], direct))
-
-    resid, second, rows_two = [], [], []
-    last = []
-    for m in micros:
-        resid.append(resid_in[m] + add_up(after(mixed_parts[m], last)))
-        second.append(normalize(resid[m]))
-        normed2 = (second[m][0] * ln_gain[1] + ln_bias[1]).astype(B16)
-        rows_two.append(spread(normed2, direct))
-        last = normed2
+    norm_two(micro_count - 1, (two_pieces[-1], up_full))
 
     flat = lambda lists: [v for parts_of in lists for v in parts_of]
     total_rows = micro_count * group_rows
     fit = max(128, (8 << 20) // (2 * total_rows))
-    hidden, slopes = [], []
+    hidden, slopes, rows_two = [], [], []
     for m in micros:
+        rows_two.append(join(after(two_pieces[m], hidden), direct))
         pairs = [expand(v, up_full) for v in rows_two[m]]
         hidden.append([a for a, _ in pairs])
         slopes.append([a for _, a in pairs])
@@ -499,77 +659,117 @@
         splits=splits,
     )
     down_full = after(down_full, grad_down)
-    grad_down = lax.psum_scatter(grad_down, "row", scatter_dimension=0)
-
-    grad_pre, back_two = [], []
+    grad_down = lax.psum_scatter(grad_down, "row", scatter_dimension=0, tiled=True)
+
+    grad_pre, back_two, back_parts = [], [], []
     for m in micros:
-        rows_m = after(grad_rows[m], back_two[-1]) if back_two else grad_rows[m]
+        slopes_m = after(slopes[m], back_two[-1:])
         grad_pre.append(
-            [
-                (
-                    slope.astype(F32)
-                    * jnp.einsum("sd,fd->sf", g, down_full, preferred_element_type=F32)
-                ).astype(B16)
-                for slope, g in zip(slopes[m], rows_m)
-            ]
+            [scaled_product(g, down_full, slope) for slope, g in zip(slopes_m, grad_rows[m])]
         )
         back_two.append(
             near_sum(
-                lambda n: jnp.einsum(
-                    "sf,df->sd", grad_pre[m][n], up_full, preferred_element_type=F32
+                lambda n, got, pieces: product(
+                    "unexpand",
+                    times_turned,
+                    [
+                        (grad_pre[m][n], (strip, units), lambda i, j: (i, 0)),
+                        (up_full, (d_tile, units), lambda i, j: (j, 0)),
+                    ],
+                    part_rows,
+                    model_width,
+                    got,
+                    pieces,
                 ),
                 direct,
+                back_parts,
             )
         )
-
-    back_parts = [send_sum(v, direct) for v in back_two]
-    grad_normed2, grad_resid, grad_mixed_rows = [], [], []
-    last = back_two[-1]
+        if m == 0:
+            back_parts.append(send_sum(back_two[m], direct))
+    grad_normed2, grad_resid, mixed_pieces, branch = [], [], [], []
+
+    shares = []
+
+    def branch_half(m, n, ready, got=None, pieces=1):
+        *outs, share = product(
+            "contract",
+            times_plain,
+            [
+                (after(hidden[m][n], ready), (strip, units), lambda i, j: (i, 0)),
+                (down_full, (units, d_tile), lambda i, j: (0, j)),
+            ],
+            part_rows,
+            model_width,
+            got,
+            pieces,
+            against=grad_rows[m][n],
+        )
+        shares.append(jnp.sum(share))
+        return outs
+
     x_tile, y_tile = min(256, model_width), min(units, fit)
+    def norm_two_back(m, parts):
+        grad_normed2.append(add_up(parts))
+        grad_resid.append(grad_block[m] + norm_back(grad_normed2[m], *second[m], ln_gain[1]))
+        return grad_resid[m].astype(B16)
+
+    chips = col_count // 2 if direct else 1
+    grad_mixed = norm_two_back(0, back_parts[0])
+    pairs = send_both(back_two[1], [grad_mixed] * chips if direct else grad_mixed, direct)
+    grad_up = weight_grad(
+        flat(rows_two),
+        after(flat(grad_pre), (grad_mixed, back_two[1])),
+        (model_width, units),
+        (x_tile, y_tile),
+        lambda i, j: (i, j),
+        x_tile,
+        y_tile,
+    )
+    others = [branch_half(m, 1, grad_up)[0] for m in micros] if direct else [None] * micro_count
+    pairs = after(pairs, (grad_up, others if direct else ()))
+    grad_up = lax.psum_scatter(grad_up, "row", scatter_dimension=0, tiled=True)
+    mixed_pieces.append(last_half(pairs, direct))
+    mixed_pieces.append(send_out(norm_two_back(1, first_half(pairs, direct)), direct))
+    if direct:
+        others = [flip(v, 1) for v in after(others, pairs)]
+
+    grad_planes, grad_mixed_rows = [], []
     for m in micros:
-        grad_normed2.append(add_up(after(back_parts[m], last)))
-        grad_resid.append(grad_block[m] + norm_back(grad_normed2[m], *second[m], ln_gain[1]))
-        grad_mixed = grad_resid[m].astype(B16)
-        grad_mixed_rows.append(spread(grad_mixed, direct))
-        if m == 0:
-            grad_up = weight_grad(
-                flat(rows_two),
-                after(flat(grad_pre), grad_mixed),
-                (model_width, units),
-                (x_tile, y_tile),
-                lambda i, j: (i, j),
-                x_tile,
-                y_tile,
-            )
-            last = grad_up
-    grad_up = lax.psum_scatter(grad_up, "row", scatter_dimension=0, tiled=True)
-
-    branch = []
-    for m in micros:
-        hidden_m = after(hidden[m], branch[-1] if branch else grad_mixed)
-        branch.append(
-            near_sum(
-                lambda n: jnp.dot(hidden_m[n], down_full, preferred_element_type=F32), direct
-            )
-        )
-
-    grad_planes = []
-    last = branch[-1]
-    for m in micros:
-        rows_m = after(grad_mixed_rows[m], last)
-        grad_att = jnp.concatenate(
-            [
-                jnp.einsum("sd,hd->sh", v, out_full, preferred_element_type=F32).astype(B16)
-                for v in rows_m
-            ],
-            axis=0,
-        )
+        ready = ()
+        if m == 1:
+            branch = [branch_half(n, 0, grad_planes[0], others[n], chips) for n in micros]
+            if direct:
+                branch_pairs = send_both(*branch, direct)
+            else:
+                branch_pairs = [v for near in branch for v in send_sum(near, direct)]
+            ready = (branch, grad_planes[0], grad_down)
+        grad_mixed_rows.append(join(after(mixed_pieces[m], ready), direct))
+        grad_att = unmix(grad_mixed_rows[m], four_full)
         grad_planes.append(
             attention_back(
                 spots, saved[m], grad_att, tables[m], seg_cols[m], seg_rows[m], seq_len, tok_dev
             )
         )
-        last = grad_planes[-1]
+
+    def back_sum(planes_m, gate, later):
+        return near_sum(
+            lambda n, got, pieces: product(
+                "unproject",
+                times_planes,
+                [
+                    (planes_m, (3, strip, lanes), lambda i, j: (0, i + n * strips, 0)),
+                    (four_full, (3, d_tile, lanes), lambda i, j: (0, j, 0)),
+                ],
+                part_rows,
+                model_width,
+                got,
+                pieces,
+            ),
+            direct,
+            gate,
+            later,
+        )
 
     four_shape = (row_count, 4, part_width, lanes)
     grad_four = weight_grad(
@@ -593,33 +793,21 @@
         x_tile,
         lanes,
         planes=3,
-        base=grad_four,
+        base=after(grad_four, grad_up),
     )
     last = grad_four
     grad_four = lax.psum_scatter(grad_four, "row", scatter_dimension=0)
 
-    in_grads, grad_normed1, back_one = [], [], []
-    for m in micros:
-        planes_m = after(grad_planes[m], last)
-        back_one.append(
-            near_sum(
-                lambda n: jnp.einsum(
-                    "jsh,jdh->sd",
-                    planes_m[:, n * part_rows : (n + 1) * part_rows],
-                    qkv_full,
-                    preferred_element_type=F32,
-                ),
-                direct,
-            )
-        )
-        last = back_one[-1]
-    for m in micros:
-        grad_normed1.append(add_up(send_sum(back_one[m], direct)))
-        in_grads.append(grad_resid[m] + norm_back(grad_normed1[m], *first[m], ln_gain[0]))
+    back_one = [back_sum(after(v, (last, branch_pairs)), (), ()) for v in grad_planes]
+    one_parts = [send_sum(v, direct) for v in back_one]
+    branch_pairs, cotangent, earlier_outs, grad_down, grad_up = after(
+        (branch_pairs, cotangent, earlier_outs, grad_down, grad_up), back_one[-1]
+    )
+    branch_parts = [first_half(branch_pairs, direct), last_half(branch_pairs, direct)]
 
     outputs, mix_grads = [], []
     for m in micros:
-        block_out = resid[m] + add_up(send_sum(branch[m], direct))
+        block_out = resid[m] + add_up(branch_parts[m])
         earlier = earlier_outs[:, m].astype(F32)
         mix_sum = dwa_weights[0] * earlier[0]
         for level in range(1, prior_count):
@@ -629,10 +817,18 @@
             jnp.concatenate(
                 [
                     jnp.sum(grad_y[m][None] * earlier, axis=(1, 2)),
-                    jnp.sum(grad_y[m] * block_out)[None],
+                    jnp.sum(grad_y[m] * resid[m])[None],
                 ]
             )
         )
+
+    grad_earlier = (
+        dwa_weights[:prior_count, None, None, None] * cotangent.astype(F32)[None]
+    )
+    in_grads, grad_normed1 = [], []
+    for m in micros:
+        grad_normed1.append(add_up(after(one_parts[m], grad_earlier if m else ())))
+        in_grads.append(grad_resid[m] + norm_back(grad_normed1[m], *first[m], ln_gain[0]))
 
     stats = jnp.stack(
         [
@@ -642,7 +838,8 @@
             sum(jnp.sum(grad_normed2[m], axis=0) for m in micros),
         ]
     )
-    mix_row = jnp.pad(sum(mix_grads), (0, part_width - prior_count - 1))
+    mix_sum = sum(mix_grads).at[prior_count].add(sum(shares) / dwa_weights[prior_count])
+    mix_row = jnp.pad(mix_sum, (0, part_width - prior_count - 1))
     slabs = jnp.concatenate(
         [
             jnp.moveaxis(stats.reshape(4, row_count, part_width), 1, 0),
@@ -659,9 +856,6 @@
         slab = slab + flip(slab, bits)
         bits *= 2
 
-    grad_earlier = (
-        dwa_weights[:prior_count, None, None, None] * cotangent.astype(F32)[None]
-    )
     return (
         jnp.stack(outputs),
         jnp.stack(in_grads),
@@ -671,7 +865,7 @@
         .reshape(lanes, part_width)
         .astype(F32),
         grad_up.astype(F32),
-        grad_down.astype(F32),
+        grad_down[0].astype(F32),
         slab[:2],
         slab[2:4],
         slab[4, : prior_count + 1],

time: 674 us -> 618 us (0.917)
  matrix products: 94.4 us -> 0 us
  Pallas kernels: 115 us -> 203 us
  waiting for transfers between devices: 247 us -> 193 us
  local copies, waits for them, and re-layouts: 43.6 us -> 67.3 us
  other arithmetic: 79.1 us -> 60.5 us
  starting transfers between devices: 74.1 us -> 66.7 us
    dot_general x28 -> x0, matrix products: 94.4 us -> none  [the longest x4 17.8 us: body(): jnp.einsum('sd,fd->sf', g, down_full, preferred_element_type=F32)]
    pallas_call x0 -> x24, Pallas kernels: none -> 90 us  [the longest x16 60.9 us: product(): pl.pallas_call(functools.partial(product_kernel, make=make, in_count=len(...]
    ppermute x67 -> x61, waiting for transfers between devices: 245 us -> 189 us  [flip(): return lax.ppermute(values, 'col', [(i, i ^ bits) for i in range(count)])]
    unnamed x236 -> x318, local copies, waits for them, and re-layouts: 16.8 us -> 48.2 us
    slice x11 -> x6, local copies, waits for them, and re-layouts: 11.4 us -> 1.92 us  [the longest x5 1.3 us: last_half(): return [v[v.shape[0] // 2:] for v in pairs] if direct else pairs[1:]]
    ppermute x67 -> x61, starting transfers between devices: 61.8 us -> 54.7 us  [flip(): return lax.ppermute(values, 'col', [(i, i ^ bits) for i in range(count)])]
  transfers between devices with their start and end apart: 79 -> 73, of which waited for: 36 -> 28; matrix products, arithmetic and copies ran while one was open for 26% -> 14% of each run, Pallas kernels for 16% -> 33%
where the time goes in v3:
time: 618 us; the launch traced here: 611 us
  Pallas kernels  203 us (33%)
  waiting for transfers between devices  193 us (31%)
  local copies, waits for them, and re-layouts  67.3 us (11%)
  starting transfers between devices  66.7 us (11%)
  other arithmetic  60.5 us (10%)
  between operations  20.2 us (3%)
    ppermute x61, waiting for transfers between devices, flip(): return lax.ppermute(values, 'col', [(i, i ^ bits) for i in range(count)])  189 us
    pallas_call x16, Pallas kernels, product(): pl.pallas_call(functools.partial(product_kernel, make=make, in_count=len(...  60.9 us
    ppermute x61, starting transfers between devices, flip(): return lax.ppermute(values, 'col', [(i, i ^ bits) for i in range(count)])  54.7 us
    unnamed x318, local copies, waits for them, and re-layouts  48.2 us
    pallas_call x4, Pallas kernels, weight_grad(): pl.pallas_call(functools.partial(weight_kernel, x_count=len(xs), y_count=...  43.9 us
    pallas_call x2, Pallas kernels, attention_back(): pl.pallas_call(functools.partial(attend_backward, piece=piece, blk=min(25...  25.5 us
    pallas_call x4, Pallas kernels, expand(): pl.pallas_call(expand_kernel, out_shape=(full, full), grid=(rows // strip...  23.8 us
    pallas_call x2, Pallas kernels, attention(): pl.pallas_call(functools.partial(attend_forward, piece=piece, blk=min(256...  20 us
  transfers between devices with their start and end apart: 73, of which 28 were waited for; matrix products, arithmetic and copies ran while one was open for 14% of the time, Pallas kernels for 33%

profile of v3, /device:TPU:0, one launch (start us, length us, event | category | flops | bytes accessed | tf_op | source)
XLA Modules:
  0.0 611.0 jit_solution(17798216943373153550)
XLA Ops:
  8.0 4.1 collective-permute-start.1
  13.7 2.2 collective-permute-start.2
  20.8 2.5 collective-permute-start.5
  27.2 9.5 %collective-permute-done.5 = bf16[128,2048]{1,0:T(8,128)(2,1)S(1)} collective-permute-done((bf16[128,2048]{1,0:T(8,128)(2,1)S(1)}, bf16[128,2048]{1,0:T(8,128)(2,1)S(1)}, u32[]{:S(2)}, u32[]{:S(2)}) %collective-permute-start.5) | collective-permute-done | bytes 524320 | tf_op jit(solution)/shard_map/ppermute | solution.py:465
  36.6 9.2 %collective-permute-done.4 = bf16[128,2048]{1,0:T(8,128)(2,1)S(1)} collective-permute-done((bf16[128,2048]{1,0:T(8,128)(2,1)S(1)}, bf16[128,2048]{1,0:T(8,128)(2,1)S(1)}, u32[]{:S(2)}, u32[]{:S(2)}) %collective-permute-start.4) | collective-permute-done | bytes 524320 | tf_op jit(solution)/shard_map/ppermute | solution.py:465
  49.4 12.2 %collective-permute-done.8 = bf16[128,2048]{1,0:T(8,128)(2,1)S(1)} collective-permute-done((bf16[128,2048]{1,0:T(8,128)(2,1)S(1)}, bf16[128,2048]{1,0:T(8,128)(2,1)S(1)}, u32[]{:S(2)}, u32[]{:S(2)}) %collective-permute-start.8) | collective-permute-done | bytes 524320 | tf_op jit(solution)/shard_map/ppermute | solution.py:465
  61.7 10.3 %collective-permute-done.7 = bf16[128,2048]{1,0:T(8,128)(2,1)S(1)} collective-permute-done((bf16[128,2048]{1,0:T(8,128)(2,1)S(1)}, bf16[128,2048]{1,0:T(8,128)(2,1)S(1)}, u32[]{:S(2)}, u32[]{:S(2)}) %collective-permute-start.7) | collective-permute-done | bytes 524320 | tf_op jit(solution)/shard_map/ppermute | solution.py:465
  75.6 12.2 %collective-permute-done.11 = bf16[128,2048]{1,0:T(8,128)(2,1)S(1)} collective-permute-done((bf16[128,2048]{1,0:T(8,128)(2,1)S(1)}, bf16[128,2048]{1,0:T(8,128)(2,1)S(1)}, u32[]{:S(2)}, u32[]{:S(2)}) %collective-permute-start.11) | collective-permute-done | bytes 524320 | tf_op jit(solution)/shard_map/ppermute | solution.py:465
  87.8 10.2 %collective-permute-done.10 = bf16[128,2048]{1,0:T(8,128)(2,1)S(1)} collective-permute-done((bf16[128,2048]{1,0:T(8,128)(2,1)S(1)}, bf16[128,2048]{1,0:T(8,128)(2,1)S(1)}, u32[]{:S(2)}, u32[]{:S(2)}) %collective-permute-start.10) | collective-permute-done | bytes 524320 | tf_op jit(solution)/shard_map/ppermute | solution.py:465
  111.3 5.6 project.2
  118.5 10.1 %attend_forward.2 = (bf16[1024,256]{1,0:T(8,128)(2,1)S(1)}, bf16[1024,256]{1,0:T(8,128)(2,1)S(1)}, bf16[1024,256]{1,0:T(8,128)(2,1)S(1)}, bf16[1024,256]{1,0:T(8,128)(2,1)S(1)}, f32[4,8,1024]{2,1,0:T(8,128)S(1)}) custom-call(s32[8]{0:T(128)S(1)} %shift-right-arithmetic_add_fusion.spot_ref, f32[3,1024,256]{2,1,0:T(8,128)} %bitcast.203, ...), custom_call_target="tpu_custom_call" | custom-call | flops 1000 | bytes 1000 | tf_op jit(solution)/shard_map/attend_forward/pallas_call | solution.py:183
  135.8 2.6 mix.5
  145.4 2.2 copy-done.2
  147.7 5.4 project.3
  154.8 9.8 %attend_forward.3 = (bf16[1024,256]{1,0:T(8,128)(2,1)S(1)}, bf16[1024,256]{1,0:T(8,128)(2,1)S(1)}, bf16[1024,256]{1,0:T(8,128)(2,1)S(1)}, bf16[1024,256]{1,0:T(8,128)(2,1)S(1)}, f32[4,8,1024]{2,1,0:T(8,128)S(1)}) custom-call(s32[8]{0:T(128)S(1)} %shift-right-arithmetic_add_fusion.spot_ref, f32[3,1024,256]{2,1,0:T(8,128)} %bitcast.200, ...), custom_call_target="tpu_custom_call" | custom-call | flops 1000 | bytes 1000 | tf_op jit(solution)/shard_map/attend_forward/pallas_call | solution.py:183
  168.5 2.8 mix.6
  176.7 10.4 %collective-permute-done.23 = bf16[128,2048]{1,0:T(8,128)(2,1)} collective-permute-done((bf16[128,2048]{1,0:T(8,128)(2,1)S(1)}, bf16[128,2048]{1,0:T(8,128)(2,1)}, u32[]{:S(2)}, u32[]{:S(2)}) %collective-permute-start.23) | collective-permute-done | bytes 524320 | tf_op jit(solution)/shard_map/ppermute | solution.py:465
  187.1 10.7 %collective-permute-done.22 = bf16[128,2048]{1,0:T(8,128)(2,1)} collective-permute-done((bf16[128,2048]{1,0:T(8,128)(2,1)S(1)}, bf16[128,2048]{1,0:T(8,128)(2,1)}, u32[]{:S(2)}, u32[]{:S(2)}) %collective-permute-start.22) | collective-permute-done | bytes 524320 | tf_op jit(solution)/shard_map/ppermute | solution.py:465
  198.8 4.2 mix.7
  212.2 5.9 collective-permute-done.26
  218.1 11.5 %collective-permute-done.27 = bf16[128,2048]{1,0:T(8,128)(2,1)} collective-permute-done((bf16[128,2048]{1,0:T(8,128)(2,1)}, bf16[128,2048]{1,0:T(8,128)(2,1)}, u32[]{:S(2)}, u32[]{:S(2)}) %collective-permute-start.27) | collective-permute-done | bytes 524320 | tf_op jit(solution)/shard_map/ppermute | solution.py:465
  236.7 5.9 expand.4
  243.6 5.9 expand.5
  249.6 7.3 %collective-permute-done.30 = bf16[128,2048]{1,0:T(8,128)(2,1)S(1)} collective-permute-done((bf16[128,2048]{1,0:T(8,128)(2,1)S(1)}, bf16[128,2048]{1,0:T(8,128)(2,1)S(1)}, u32[]{:S(2)}, u32[]{:S(2)}) %collective-permute-start.30) | collective-permute-done | bytes 524320 | tf_op jit(solution)/shard_map/ppermute | solution.py:465
  258.2 5.8 expand.6
  264.1 6.2 %expand.7 = (bf16[512,1024]{1,0:T(8,128)(2,1)S(1)}, bf16[512,1024]{1,0:T(8,128)(2,1)S(1)}) custom-call(bf16[512,2048]{1,0:T(8,128)(2,1)S(1)} %collective-permute-done.32.x_ref.refs_3_, bf16[2048,1024]{1,0:T(8,128)(2,1)} %all-gather.6.cloned.1.call-done.w_ref.refs_1_), custom_call_target="tpu_custom_call" | custom-call | flops 1000 | bytes 1000 | tf_op jit(solution)/shard_map/expand/pallas_call | solution.py:233
  272.6 14.4 %weight_grad.4 = bf16[4,1024,512]{2,1,0:T(8,128)(2,1)} custom-call(bf16[512,1024]{1,0:T(8,128)(2,1)S(1)} %get-tuple-element.235.refs_0_, bf16[512,1024]{1,0:T(8,128)(2,1)S(1)} %copy-done.56, bf16[512,1024]{1,0:T(8,128)(2,1)S(1)} %get-tuple-element.238.refs_2_.refs_0_, bf16[512,1024]{1,0:T(8,128)(2,1)S(1)} %get-tuple-element.224.refs_3_.refs_0_, ...), custom_call_target="tpu_custom_call" | custom-call | flops 1000 | bytes 1000 | tf_op jit(solution)/shard_map/weight_grad/pallas_call | solution.py:442
  289.1 2.3 copy-done.10
  291.4 5.8 scaled_product.5.refs_0_.refs_5_
  297.2 3.1 unexpand.4
  300.6 3.3 scaled_product.4.refs_0_.refs_4_
  304.6 3.3 unexpand.5
  311.5 3.3 scaled_product.7.refs_0_.refs_7_
  314.8 3.1 unexpand.6
  317.9 4.8 collective-permute-done.36
  322.8 11.2 %collective-permute-done.37 = bf16[128,2048]{1,0:T(8,128)(2,1)S(1)} collective-permute-done((bf16[128,2048]{1,0:T(8,128)(2,1)S(1)}, bf16[128,2048]{1,0:T(8,128)(2,1)S(1)}, u32[]{:S(2)}, u32[]{:S(2)}) %collective-permute-start.37) | collective-permute-done | bytes 524320 | tf_op jit(solution)/shard_map/ppermute | solution.py:465
  334.0 3.3 scaled_product.6.refs_0_.refs_6_
  339.0 2.4 fusion.63
  341.4 3.3 unexpand.7
  348.0 12.7 %weight_grad.5 = bf16[2048,1024]{1,0:T(8,128)(2,1)} custom-call(bf16[512,2048]{1,0:T(8,128)(2,1)} %constant_dynamic-update-slice_fusion.8.x_ref.refs_0_, bf16[512,2048]{1,0:T(8,128)(2,1)} %collective-permute-done.24.x_ref.refs_1_, bf16[512,2048]{1,0:T(8,128)(2,1)} %copy-done.31, bf16[512,2048]{1,0:T(8,128)(2,1)} %copy-done.35, ...), custom_call_target="tpu_custom_call" | custom-call | flops 1000 | bytes 1000 | tf_op jit(solution)/shard_map/weight_grad/pallas_call | solution.py:442
  360.7 2.4 pad_maximum_fusion.2
  367.9 4.4 contract.5
  372.3 5.4 contract.4
  377.7 12.4 %collective-permute-done.42 = bf16[256,2048]{1,0:T(8,128)(2,1)S(1)} collective-permute-done((bf16[256,2048]{1,0:T(8,128)(2,1)S(1)}, bf16[256,2048]{1,0:T(8,128)(2,1)S(1)}, u32[]{:S(2)}, u32[]{:S(2)}) %collective-permute-start.42) | collective-permute-done | bytes 1048608 | tf_op jit(solution)/shard_map/ppermute | solution.py:465
  390.2 21.9 %collective-permute-done.40 = bf16[256,2048]{1,0:T(8,128)(2,1)S(1)} collective-permute-done((bf16[256,2048]{1,0:T(8,128)(2,1)S(1)}, bf16[256,2048]{1,0:T(8,128)(2,1)S(1)}, u32[]{:S(2)}, u32[]{:S(2)}) %collective-permute-start.40) | collective-permute-done | bytes 1048608 | tf_op jit(solution)/shard_map/ppermute | solution.py:465
  415.7 2.5 fusion.62
  423.2 12.7 %attend_backward.2.refs_4_.refs_0_ = bf16[3,1024,256]{2,1,0:T(8,128)(2,1)S(1)} custom-call(s32[8]{0:T(128)S(1)} %shift-right-arithmetic_add_fusion.spot_ref, bf16[1024,256]{1,0:T(8,128)(2,1)S(1)} %copy-done.75, bf16[1024,256]{1,0:T(8,128)(2,1)S(1)} %copy-done.77, bf16[1024,256]{1,0:T(8,128)(2,1)S(1)} %copy-done.79, bf16[1024,256]{1,0:T(8,128)(2,1)S(1)} %bitcast.207, ...), custom_call_target="tpu_custom_call" | custom-call | flops 1000 | bytes 1000 | tf_op jit(solution)/shard_map/attend_backward/pallas_call | solution.py:202
  436.0 5.5 contract.6
  444.7 5.1 contract.7
  464.2 12.7 %attend_backward.3.refs_5_.refs_0_ = bf16[3,1024,256]{2,1,0:T(8,128)(2,1)S(1)} custom-call(s32[8]{0:T(128)S(1)} %shift-right-arithmetic_add_fusion.spot_ref, bf16[1024,256]{1,0:T(8,128)(2,1)S(1)} %copy-done.69, bf16[1024,256]{1,0:T(8,128)(2,1)S(1)} %copy-done.71, bf16[1024,256]{1,0:T(8,128)(2,1)S(1)} %copy-done.73, bf16[1024,256]{1,0:T(8,128)(2,1)S(1)} %bitcast.206, ...), custom_call_target="tpu_custom_call" | custom-call | flops 1000 | bytes 1000 | tf_op jit(solution)/shard_map/attend_backward/pallas_call | solution.py:202
  477.0 5.8 weight_grad.6.refs_6_
  484.4 11.0 %weight_grad.7 = bf16[4,4,512,256]{3,2,1,0:T(8,128)(2,1)} custom-call(bf16[512,2048]{1,0:T(8,128)(2,1)S(1)} %copy-done.27, bf16[512,2048]{1,0:T(8,128)(2,1)} %collective-permute-done.12.refs_1_, bf16[512,2048]{1,0:T(8,128)(2,1)} %copy-done.25, bf16[512,2048]{1,0:T(8,128)(2,1)} %collective-permute-done.20.refs_1_.refs_3_, ...), custom_call_target="tpu_custom_call", output_to_operand_aliasing={{}: (6, {})} | custom-call | flops 1000 | bytes 1000 | tf_op jit(solution)/shard_map/weight_grad/pallas_call | solution.py:442
  495.4 11.5 %collective-permute-done.47 = bf16[256,2048]{1,0:T(8,128)(2,1)} collective-permute-done((bf16[256,2048]{1,0:T(8,128)(2,1)}, bf16[256,2048]{1,0:T(8,128)(2,1)}, u32[]{:S(2)}, u32[]{:S(2)}) %collective-permute-start.47) | collective-permute-done | bytes 1048608 | tf_op jit(solution)/shard_map/ppermute | solution.py:465
  509.1 3.7 unproject.6
  512.8 3.6 unproject.4
  517.0 2.8 bitcast_convert_fusion.2
  527.7 4.2 unproject.7
  534.2 5.1 unproject.5
  549.2 5.4 fusion.50
  554.6 5.3 fusion.49
  564.4 4.5 broadcast_multiply_fusion
  568.9 11.6 %collective-permute-done.57 = bf16[128,2048]{1,0:T(8,128)(2,1)S(1)} collective-permute-done((bf16[128,2048]{1,0:T(8,128)(2,1)S(1)}, bf16[128,2048]{1,0:T(8,128)(2,1)S(1)}, u32[]{:S(2)}, u32[]{:S(2)}) %collective-permute-start.57) | collective-permute-done | bytes 524320 | tf_op jit(solution)/shard_map/ppermute | solution.py:465
  582.9 3.2 collective-permute-start.63
  588.3 2.3 collective-permute-done.62
  (556 shorter events, 164.6 us)
Async XLA Ops:
  7.2 101.9 %all-gather.4.cloned.1.call-start = ((), (), s32[]{:S(2)}) async-start(), calls=%async_computation.3 | async-start | bytes 5242880 | tf_op jit(solution)/shard_map/all_gather | solution.py:571
  8.0 17.2 %collective-permute-start.1 = (bf16[4,512]{1,0:T(4,128)(2,1)S(1)}, bf16[4,512]{1,0:T(4,128)(2,1)S(1)}, u32[]{:S(2)}, u32[]{:S(2)}) collective-permute-start(bf16[4,512]{1,0:T(4,128)(2,1)S(1)} %pad_maximum_fusion.13), channel_id=1, source_target_pairs={{0,16},{8,24},{16,0},{24,8},{1,17},{9,25},{17,1},{25,9},{2,18},{10... | collective-permute-start | bytes 12296 | tf_op jit(solution)/shard_map/ppermute | solution.py:522
  12.2 12.5 %collective-permute-start = (bf16[4,512]{1,0:T(4,128)(2,1)S(1)}, bf16[4,512]{1,0:T(4,128)(2,1)S(1)}, u32[]{:S(2)}, u32[]{:S(2)}) collective-permute-start(bf16[4,512]{1,0:T(4,128)(2,1)S(1)} %pad_maximum_fusion.13), channel_id=1, source_target_pairs={{0,8},{8,16},{16,24},{24,0},{1,9},{9,17},{17,25},{25,1},{2,10},{10... | collective-permute-start | bytes 12296 | tf_op jit(solution)/shard_map/ppermute | solution.py:522
  13.7 11.6 %collective-permute-start.2 = (bf16[4,512]{1,0:T(4,128)(2,1)S(1)}, bf16[4,512]{1,0:T(4,128)(2,1)S(1)}, u32[]{:S(2)}, u32[]{:S(2)}) collective-permute-start(bf16[4,512]{1,0:T(4,128)(2,1)S(1)} %pad_maximum_fusion.13), channel_id=1, source_target_pairs={{0,24},{8,0},{16,8},{24,16},{1,25},{9,1},{17,9},{25,17},{2,26},{10... | collective-permute-start | bytes 12296 | tf_op jit(solution)/shard_map/ppermute | solution.py:522
  19.2 193.0 %all-gather.6.cloned.1.call-start = ((), (), s32[]{:S(2)}) async-start(), calls=%async_computation.4 | async-start | bytes 5242880 | tf_op jit(solution)/shard_map/all_gather | solution.py:574
  20.8 15.8 %collective-permute-start.5 = (bf16[128,2048]{1,0:T(8,128)(2,1)S(1)}, bf16[128,2048]{1,0:T(8,128)(2,1)S(1)}, u32[]{:S(2)}, u32[]{:S(2)}) collective-permute-start(bf16[128,2048]{1,0:T(8,128)(2,1)S(1)} %get-tuple-element.335), channel_id=1, source_target_pairs={{0,6},{1,7},{2,4},{3,5},{4,2},{5,3},{6,0},{7,1},{8,14},{9,15},{10,... | collective-permute-start | bytes 1572872 | tf_op jit(solution)/shard_map/ppermute | solution.py:465
  23.3 22.5 %collective-permute-start.4 = (bf16[128,2048]{1,0:T(8,128)(2,1)S(1)}, bf16[128,2048]{1,0:T(8,128)(2,1)S(1)}, u32[]{:S(2)}, u32[]{:S(2)}) collective-permute-start(bf16[128,2048]{1,0:T(8,128)(2,1)S(1)} %get-tuple-element.335), channel_id=1, source_target_pairs={{0,4},{1,5},{2,6},{3,7},{4,0},{5,1},{6,2},{7,3},{8,12},{9,13},{10,... | collective-permute-start | bytes 1572872 | tf_op jit(solution)/shard_map/ppermute | solution.py:465
  24.7 21.3 %collective-permute-start.3 = (bf16[128,2048]{1,0:T(8,128)(2,1)S(1)}, bf16[128,2048]{1,0:T(8,128)(2,1)S(1)}, u32[]{:S(2)}, u32[]{:S(2)}) collective-permute-start(bf16[128,2048]{1,0:T(8,128)(2,1)S(1)} %get-tuple-element.335), channel_id=1, source_target_pairs={{0,2},{1,3},{2,0},{3,1},{4,6},{5,7},{6,4},{7,5},{8,10},{9,11},{10,... | collective-permute-start | bytes 1572872 | tf_op jit(solution)/shard_map/ppermute | solution.py:465
  45.9 15.7 %collective-permute-start.8 = (bf16[128,2048]{1,0:T(8,128)(2,1)S(1)}, bf16[128,2048]{1,0:T(8,128)(2,1)S(1)}, u32[]{:S(2)}, u32[]{:S(2)}) collective-permute-start(bf16[128,2048]{1,0:T(8,128)(2,1)S(1)} %get-tuple-element.156), channel_id=1, source_target_pairs={{0,6},{1,7},{2,4},{3,5},{4,2},{5,3},{6,0},{7,1},{8,14},{9,15},{10,... | collective-permute-start | bytes 1572872 | tf_op jit(solution)/shard_map/ppermute | solution.py:465
  47.6 24.3 %collective-permute-start.7 = (bf16[128,2048]{1,0:T(8,128)(2,1)S(1)}, bf16[128,2048]{1,0:T(8,128)(2,1)S(1)}, u32[]{:S(2)}, u32[]{:S(2)}) collective-permute-start(bf16[128,2048]{1,0:T(8,128)(2,1)S(1)} %get-tuple-element.156), channel_id=1, source_target_pairs={{0,4},{1,5},{2,6},{3,7},{4,0},{5,1},{6,2},{7,3},{8,12},{9,13},{10,... | collective-permute-start | bytes 1572872 | tf_op jit(solution)/shard_map/ppermute | solution.py:465
  48.9 23.2 %collective-permute-start.6 = (bf16[128,2048]{1,0:T(8,128)(2,1)S(1)}, bf16[128,2048]{1,0:T(8,128)(2,1)S(1)}, u32[]{:S(2)}, u32[]{:S(2)}) collective-permute-start(bf16[128,2048]{1,0:T(8,128)(2,1)S(1)} %get-tuple-element.156), channel_id=1, source_target_pairs={{0,2},{1,3},{2,0},{3,1},{4,6},{5,7},{6,4},{7,5},{8,10},{9,11},{10,... | collective-permute-start | bytes 1572872 | tf_op jit(solution)/shard_map/ppermute | solution.py:465
  72.1 15.7 %collective-permute-start.11 = (bf16[128,2048]{1,0:T(8,128)(2,1)S(1)}, bf16[128,2048]{1,0:T(8,128)(2,1)S(1)}, u32[]{:S(2)}, u32[]{:S(2)}) collective-permute-start(bf16[128,2048]{1,0:T(8,128)(2,1)S(1)} %get-tuple-element.155), channel_id=1, source_target_pairs={{0,6},{1,7},{2,4},{3,5},{4,2},{5,3},{6,0},{7,1},{8,14},{9,15},{10,... | collective-permute-start | bytes 1572872 | tf_op jit(solution)/shard_map/ppermute | solution.py:465
  73.5 24.6 %collective-permute-start.10 = (bf16[128,2048]{1,0:T(8,128)(2,1)S(1)}, bf16[128,2048]{1,0:T(8,128)(2,1)S(1)}, u32[]{:S(2)}, u32[]{:S(2)}) collective-permute-start(bf16[128,2048]{1,0:T(8,128)(2,1)S(1)} %get-tuple-element.155), channel_id=1, source_target_pairs={{0,4},{1,5},{2,6},{3,7},{4,0},{5,1},{6,2},{7,3},{8,12},{9,13},{10,... | collective-permute-start | bytes 1572872 | tf_op jit(solution)/shard_map/ppermute | solution.py:465
  74.9 24.0 %collective-permute-start.9 = (bf16[128,2048]{1,0:T(8,128)(2,1)S(1)}, bf16[128,2048]{1,0:T(8,128)(2,1)}, u32[]{:S(2)}, u32[]{:S(2)}) collective-permute-start(bf16[128,2048]{1,0:T(8,128)(2,1)S(1)} %get-tuple-element.155), channel_id=1, source_target_pairs={{0,2},{1,3},{2,0},{3,1},{4,6},{5,7},{6,4},{7,5},{8,10},{9,11},{10,... | collective-permute-start | bytes 1572872 | tf_op jit(solution)/shard_map/ppermute | solution.py:465
  99.2 9.9 %collective-permute-start.12 = (bf16[512,2048]{1,0:T(8,128)(2,1)S(1)}, bf16[512,2048]{1,0:T(8,128)(2,1)}, u32[]{:S(2)}, u32[]{:S(2)}) collective-permute-start(bf16[512,2048]{1,0:T(8,128)(2,1)S(1)} %constant_dynamic-update-slice_fusion.refs_0_), channel_id=1, source_target_pairs={{0,1},{1,0},{2,3},{3,2},{4,5},{5,4},{6,7},{7,6},{8,9},{9,8},{10,11... | collective-permute-start | bytes 6291464 | tf_op jit(solution)/shard_map/ppermute | solution.py:465
  99.4 188.6 %all-gather.8.cloned.1.call-start = ((), (), s32[]{:S(2)}) async-start(), calls=%async_computation.5 | async-start | bytes 5242880 | tf_op jit(solution)/shard_map/all_gather | solution.py:575
  100.7 30.9 %collective-permute-start.17 = (bf16[128,2048]{1,0:T(8,128)(2,1)}, bf16[128,2048]{1,0:T(8,128)(2,1)}, u32[]{:S(2)}, u32[]{:S(2)}) collective-permute-start(bf16[128,2048]{1,0:T(8,128)(2,1)} %get-tuple-element.167), channel_id=1, source_target_pairs={{0,2},{1,3},{2,0},{3,1},{4,6},{5,7},{6,4},{7,5},{8,10},{9,11},{10,... | collective-permute-start | bytes 1572872 | tf_op jit(solution)/shard_map/ppermute | solution.py:465
  102.9 29.9 %collective-permute-start.18 = (bf16[128,2048]{1,0:T(8,128)(2,1)}, bf16[128,2048]{1,0:T(8,128)(2,1)}, u32[]{:S(2)}, u32[]{:S(2)}) collective-permute-start(bf16[128,2048]{1,0:T(8,128)(2,1)} %get-tuple-element.167), channel_id=1, source_target_pairs={{0,4},{1,5},{2,6},{3,7},{4,0},{5,1},{6,2},{7,3},{8,12},{9,13},{10,... | collective-permute-start | bytes 1572872 | tf_op jit(solution)/shard_map/ppermute | solution.py:465
  107.3 26.6 %collective-permute-start.19 = (bf16[128,2048]{1,0:T(8,128)(2,1)}, bf16[128,2048]{1,0:T(8,128)(2,1)}, u32[]{:S(2)}, u32[]{:S(2)}) collective-permute-start(bf16[128,2048]{1,0:T(8,128)(2,1)} %get-tuple-element.167), channel_id=1, source_target_pairs={{0,6},{1,7},{2,4},{3,5},{4,2},{5,3},{6,0},{7,1},{8,14},{9,15},{10,... | collective-permute-start | bytes 1572872 | tf_op jit(solution)/shard_map/ppermute | solution.py:465
  135.0 10.5 %collective-permute-start.20 = (bf16[512,2048]{1,0:T(8,128)(2,1)S(1)}, bf16[512,2048]{1,0:T(8,128)(2,1)}, u32[]{:S(2)}, u32[]{:S(2)}) collective-permute-start(bf16[512,2048]{1,0:T(8,128)(2,1)S(1)} %constant_dynamic-update-slice_fusion.4.refs_0_.refs_2_), channel_id=1, source_target_pairs={{0,1},{1,0},{2,3},{3,2},{4,5},{5,4},{6,7},{7,6},{8,9},{9,8},{10,11... | collective-permute-start | bytes 6291464 | tf_op jit(solution)/shard_map/ppermute | solution.py:465
  138.4 26.2 %collective-permute-start.14 = (bf16[128,2048]{1,0:T(8,128)(2,1)}, bf16[128,2048]{1,0:T(8,128)(2,1)}, u32[]{:S(2)}, u32[]{:S(2)}) collective-permute-start(bf16[128,2048]{1,0:T(8,128)(2,1)} %get-tuple-element.164), channel_id=1, source_target_pairs={{0,2},{1,3},{2,0},{3,1},{4,6},{5,7},{6,4},{7,5},{8,10},{9,11},{10,... | collective-permute-start | bytes 1572872 | tf_op jit(solution)/shard_map/ppermute | solution.py:465
  139.9 25.2 %collective-permute-start.15 = (bf16[128,2048]{1,0:T(8,128)(2,1)}, bf16[128,2048]{1,0:T(8,128)(2,1)}, u32[]{:S(2)}, u32[]{:S(2)}) collective-permute-start(bf16[128,2048]{1,0:T(8,128)(2,1)} %get-tuple-element.165), channel_id=1, source_target_pairs={{0,4},{1,5},{2,6},{3,7},{4,0},{5,1},{6,2},{7,3},{8,12},{9,13},{10,... | collective-permute-start | bytes 1572872 | tf_op jit(solution)/shard_map/ppermute | solution.py:465
  140.3 24.9 %collective-permute-start.16 = (bf16[128,2048]{1,0:T(8,128)(2,1)}, bf16[128,2048]{1,0:T(8,128)(2,1)}, u32[]{:S(2)}, u32[]{:S(2)}) collective-permute-start(bf16[128,2048]{1,0:T(8,128)(2,1)} %get-tuple-element.166), channel_id=1, source_target_pairs={{0,6},{1,7},{2,4},{3,5},{4,2},{5,3},{6,0},{7,1},{8,14},{9,15},{10,... | collective-permute-start | bytes 1572872 | tf_op jit(solution)/shard_map/ppermute | solution.py:465
  171.2 26.8 %collective-permute-start.25 = (bf16[512,2048]{1,0:T(8,128)(2,1)}, bf16[512,2048]{1,0:T(8,128)(2,1)}, u32[]{:S(2)}, u32[]{:S(2)}) collective-permute-start(bf16[512,2048]{1,0:T(8,128)(2,1)} %mix.6), channel_id=1, source_target_pairs={{0,1},{1,0},{2,3},{3,2},{4,5},{5,4},{6,7},{7,6},{8,9},{9,8},{10,11... | collective-permute-start | bytes 6291464 | tf_op jit(solution)/shard_map/ppermute | solution.py:465
  171.2 15.8 %collective-permute-start.23 = (bf16[128,2048]{1,0:T(8,128)(2,1)S(1)}, bf16[128,2048]{1,0:T(8,128)(2,1)}, u32[]{:S(2)}, u32[]{:S(2)}) collective-permute-start(bf16[128,2048]{1,0:T(8,128)(2,1)S(1)} %add_convert_fusion.1), channel_id=1, source_target_pairs={{0,6},{1,7},{2,4},{3,5},{4,2},{5,3},{6,0},{7,1},{8,14},{9,15},{10,... | collective-permute-start | bytes 1572872 | tf_op jit(solution)/shard_map/ppermute | solution.py:465
  172.7 25.1 %collective-permute-start.22 = (bf16[128,2048]{1,0:T(8,128)(2,1)S(1)}, bf16[128,2048]{1,0:T(8,128)(2,1)}, u32[]{:S(2)}, u32[]{:S(2)}) collective-permute-start(bf16[128,2048]{1,0:T(8,128)(2,1)S(1)} %add_convert_fusion.1), channel_id=1, source_target_pairs={{0,4},{1,5},{2,6},{3,7},{4,0},{5,1},{6,2},{7,3},{8,12},{9,13},{10,... | collective-permute-start | bytes 1572872 | tf_op jit(solution)/shard_map/ppermute | solution.py:465
  174.3 23.7 %collective-permute-start.21 = (bf16[128,2048]{1,0:T(8,128)(2,1)S(1)}, bf16[128,2048]{1,0:T(8,128)(2,1)}, u32[]{:S(2)}, u32[]{:S(2)}) collective-permute-start(bf16[128,2048]{1,0:T(8,128)(2,1)S(1)} %add_convert_fusion.1), channel_id=1, source_target_pairs={{0,2},{1,3},{2,0},{3,1},{4,6},{5,7},{6,4},{7,5},{8,10},{9,11},{10,... | collective-permute-start | bytes 1572872 | tf_op jit(solution)/shard_map/ppermute | solution.py:465
  174.8 275.1 %reduce-scatter.4.cloned.1.call-start = ((), (), s32[]{:S(2)}) async-start(), calls=%async_computation.6 | async-start | bytes 5242880 | tf_op jit(solution)/shard_map/reduce_scatter | solution.py:662
  176.6 94.6 %collective-permute-start.33 = (bf16[512,2048]{1,0:T(8,128)(2,1)S(1)}, bf16[512,2048]{1,0:T(8,128)(2,1)}, u32[]{:S(2)}, u32[]{:S(2)}) collective-permute-start(bf16[512,2048]{1,0:T(8,128)(2,1)S(1)} %pad_maximum_fusion.refs_4_.x_ref.refs_3_), channel_id=1, source_target_pairs={{0,1},{1,0},{2,3},{3,2},{4,5},{5,4},{6,7},{7,6},{8,9},{9,8},{10,11... | collective-permute-start | bytes 6291464 | tf_op jit(solution)/shard_map/ppermute | solution.py:465
  203.1 15.0 %collective-permute-start.26 = (bf16[128,2048]{1,0:T(8,128)(2,1)}, bf16[128,2048]{1,0:T(8,128)(2,1)S(1)}, u32[]{:S(2)}, u32[]{:S(2)}) collective-permute-start(bf16[128,2048]{1,0:T(8,128)(2,1)} %get-tuple-element.187), channel_id=1, source_target_pairs={{0,2},{1,3},{2,0},{3,1},{4,6},{5,7},{6,4},{7,5},{8,10},{9,11},{10,... | collective-permute-start | bytes 1572872 | tf_op jit(solution)/shard_map/ppermute | solution.py:465
  204.4 25.1 %collective-permute-start.27 = (bf16[128,2048]{1,0:T(8,128)(2,1)}, bf16[128,2048]{1,0:T(8,128)(2,1)}, u32[]{:S(2)}, u32[]{:S(2)}) collective-permute-start(bf16[128,2048]{1,0:T(8,128)(2,1)} %get-tuple-element.188), channel_id=1, source_target_pairs={{0,4},{1,5},{2,6},{3,7},{4,0},{5,1},{6,2},{7,3},{8,12},{9,13},{10,... | collective-permute-start | bytes 1572872 | tf_op jit(solution)/shard_map/ppermute | solution.py:465
  205.0 24.5 %collective-permute-start.28 = (bf16[128,2048]{1,0:T(8,128)(2,1)}, bf16[128,2048]{1,0:T(8,128)(2,1)}, u32[]{:S(2)}, u32[]{:S(2)}) collective-permute-start(bf16[128,2048]{1,0:T(8,128)(2,1)} %get-tuple-element.189), channel_id=1, source_target_pairs={{0,6},{1,7},{2,4},{3,5},{4,2},{5,3},{6,0},{7,1},{8,14},{9,15},{10,... | collective-permute-start | bytes 1572872 | tf_op jit(solution)/shard_map/ppermute | solution.py:465
  212.2 31.4 %collective-permute-start.24 = (bf16[512,2048]{1,0:T(8,128)(2,1)}, bf16[512,2048]{1,0:T(8,128)(2,1)}, u32[]{:S(2)}, u32[]{:S(2)}) collective-permute-start(bf16[512,2048]{1,0:T(8,128)(2,1)} %constant_dynamic-update-slice_fusion.8.x_ref.refs_0_), channel_id=1, source_target_pairs={{0,1},{1,0},{2,3},{3,2},{4,5},{5,4},{6,7},{7,6},{8,9},{9,8},{10,11... | collective-permute-start | bytes 6291464 | tf_op jit(solution)/shard_map/ppermute | solution.py:465
  231.9 17.6 %collective-permute-start.31 = (bf16[128,2048]{1,0:T(8,128)(2,1)S(1)}, bf16[128,2048]{1,0:T(8,128)(2,1)S(1)}, u32[]{:S(2)}, u32[]{:S(2)}) collective-permute-start(bf16[128,2048]{1,0:T(8,128)(2,1)S(1)} %add_convert_fusion), channel_id=1, source_target_pairs={{0,6},{1,7},{2,4},{3,5},{4,2},{5,3},{6,0},{7,1},{8,14},{9,15},{10,... | collective-permute-start | bytes 1572872 | tf_op jit(solution)/shard_map/ppermute | solution.py:465
  233.5 23.4 %collective-permute-start.30 = (bf16[128,2048]{1,0:T(8,128)(2,1)S(1)}, bf16[128,2048]{1,0:T(8,128)(2,1)S(1)}, u32[]{:S(2)}, u32[]{:S(2)}) collective-permute-start(bf16[128,2048]{1,0:T(8,128)(2,1)S(1)} %add_convert_fusion), channel_id=1, source_target_pairs={{0,4},{1,5},{2,6},{3,7},{4,0},{5,1},{6,2},{7,3},{8,12},{9,13},{10,... | collective-permute-start | bytes 1572872 | tf_op jit(solution)/shard_map/ppermute | solution.py:465
  233.9 23.0 %collective-permute-start.29 = (bf16[128,2048]{1,0:T(8,128)(2,1)S(1)}, bf16[128,2048]{1,0:T(8,128)(2,1)S(1)}, u32[]{:S(2)}, u32[]{:S(2)}) collective-permute-start(bf16[128,2048]{1,0:T(8,128)(2,1)S(1)} %add_convert_fusion), channel_id=1, source_target_pairs={{0,2},{1,3},{2,0},{3,1},{4,6},{5,7},{6,4},{7,5},{8,10},{9,11},{10,... | collective-permute-start | bytes 1572872 | tf_op jit(solution)/shard_map/ppermute | solution.py:465
  258.0 13.2 %collective-permute-start.34 = (bf16[512,2048]{1,0:T(8,128)(2,1)S(1)}, bf16[512,2048]{1,0:T(8,128)(2,1)S(1)}, u32[]{:S(2)}, u32[]{:S(2)}) collective-permute-start(bf16[512,2048]{1,0:T(8,128)(2,1)S(1)} %constant_dynamic-update-slice_fusion.12.refs_6_.x_ref.refs_3_), channel_id=1, source_target_pairs={{0,1},{1,0},{2,3},{3,2},{4,5},{5,4},{6,7},{7,6},{8,9},{9,8},{10,11... | collective-permute-start | bytes 6291464 | tf_op jit(solution)/shard_map/ppermute | solution.py:465
  287.9 194.9 %reduce-scatter.6.cloned.1.call-start = ((), (), s32[]{:S(2)}) async-start(), calls=%async_computation.7 | async-start | bytes 5242880 | tf_op jit(solution)/shard_map/reduce_scatter | solution.py:731
  307.9 14.9 %collective-permute-start.36 = (bf16[128,2048]{1,0:T(8,128)(2,1)S(1)}, bf16[128,2048]{1,0:T(8,128)(2,1)S(1)}, u32[]{:S(2)}, u32[]{:S(2)}) collective-permute-start(bf16[128,2048]{1,0:T(8,128)(2,1)S(1)} %get-tuple-element.208), channel_id=1, source_target_pairs={{0,2},{1,3},{2,0},{3,1},{4,6},{5,7},{6,4},{7,5},{8,10},{9,11},{10,... | collective-permute-start | bytes 1572872 | tf_op jit(solution)/shard_map/ppermute | solution.py:465
  309.0 24.9 %collective-permute-start.37 = (bf16[128,2048]{1,0:T(8,128)(2,1)S(1)}, bf16[128,2048]{1,0:T(8,128)(2,1)S(1)}, u32[]{:S(2)}, u32[]{:S(2)}) collective-permute-start(bf16[128,2048]{1,0:T(8,128)(2,1)S(1)} %get-tuple-element.209), channel_id=1, source_target_pairs={{0,4},{1,5},{2,6},{3,7},{4,0},{5,1},{6,2},{7,3},{8,12},{9,13},{10,... | collective-permute-start | bytes 1572872 | tf_op jit(solution)/shard_map/ppermute | solution.py:465
  310.4 23.5 %collective-permute-start.38 = (bf16[128,2048]{1,0:T(8,128)(2,1)S(1)}, bf16[128,2048]{1,0:T(8,128)(2,1)S(1)}, u32[]{:S(2)}, u32[]{:S(2)}) collective-permute-start(bf16[128,2048]{1,0:T(8,128)(2,1)S(1)} %get-tuple-element.210), channel_id=1, source_target_pairs={{0,6},{1,7},{2,4},{3,5},{4,2},{5,3},{6,0},{7,1},{8,14},{9,15},{10,... | collective-permute-start | bytes 1572872 | tf_op jit(solution)/shard_map/ppermute | solution.py:465
  360.6 239.9 %reduce-scatter.8.cloned.1.call-start = ((), (), s32[]{:S(2)}) async-start(), calls=%async_computation.8 | async-start | bytes 5242880 | tf_op jit(solution)/shard_map/reduce_scatter | solution.py:799
  363.1 27.0 %collective-permute-start.42 = (bf16[256,2048]{1,0:T(8,128)(2,1)S(1)}, bf16[256,2048]{1,0:T(8,128)(2,1)S(1)}, u32[]{:S(2)}, u32[]{:S(2)}) collective-permute-start(bf16[256,2048]{1,0:T(8,128)(2,1)S(1)} %get-tuple-element.337), channel_id=1, source_target_pairs={{0,6},{1,7},{2,4},{3,5},{4,2},{5,3},{6,0},{7,1},{8,14},{9,15},{10,... | collective-permute-start | bytes 3145736 | tf_op jit(solution)/shard_map/ppermute | solution.py:465
  364.6 47.4 %collective-permute-start.40 = (bf16[256,2048]{1,0:T(8,128)(2,1)S(1)}, bf16[256,2048]{1,0:T(8,128)(2,1)S(1)}, u32[]{:S(2)}, u32[]{:S(2)}) collective-permute-start(bf16[256,2048]{1,0:T(8,128)(2,1)S(1)} %get-tuple-element.338), channel_id=1, source_target_pairs={{0,2},{1,3},{2,0},{3,1},{4,6},{5,7},{6,4},{7,5},{8,10},{9,11},{10,... | collective-permute-start | bytes 3145736 | tf_op jit(solution)/shard_map/ppermute | solution.py:465
  366.1 46.0 %collective-permute-start.41 = (bf16[256,2048]{1,0:T(8,128)(2,1)S(1)}, bf16[256,2048]{1,0:T(8,128)(2,1)S(1)}, u32[]{:S(2)}, u32[]{:S(2)}) collective-permute-start(bf16[256,2048]{1,0:T(8,128)(2,1)S(1)} %get-tuple-element.339), channel_id=1, source_target_pairs={{0,4},{1,5},{2,6},{3,7},{4,0},{5,1},{6,2},{7,3},{8,12},{9,13},{10,... | collective-permute-start | bytes 3145736 | tf_op jit(solution)/shard_map/ppermute | solution.py:465
  413.7 7.3 %collective-permute-start.43 = (bf16[512,2048]{1,0:T(8,128)(2,1)S(1)}, bf16[512,2048]{1,0:T(8,128)(2,1)S(1)}, u32[]{:S(2)}, u32[]{:S(2)}) collective-permute-start(bf16[512,2048]{1,0:T(8,128)(2,1)S(1)} %constant_dynamic-update-slice_fusion.20.refs_0_.refs_2_), channel_id=1, source_target_pairs={{0,1},{1,0},{2,3},{3,2},{4,5},{5,4},{6,7},{7,6},{8,9},{9,8},{10,11... | collective-permute-start | bytes 6291464 | tf_op jit(solution)/shard_map/ppermute | solution.py:465
  413.8 22.1 %collective-permute-start.44 = (bf16[512,2048]{1,0:T(8,128)(2,1)}, bf16[512,2048]{1,0:T(8,128)(2,1)}, u32[]{:S(2)}, u32[]{:S(2)}) collective-permute-start(bf16[512,2048]{1,0:T(8,128)(2,1)} %get-tuple-element.236), channel_id=1, source_target_pairs={{0,1},{1,0},{2,3},{3,2},{4,5},{5,4},{6,7},{7,6},{8,9},{9,8},{10,11... | collective-permute-start | bytes 6291464 | tf_op jit(solution)/shard_map/ppermute | solution.py:465
  414.2 30.5 %collective-permute-start.45 = (bf16[512,2048]{1,0:T(8,128)(2,1)}, bf16[512,2048]{1,0:T(8,128)(2,1)}, u32[]{:S(2)}, u32[]{:S(2)}) collective-permute-start(bf16[512,2048]{1,0:T(8,128)(2,1)} %get-tuple-element.239), channel_id=1, source_target_pairs={{0,1},{1,0},{2,3},{3,2},{4,5},{5,4},{6,7},{7,6},{8,9},{9,8},{10,11... | collective-permute-start | bytes 6291464 | tf_op jit(solution)/shard_map/ppermute | solution.py:465
  418.2 31.6 %collective-permute-start.51 = (bf16[128,2048]{1,0:T(8,128)(2,1)}, bf16[128,2048]{1,0:T(8,128)(2,1)}, u32[]{:S(2)}, u32[]{:S(2)}) collective-permute-start(bf16[128,2048]{1,0:T(8,128)(2,1)} %get-tuple-element.250), channel_id=1, source_target_pairs={{0,6},{1,7},{2,4},{3,5},{4,2},{5,3},{6,0},{7,1},{8,14},{9,15},{10,... | collective-permute-start | bytes 1572872 | tf_op jit(solution)/shard_map/ppermute | solution.py:465
  419.9 30.0 %collective-permute-start.50 = (bf16[128,2048]{1,0:T(8,128)(2,1)}, bf16[128,2048]{1,0:T(8,128)(2,1)}, u32[]{:S(2)}, u32[]{:S(2)}) collective-permute-start(bf16[128,2048]{1,0:T(8,128)(2,1)} %get-tuple-element.250), channel_id=1, source_target_pairs={{0,4},{1,5},{2,6},{3,7},{4,0},{5,1},{6,2},{7,3},{8,12},{9,13},{10,... | collective-permute-start | bytes 1572872 | tf_op jit(solution)/shard_map/ppermute | solution.py:465
  420.9 28.9 %collective-permute-start.49 = (bf16[128,2048]{1,0:T(8,128)(2,1)}, bf16[128,2048]{1,0:T(8,128)(2,1)}, u32[]{:S(2)}, u32[]{:S(2)}) collective-permute-start(bf16[128,2048]{1,0:T(8,128)(2,1)} %get-tuple-element.250), channel_id=1, source_target_pairs={{0,2},{1,3},{2,0},{3,1},{4,6},{5,7},{6,4},{7,5},{8,10},{9,11},{10,... | collective-permute-start | bytes 1572872 | tf_op jit(solution)/shard_map/ppermute | solution.py:465
  457.7 37.8 %collective-permute-start.48 = (bf16[256,2048]{1,0:T(8,128)(2,1)}, bf16[256,2048]{1,0:T(8,128)(2,1)}, u32[]{:S(2)}, u32[]{:S(2)}) collective-permute-start(bf16[256,2048]{1,0:T(8,128)(2,1)} %pad_maximum_fusion.9), channel_id=1, source_target_pairs={{0,6},{1,7},{2,4},{3,5},{4,2},{5,3},{6,0},{7,1},{8,14},{9,15},{10,... | collective-permute-start | bytes 3145736 | tf_op jit(solution)/shard_map/ppermute | solution.py:465
  459.2 47.7 %collective-permute-start.47 = (bf16[256,2048]{1,0:T(8,128)(2,1)}, bf16[256,2048]{1,0:T(8,128)(2,1)}, u32[]{:S(2)}, u32[]{:S(2)}) collective-permute-start(bf16[256,2048]{1,0:T(8,128)(2,1)} %pad_maximum_fusion.8), channel_id=1, source_target_pairs={{0,4},{1,5},{2,6},{3,7},{4,0},{5,1},{6,2},{7,3},{8,12},{9,13},{10,... | collective-permute-start | bytes 3145736 | tf_op jit(solution)/shard_map/ppermute | solution.py:465
  460.3 46.6 %collective-permute-start.46 = (bf16[256,2048]{1,0:T(8,128)(2,1)}, bf16[256,2048]{1,0:T(8,128)(2,1)}, u32[]{:S(2)}, u32[]{:S(2)}) collective-permute-start(bf16[256,2048]{1,0:T(8,128)(2,1)} %pad_maximum_fusion.7), channel_id=1, source_target_pairs={{0,2},{1,3},{2,0},{3,1},{4,6},{5,7},{6,4},{7,5},{8,10},{9,11},{10,... | collective-permute-start | bytes 3145736 | tf_op jit(solution)/shard_map/ppermute | solution.py:465
  512.7 12.1 %collective-permute-start.54 = (bf16[512,2048]{1,0:T(8,128)(2,1)}, bf16[512,2048]{1,0:T(8,128)(2,1)}, u32[]{:S(2)}, u32[]{:S(2)}) collective-permute-start(bf16[512,2048]{1,0:T(8,128)(2,1)} %unproject.6), channel_id=1, source_target_pairs={{0,1},{1,0},{2,3},{3,2},{4,5},{5,4},{6,7},{7,6},{8,9},{9,8},{10,11... | collective-permute-start | bytes 6291464 | tf_op jit(solution)/shard_map/ppermute | solution.py:465
  516.4 16.7 %collective-permute-start.53 = (bf16[512,2048]{1,0:T(8,128)(2,1)}, bf16[512,2048]{1,0:T(8,128)(2,1)}, u32[]{:S(2)}, u32[]{:S(2)}) collective-permute-start(bf16[512,2048]{1,0:T(8,128)(2,1)} %unproject.4), channel_id=1, source_target_pairs={{0,1},{1,0},{2,3},{3,2},{4,5},{5,4},{6,7},{7,6},{8,9},{9,8},{10,11... | collective-permute-start | bytes 6291464 | tf_op jit(solution)/shard_map/ppermute | solution.py:465
  531.9 31.2 %collective-permute-start.55 = (bf16[128,2048]{1,0:T(8,128)(2,1)S(1)}, bf16[128,2048]{1,0:T(8,128)(2,1)S(1)}, u32[]{:S(2)}, u32[]{:S(2)}) collective-permute-start(bf16[128,2048]{1,0:T(8,128)(2,1)S(1)} %get-tuple-element.268), channel_id=1, source_target_pairs={{0,2},{1,3},{2,0},{3,1},{4,6},{5,7},{6,4},{7,5},{8,10},{9,11},{10,... | collective-permute-start | bytes 1572872 | tf_op jit(solution)/shard_map/ppermute | solution.py:465
  533.2 35.7 %collective-permute-start.56 = (bf16[128,2048]{1,0:T(8,128)(2,1)S(1)}, bf16[128,2048]{1,0:T(8,128)(2,1)S(1)}, u32[]{:S(2)}, u32[]{:S(2)}) collective-permute-start(bf16[128,2048]{1,0:T(8,128)(2,1)S(1)} %get-tuple-element.269), channel_id=1, source_target_pairs={{0,4},{1,5},{2,6},{3,7},{4,0},{5,1},{6,2},{7,3},{8,12},{9,13},{10,... | collective-permute-start | bytes 1572872 | tf_op jit(solution)/shard_map/ppermute | solution.py:465
  539.3 41.2 %collective-permute-start.58 = (bf16[128,2048]{1,0:T(8,128)(2,1)S(1)}, bf16[128,2048]{1,0:T(8,128)(2,1)S(1)}, u32[]{:S(2)}, u32[]{:S(2)}) collective-permute-start(bf16[128,2048]{1,0:T(8,128)(2,1)S(1)} %get-tuple-element.258), channel_id=1, source_target_pairs={{0,2},{1,3},{2,0},{3,1},{4,6},{5,7},{6,4},{7,5},{8,10},{9,11},{10,... | collective-permute-start | bytes 1572872 | tf_op jit(solution)/shard_map/ppermute | solution.py:465
  540.2 40.4 %collective-permute-start.59 = (bf16[128,2048]{1,0:T(8,128)(2,1)S(1)}, bf16[128,2048]{1,0:T(8,128)(2,1)S(1)}, u32[]{:S(2)}, u32[]{:S(2)}) collective-permute-start(bf16[128,2048]{1,0:T(8,128)(2,1)S(1)} %get-tuple-element.259), channel_id=1, source_target_pairs={{0,4},{1,5},{2,6},{3,7},{4,0},{5,1},{6,2},{7,3},{8,12},{9,13},{10,... | collective-permute-start | bytes 1572872 | tf_op jit(solution)/shard_map/ppermute | solution.py:465
  541.2 39.4 %collective-permute-start.60 = (bf16[128,2048]{1,0:T(8,128)(2,1)S(1)}, bf16[128,2048]{1,0:T(8,128)(2,1)S(1)}, u32[]{:S(2)}, u32[]{:S(2)}) collective-permute-start(bf16[128,2048]{1,0:T(8,128)(2,1)S(1)} %get-tuple-element.260), channel_id=1, source_target_pairs={{0,6},{1,7},{2,4},{3,5},{4,2},{5,3},{6,0},{7,1},{8,14},{9,15},{10,... | collective-permute-start | bytes 1572872 | tf_op jit(solution)/shard_map/ppermute | solution.py:465
  563.1 17.4 %collective-permute-start.57 = (bf16[128,2048]{1,0:T(8,128)(2,1)S(1)}, bf16[128,2048]{1,0:T(8,128)(2,1)S(1)}, u32[]{:S(2)}, u32[]{:S(2)}) collective-permute-start(bf16[128,2048]{1,0:T(8,128)(2,1)S(1)} %get-tuple-element.270), channel_id=1, source_target_pairs={{0,6},{1,7},{2,4},{3,5},{4,2},{5,3},{6,0},{7,1},{8,14},{9,15},{10,... | collective-permute-start | bytes 1572872 | tf_op jit(solution)/shard_map/ppermute | solution.py:465
  582.3 8.3 %collective-permute-start.62 = (f32[8,512]{1,0:T(8,128)S(1)}, f32[8,512]{1,0:T(8,128)S(1)}, u32[]{:S(2)}, u32[]{:S(2)}) collective-permute-start(f32[8,512]{1,0:T(8,128)S(1)} %get-tuple-element.342), channel_id=1, source_target_pairs={{0,16},{8,24},{16,0},{24,8},{1,17},{9,25},{17,1},{25,9},{2,18},{10... | collective-permute-start | bytes 49160 | tf_op jit(solution)/shard_map/ppermute | solution.py:522
  582.9 7.7 %collective-permute-start.63 = (f32[8,512]{1,0:T(8,128)S(1)}, f32[8,512]{1,0:T(8,128)S(1)}, u32[]{:S(2)}, u32[]{:S(2)}) collective-permute-start(f32[8,512]{1,0:T(8,128)S(1)} %get-tuple-element.343), channel_id=1, source_target_pairs={{0,24},{8,0},{16,8},{24,16},{1,25},{9,1},{17,9},{25,17},{2,26},{10... | collective-permute-start | bytes 49160 | tf_op jit(solution)/shard_map/ppermute | solution.py:522
  (158 other events, 1554.4 us)
Sparse Core Ops, SparseCore 0:
  19.3 78.9 all-gather.3
  99.8 79.2 all-gather.5
  180.7 79.2 all-gather.7
  288.1 74.0 reduce-scatter.3
  364.9 77.2 reduce-scatter.5
  517.0 75.1 reduce-scatter.7

commit v4 on v3

--- a/solution.py
+++ b/solution.py
@@ -793,7 +793,7 @@
         x_tile,
         lanes,
         planes=3,
-        base=after(grad_four, grad_up),
+        base=grad_four,
     )
     last = grad_four
     grad_four = lax.psum_scatter(grad_four, "row", scatter_dimension=0)

time: 618 us -> 615 us (level)
  waiting for transfers between devices: 193 us -> 175 us
  local copies, waits for them, and re-layouts: 67.3 us -> 75.8 us
  other arithmetic: 60.5 us -> 67.2 us
    ppermute x61, waiting for transfers between devices: 189 us -> 175 us  [flip(): return lax.ppermute(values, 'col', [(i, i ^ bits) for i in range(count)])]
    unnamed x318 -> x316, local copies, waits for them, and re-layouts: 48.2 us -> 54.8 us
  transfers between devices with their start and end apart: 73 -> 73, of which waited for: 28 -> 29; matrix products, arithmetic and copies ran while one was open for 14% -> 16% of each run, Pallas kernels for 33% -> 34%
where the time goes in v4:
time: 615 us; the launch traced here: 608 us
  Pallas kernels  204 us (33%)
  waiting for transfers between devices  175 us (28%)
  local copies, waits for them, and re-layouts  75.8 us (12%)
  other arithmetic  67.2 us (11%)
  starting transfers between devices  65.7 us (11%)
  between operations  20 us (3%)
    ppermute x61, waiting for transfers between devices, flip(): return lax.ppermute(values, 'col', [(i, i ^ bits) for i in range(count)])  175 us
    pallas_call x16, Pallas kernels, product(): pl.pallas_call(functools.partial(product_kernel, make=make, in_count=len(...  61.8 us
    unnamed x316, local copies, waits for them, and re-layouts  54.8 us
    ppermute x61, starting transfers between devices, flip(): return lax.ppermute(values, 'col', [(i, i ^ bits) for i in range(count)])  53.7 us
    pallas_call x4, Pallas kernels, weight_grad(): pl.pallas_call(functools.partial(weight_kernel, x_count=len(xs), y_count=...  44 us
    pallas_call x2, Pallas kernels, attention_back(): pl.pallas_call(functools.partial(attend_backward, piece=piece, blk=min(25...  25.6 us
    pallas_call x4, Pallas kernels, expand(): pl.pallas_call(expand_kernel, out_shape=(full, full), grid=(rows // strip...  23.9 us
    pallas_call x2, Pallas kernels, attention(): pl.pallas_call(functools.partial(attend_forward, piece=piece, blk=min(256...  20 us
  transfers between devices with their start and end apart: 73, of which 29 were waited for; matrix products, arithmetic and copies ran while one was open for 16% of the time, Pallas kernels for 34%

profile of v4, /device:TPU:0, one launch (start us, length us, event | category | flops | bytes accessed | tf_op | source)
XLA Modules:
  0.0 607.9 jit_solution(13437453748839925517)
XLA Ops:
  8.0 4.1 collective-permute-start.1
  13.7 2.2 collective-permute-start.2
  20.8 2.5 collective-permute-start.5
  27.1 9.5 %collective-permute-done.5 = bf16[128,2048]{1,0:T(8,128)(2,1)S(1)} collective-permute-done((bf16[128,2048]{1,0:T(8,128)(2,1)S(1)}, bf16[128,2048]{1,0:T(8,128)(2,1)S(1)}, u32[]{:S(2)}, u32[]{:S(2)}) %collective-permute-start.5) | collective-permute-done | bytes 524320 | tf_op jit(solution)/shard_map/ppermute | solution.py:465
  36.6 9.2 %collective-permute-done.4 = bf16[128,2048]{1,0:T(8,128)(2,1)S(1)} collective-permute-done((bf16[128,2048]{1,0:T(8,128)(2,1)S(1)}, bf16[128,2048]{1,0:T(8,128)(2,1)S(1)}, u32[]{:S(2)}, u32[]{:S(2)}) %collective-permute-start.4) | collective-permute-done | bytes 524320 | tf_op jit(solution)/shard_map/ppermute | solution.py:465
  49.4 12.2 %collective-permute-done.8 = bf16[128,2048]{1,0:T(8,128)(2,1)S(1)} collective-permute-done((bf16[128,2048]{1,0:T(8,128)(2,1)S(1)}, bf16[128,2048]{1,0:T(8,128)(2,1)S(1)}, u32[]{:S(2)}, u32[]{:S(2)}) %collective-permute-start.8) | collective-permute-done | bytes 524320 | tf_op jit(solution)/shard_map/ppermute | solution.py:465
  61.6 10.3 %collective-permute-done.7 = bf16[128,2048]{1,0:T(8,128)(2,1)S(1)} collective-permute-done((bf16[128,2048]{1,0:T(8,128)(2,1)S(1)}, bf16[128,2048]{1,0:T(8,128)(2,1)S(1)}, u32[]{:S(2)}, u32[]{:S(2)}) %collective-permute-start.7) | collective-permute-done | bytes 524320 | tf_op jit(solution)/shard_map/ppermute | solution.py:465
  75.5 12.2 %collective-permute-done.11 = bf16[128,2048]{1,0:T(8,128)(2,1)S(1)} collective-permute-done((bf16[128,2048]{1,0:T(8,128)(2,1)S(1)}, bf16[128,2048]{1,0:T(8,128)(2,1)S(1)}, u32[]{:S(2)}, u32[]{:S(2)}) %collective-permute-start.11) | collective-permute-done | bytes 524320 | tf_op jit(solution)/shard_map/ppermute | solution.py:465
  87.8 10.2 %collective-permute-done.10 = bf16[128,2048]{1,0:T(8,128)(2,1)S(1)} collective-permute-done((bf16[128,2048]{1,0:T(8,128)(2,1)S(1)}, bf16[128,2048]{1,0:T(8,128)(2,1)S(1)}, u32[]{:S(2)}, u32[]{:S(2)}) %collective-permute-start.10) | collective-permute-done | bytes 524320 | tf_op jit(solution)/shard_map/ppermute | solution.py:465
  111.2 5.6 project.2
  118.5 10.2 %attend_forward.2 = (bf16[1024,256]{1,0:T(8,128)(2,1)S(1)}, bf16[1024,256]{1,0:T(8,128)(2,1)S(1)}, bf16[1024,256]{1,0:T(8,128)(2,1)S(1)}, bf16[1024,256]{1,0:T(8,128)(2,1)S(1)}, f32[4,8,1024]{2,1,0:T(8,128)S(1)}) custom-call(s32[8]{0:T(128)S(1)} %shift-right-arithmetic_add_fusion.spot_ref, f32[3,1024,256]{2,1,0:T(8,128)} %bitcast.203, ...), custom_call_target="tpu_custom_call" | custom-call | flops 1000 | bytes 1000 | tf_op jit(solution)/shard_map/attend_forward/pallas_call | solution.py:183
  135.7 2.6 mix.5
  147.5 5.4 project.3
  154.6 9.8 %attend_forward.3 = (bf16[1024,256]{1,0:T(8,128)(2,1)S(1)}, bf16[1024,256]{1,0:T(8,128)(2,1)S(1)}, bf16[1024,256]{1,0:T(8,128)(2,1)S(1)}, bf16[1024,256]{1,0:T(8,128)(2,1)S(1)}, f32[4,8,1024]{2,1,0:T(8,128)S(1)}) custom-call(s32[8]{0:T(128)S(1)} %shift-right-arithmetic_add_fusion.spot_ref, f32[3,1024,256]{2,1,0:T(8,128)} %bitcast.200, ...), custom_call_target="tpu_custom_call" | custom-call | flops 1000 | bytes 1000 | tf_op jit(solution)/shard_map/attend_forward/pallas_call | solution.py:183
  169.2 2.8 mix.6
  177.4 10.6 %collective-permute-done.23 = bf16[128,2048]{1,0:T(8,128)(2,1)} collective-permute-done((bf16[128,2048]{1,0:T(8,128)(2,1)}, bf16[128,2048]{1,0:T(8,128)(2,1)}, u32[]{:S(2)}, u32[]{:S(2)}) %collective-permute-start.23) | collective-permute-done | bytes 524320 | tf_op jit(solution)/shard_map/ppermute | solution.py:465
  188.0 10.7 %collective-permute-done.22 = bf16[128,2048]{1,0:T(8,128)(2,1)} collective-permute-done((bf16[128,2048]{1,0:T(8,128)(2,1)}, bf16[128,2048]{1,0:T(8,128)(2,1)}, u32[]{:S(2)}, u32[]{:S(2)}) %collective-permute-start.22) | collective-permute-done | bytes 524320 | tf_op jit(solution)/shard_map/ppermute | solution.py:465
  200.7 4.2 mix.7
  214.9 6.0 collective-permute-done.26
  220.8 11.4 %collective-permute-done.27 = bf16[128,2048]{1,0:T(8,128)(2,1)} collective-permute-done((bf16[128,2048]{1,0:T(8,128)(2,1)}, bf16[128,2048]{1,0:T(8,128)(2,1)}, u32[]{:S(2)}, u32[]{:S(2)}) %collective-permute-start.27) | collective-permute-done | bytes 524320 | tf_op jit(solution)/shard_map/ppermute | solution.py:465
  232.2 2.2 fusion.64
  239.8 5.9 expand.4
  247.7 5.9 expand.5
  253.7 6.4 %collective-permute-done.30 = bf16[128,2048]{1,0:T(8,128)(2,1)S(1)} collective-permute-done((bf16[128,2048]{1,0:T(8,128)(2,1)S(1)}, bf16[128,2048]{1,0:T(8,128)(2,1)S(1)}, u32[]{:S(2)}, u32[]{:S(2)}) %collective-permute-start.30) | collective-permute-done | bytes 524320 | tf_op jit(solution)/shard_map/ppermute | solution.py:465
  261.2 5.9 expand.6
  268.1 6.2 %expand.7 = (bf16[512,1024]{1,0:T(8,128)(2,1)S(1)}, bf16[512,1024]{1,0:T(8,128)(2,1)S(1)}) custom-call(bf16[512,2048]{1,0:T(8,128)(2,1)S(1)} %collective-permute-done.32.x_ref.refs_3_, bf16[2048,1024]{1,0:T(8,128)(2,1)} %all-gather.6.cloned.1.call-done.w_ref.refs_1_), custom_call_target="tpu_custom_call" | custom-call | flops 1000 | bytes 1000 | tf_op jit(solution)/shard_map/expand/pallas_call | solution.py:233
  276.6 14.4 %weight_grad.4 = bf16[4,1024,512]{2,1,0:T(8,128)(2,1)} custom-call(bf16[512,1024]{1,0:T(8,128)(2,1)S(1)} %copy-done.52, bf16[512,1024]{1,0:T(8,128)(2,1)S(1)} %copy-done.57, bf16[512,1024]{1,0:T(8,128)(2,1)S(1)} %get-tuple-element.237.refs_2_.refs_0_, bf16[512,1024]{1,0:T(8,128)(2,1)S(1)} %get-tuple-element.223.refs_3_.refs_0_, ...), custom_call_target="tpu_custom_call" | custom-call | flops 1000 | bytes 1000 | tf_op jit(solution)/shard_map/weight_grad/pallas_call | solution.py:442
  293.2 2.3 copy-done.11
  295.5 5.7 scaled_product.5.refs_0_.refs_5_
  301.3 3.1 unexpand.4
  304.6 3.3 scaled_product.4.refs_0_.refs_4_
  308.7 3.3 unexpand.5
  315.6 3.3 scaled_product.7.refs_0_.refs_7_
  318.9 3.1 unexpand.6
  322.0 4.8 collective-permute-done.36
  326.9 11.1 %collective-permute-done.37 = bf16[128,2048]{1,0:T(8,128)(2,1)S(1)} collective-permute-done((bf16[128,2048]{1,0:T(8,128)(2,1)S(1)}, bf16[128,2048]{1,0:T(8,128)(2,1)S(1)}, u32[]{:S(2)}, u32[]{:S(2)}) %collective-permute-start.37) | collective-permute-done | bytes 524320 | tf_op jit(solution)/shard_map/ppermute | solution.py:465
  338.0 3.3 scaled_product.6.refs_0_.refs_6_
  345.1 3.3 unexpand.7
  348.5 2.3 pad_maximum_fusion.2
  354.3 12.7 %weight_grad.5 = bf16[2048,1024]{1,0:T(8,128)(2,1)} custom-call(bf16[512,2048]{1,0:T(8,128)(2,1)} %constant_dynamic-update-slice_fusion.8.x_ref.refs_0_, bf16[512,2048]{1,0:T(8,128)(2,1)} %collective-permute-done.24.x_ref.refs_1_, bf16[512,2048]{1,0:T(8,128)(2,1)} %copy-done.33, bf16[512,2048]{1,0:T(8,128)(2,1)} %copy-done.37, ...), custom_call_target="tpu_custom_call" | custom-call | flops 1000 | bytes 1000 | tf_op jit(solution)/shard_map/weight_grad/pallas_call | solution.py:442
  372.0 4.4 contract.5
  376.4 5.5 contract.4
  381.9 18.0 %collective-permute-done.40 = bf16[256,2048]{1,0:T(8,128)(2,1)} collective-permute-done((bf16[256,2048]{1,0:T(8,128)(2,1)}, bf16[256,2048]{1,0:T(8,128)(2,1)}, u32[]{:S(2)}, u32[]{:S(2)}) %collective-permute-start.40) | collective-permute-done | bytes 1048608 | tf_op jit(solution)/shard_map/ppermute | solution.py:465
  406.9 2.5 fusion.62
  414.4 12.9 %attend_backward.2.refs_4_.refs_0_ = bf16[3,1024,256]{2,1,0:T(8,128)(2,1)S(1)} custom-call(s32[8]{0:T(128)S(1)} %shift-right-arithmetic_add_fusion.spot_ref, bf16[1024,256]{1,0:T(8,128)(2,1)S(1)} %copy-done.76, bf16[1024,256]{1,0:T(8,128)(2,1)S(1)} %copy-done.78, bf16[1024,256]{1,0:T(8,128)(2,1)S(1)} %copy-done.80, bf16[1024,256]{1,0:T(8,128)(2,1)S(1)} %bitcast.207, ...), custom_call_target="tpu_custom_call" | custom-call | flops 1000 | bytes 1000 | tf_op jit(solution)/shard_map/attend_backward/pallas_call | solution.py:202
  427.3 5.5 contract.6
  436.0 5.1 contract.7
  455.6 12.7 %attend_backward.3.refs_5_.refs_0_ = bf16[3,1024,256]{2,1,0:T(8,128)(2,1)S(1)} custom-call(s32[8]{0:T(128)S(1)} %shift-right-arithmetic_add_fusion.spot_ref, bf16[1024,256]{1,0:T(8,128)(2,1)S(1)} %copy-done.70, bf16[1024,256]{1,0:T(8,128)(2,1)S(1)} %copy-done.72, bf16[1024,256]{1,0:T(8,128)(2,1)S(1)} %copy-done.74, bf16[1024,256]{1,0:T(8,128)(2,1)S(1)} %bitcast.206, ...), custom_call_target="tpu_custom_call" | custom-call | flops 1000 | bytes 1000 | tf_op jit(solution)/shard_map/attend_backward/pallas_call | solution.py:202
  468.5 5.9 weight_grad.6.refs_6_
  475.4 11.0 %weight_grad.7 = bf16[4,4,512,256]{3,2,1,0:T(8,128)(2,1)} custom-call(bf16[512,2048]{1,0:T(8,128)(2,1)S(1)} %copy-done.29, bf16[512,2048]{1,0:T(8,128)(2,1)} %collective-permute-done.12.refs_1_, bf16[512,2048]{1,0:T(8,128)(2,1)} %copy-done.27, bf16[512,2048]{1,0:T(8,128)(2,1)} %collective-permute-done.20.refs_1_.refs_3_, ...), custom_call_target="tpu_custom_call", output_to_operand_aliasing={{}: (6, {})} | custom-call | flops 1000 | bytes 1000 | tf_op jit(solution)/shard_map/weight_grad/pallas_call | solution.py:442
  486.4 12.7 %collective-permute-done.47 = bf16[256,2048]{1,0:T(8,128)(2,1)} collective-permute-done((bf16[256,2048]{1,0:T(8,128)(2,1)}, bf16[256,2048]{1,0:T(8,128)(2,1)}, u32[]{:S(2)}, u32[]{:S(2)}) %collective-permute-start.47) | collective-permute-done | bytes 1048608 | tf_op jit(solution)/shard_map/ppermute | solution.py:465
  501.3 3.6 unproject.6
  504.9 3.6 unproject.4
  511.6 5.1 unproject.7
  521.0 2.8 bitcast_convert_fusion.2
  531.8 5.1 unproject.5
  542.0 2.7 collective-permute-done.57
  544.7 4.0 fusion
  550.5 4.5 broadcast_multiply_fusion
  555.1 9.7 %collective-permute-done.59 = bf16[128,2048]{1,0:T(8,128)(2,1)S(1)} collective-permute-done((bf16[128,2048]{1,0:T(8,128)(2,1)S(1)}, bf16[128,2048]{1,0:T(8,128)(2,1)S(1)}, u32[]{:S(2)}, u32[]{:S(2)}) %collective-permute-start.59) | collective-permute-done | bytes 524320 | tf_op jit(solution)/shard_map/ppermute | solution.py:465
  566.2 3.0 fusion.34
  570.0 3.2 collective-permute-start.63
  574.7 5.5 fusion.50
  581.5 5.4 fusion.49
  (553 shorter events, 173.2 us)
Async XLA Ops:
  7.2 101.8 %all-gather.4.cloned.1.call-start = ((), (), s32[]{:S(2)}) async-start(), calls=%async_computation.3 | async-start | bytes 5242880 | tf_op jit(solution)/shard_map/all_gather | solution.py:571
  8.0 17.2 %collective-permute-start.1 = (bf16[4,512]{1,0:T(4,128)(2,1)S(1)}, bf16[4,512]{1,0:T(4,128)(2,1)S(1)}, u32[]{:S(2)}, u32[]{:S(2)}) collective-permute-start(bf16[4,512]{1,0:T(4,128)(2,1)S(1)} %pad_maximum_fusion.13), channel_id=1, source_target_pairs={{0,16},{8,24},{16,0},{24,8},{1,17},{9,25},{17,1},{25,9},{2,18},{10... | collective-permute-start | bytes 12296 | tf_op jit(solution)/shard_map/ppermute | solution.py:522
  12.2 12.5 %collective-permute-start = (bf16[4,512]{1,0:T(4,128)(2,1)S(1)}, bf16[4,512]{1,0:T(4,128)(2,1)S(1)}, u32[]{:S(2)}, u32[]{:S(2)}) collective-permute-start(bf16[4,512]{1,0:T(4,128)(2,1)S(1)} %pad_maximum_fusion.13), channel_id=1, source_target_pairs={{0,8},{8,16},{16,24},{24,0},{1,9},{9,17},{17,25},{25,1},{2,10},{10... | collective-permute-start | bytes 12296 | tf_op jit(solution)/shard_map/ppermute | solution.py:522
  13.7 11.6 %collective-permute-start.2 = (bf16[4,512]{1,0:T(4,128)(2,1)S(1)}, bf16[4,512]{1,0:T(4,128)(2,1)S(1)}, u32[]{:S(2)}, u32[]{:S(2)}) collective-permute-start(bf16[4,512]{1,0:T(4,128)(2,1)S(1)} %pad_maximum_fusion.13), channel_id=1, source_target_pairs={{0,24},{8,0},{16,8},{24,16},{1,25},{9,1},{17,9},{25,17},{2,26},{10... | collective-permute-start | bytes 12296 | tf_op jit(solution)/shard_map/ppermute | solution.py:522
  19.2 195.7 %all-gather.6.cloned.1.call-start = ((), (), s32[]{:S(2)}) async-start(), calls=%async_computation.4 | async-start | bytes 5242880 | tf_op jit(solution)/shard_map/all_gather | solution.py:574
  20.8 15.8 %collective-permute-start.5 = (bf16[128,2048]{1,0:T(8,128)(2,1)S(1)}, bf16[128,2048]{1,0:T(8,128)(2,1)S(1)}, u32[]{:S(2)}, u32[]{:S(2)}) collective-permute-start(bf16[128,2048]{1,0:T(8,128)(2,1)S(1)} %get-tuple-element.333), channel_id=1, source_target_pairs={{0,6},{1,7},{2,4},{3,5},{4,2},{5,3},{6,0},{7,1},{8,14},{9,15},{10,... | collective-permute-start | bytes 1572872 | tf_op jit(solution)/shard_map/ppermute | solution.py:465
  23.3 22.5 %collective-permute-start.4 = (bf16[128,2048]{1,0:T(8,128)(2,1)S(1)}, bf16[128,2048]{1,0:T(8,128)(2,1)S(1)}, u32[]{:S(2)}, u32[]{:S(2)}) collective-permute-start(bf16[128,2048]{1,0:T(8,128)(2,1)S(1)} %get-tuple-element.333), channel_id=1, source_target_pairs={{0,4},{1,5},{2,6},{3,7},{4,0},{5,1},{6,2},{7,3},{8,12},{9,13},{10,... | collective-permute-start | bytes 1572872 | tf_op jit(solution)/shard_map/ppermute | solution.py:465
  24.6 21.3 %collective-permute-start.3 = (bf16[128,2048]{1,0:T(8,128)(2,1)S(1)}, bf16[128,2048]{1,0:T(8,128)(2,1)S(1)}, u32[]{:S(2)}, u32[]{:S(2)}) collective-permute-start(bf16[128,2048]{1,0:T(8,128)(2,1)S(1)} %get-tuple-element.333), channel_id=1, source_target_pairs={{0,2},{1,3},{2,0},{3,1},{4,6},{5,7},{6,4},{7,5},{8,10},{9,11},{10,... | collective-permute-start | bytes 1572872 | tf_op jit(solution)/shard_map/ppermute | solution.py:465
  45.9 15.7 %collective-permute-start.8 = (bf16[128,2048]{1,0:T(8,128)(2,1)S(1)}, bf16[128,2048]{1,0:T(8,128)(2,1)S(1)}, u32[]{:S(2)}, u32[]{:S(2)}) collective-permute-start(bf16[128,2048]{1,0:T(8,128)(2,1)S(1)} %get-tuple-element.155), channel_id=1, source_target_pairs={{0,6},{1,7},{2,4},{3,5},{4,2},{5,3},{6,0},{7,1},{8,14},{9,15},{10,... | collective-permute-start | bytes 1572872 | tf_op jit(solution)/shard_map/ppermute | solution.py:465
  47.6 24.3 %collective-permute-start.7 = (bf16[128,2048]{1,0:T(8,128)(2,1)S(1)}, bf16[128,2048]{1,0:T(8,128)(2,1)S(1)}, u32[]{:S(2)}, u32[]{:S(2)}) collective-permute-start(bf16[128,2048]{1,0:T(8,128)(2,1)S(1)} %get-tuple-element.155), channel_id=1, source_target_pairs={{0,4},{1,5},{2,6},{3,7},{4,0},{5,1},{6,2},{7,3},{8,12},{9,13},{10,... | collective-permute-start | bytes 1572872 | tf_op jit(solution)/shard_map/ppermute | solution.py:465
  48.9 23.2 %collective-permute-start.6 = (bf16[128,2048]{1,0:T(8,128)(2,1)S(1)}, bf16[128,2048]{1,0:T(8,128)(2,1)S(1)}, u32[]{:S(2)}, u32[]{:S(2)}) collective-permute-start(bf16[128,2048]{1,0:T(8,128)(2,1)S(1)} %get-tuple-element.155), channel_id=1, source_target_pairs={{0,2},{1,3},{2,0},{3,1},{4,6},{5,7},{6,4},{7,5},{8,10},{9,11},{10,... | collective-permute-start | bytes 1572872 | tf_op jit(solution)/shard_map/ppermute | solution.py:465
  72.1 15.7 %collective-permute-start.11 = (bf16[128,2048]{1,0:T(8,128)(2,1)S(1)}, bf16[128,2048]{1,0:T(8,128)(2,1)S(1)}, u32[]{:S(2)}, u32[]{:S(2)}) collective-permute-start(bf16[128,2048]{1,0:T(8,128)(2,1)S(1)} %get-tuple-element.154), channel_id=1, source_target_pairs={{0,6},{1,7},{2,4},{3,5},{4,2},{5,3},{6,0},{7,1},{8,14},{9,15},{10,... | collective-permute-start | bytes 1572872 | tf_op jit(solution)/shard_map/ppermute | solution.py:465
  73.5 24.6 %collective-permute-start.10 = (bf16[128,2048]{1,0:T(8,128)(2,1)S(1)}, bf16[128,2048]{1,0:T(8,128)(2,1)S(1)}, u32[]{:S(2)}, u32[]{:S(2)}) collective-permute-start(bf16[128,2048]{1,0:T(8,128)(2,1)S(1)} %get-tuple-element.154), channel_id=1, source_target_pairs={{0,4},{1,5},{2,6},{3,7},{4,0},{5,1},{6,2},{7,3},{8,12},{9,13},{10,... | collective-permute-start | bytes 1572872 | tf_op jit(solution)/shard_map/ppermute | solution.py:465
  74.9 23.9 %collective-permute-start.9 = (bf16[128,2048]{1,0:T(8,128)(2,1)S(1)}, bf16[128,2048]{1,0:T(8,128)(2,1)}, u32[]{:S(2)}, u32[]{:S(2)}) collective-permute-start(bf16[128,2048]{1,0:T(8,128)(2,1)S(1)} %get-tuple-element.154), channel_id=1, source_target_pairs={{0,2},{1,3},{2,0},{3,1},{4,6},{5,7},{6,4},{7,5},{8,10},{9,11},{10,... | collective-permute-start | bytes 1572872 | tf_op jit(solution)/shard_map/ppermute | solution.py:465
  99.1 9.9 %collective-permute-start.12 = (bf16[512,2048]{1,0:T(8,128)(2,1)S(1)}, bf16[512,2048]{1,0:T(8,128)(2,1)}, u32[]{:S(2)}, u32[]{:S(2)}) collective-permute-start(bf16[512,2048]{1,0:T(8,128)(2,1)S(1)} %constant_dynamic-update-slice_fusion.refs_0_), channel_id=1, source_target_pairs={{0,1},{1,0},{2,3},{3,2},{4,5},{5,4},{6,7},{7,6},{8,9},{9,8},{10,11... | collective-permute-start | bytes 6291464 | tf_op jit(solution)/shard_map/ppermute | solution.py:465
  99.3 192.8 %all-gather.8.cloned.1.call-start = ((), (), s32[]{:S(2)}) async-start(), calls=%async_computation.5 | async-start | bytes 5242880 | tf_op jit(solution)/shard_map/all_gather | solution.py:575
  100.7 31.0 %collective-permute-start.17 = (bf16[128,2048]{1,0:T(8,128)(2,1)}, bf16[128,2048]{1,0:T(8,128)(2,1)}, u32[]{:S(2)}, u32[]{:S(2)}) collective-permute-start(bf16[128,2048]{1,0:T(8,128)(2,1)} %get-tuple-element.166), channel_id=1, source_target_pairs={{0,2},{1,3},{2,0},{3,1},{4,6},{5,7},{6,4},{7,5},{8,10},{9,11},{10,... | collective-permute-start | bytes 1572872 | tf_op jit(solution)/shard_map/ppermute | solution.py:465
  102.8 29.9 %collective-permute-start.18 = (bf16[128,2048]{1,0:T(8,128)(2,1)}, bf16[128,2048]{1,0:T(8,128)(2,1)}, u32[]{:S(2)}, u32[]{:S(2)}) collective-permute-start(bf16[128,2048]{1,0:T(8,128)(2,1)} %get-tuple-element.166), channel_id=1, source_target_pairs={{0,4},{1,5},{2,6},{3,7},{4,0},{5,1},{6,2},{7,3},{8,12},{9,13},{10,... | collective-permute-start | bytes 1572872 | tf_op jit(solution)/shard_map/ppermute | solution.py:465
  107.2 26.6 %collective-permute-start.19 = (bf16[128,2048]{1,0:T(8,128)(2,1)}, bf16[128,2048]{1,0:T(8,128)(2,1)}, u32[]{:S(2)}, u32[]{:S(2)}) collective-permute-start(bf16[128,2048]{1,0:T(8,128)(2,1)} %get-tuple-element.166), channel_id=1, source_target_pairs={{0,6},{1,7},{2,4},{3,5},{4,2},{5,3},{6,0},{7,1},{8,14},{9,15},{10,... | collective-permute-start | bytes 1572872 | tf_op jit(solution)/shard_map/ppermute | solution.py:465
  134.9 10.4 %collective-permute-start.20 = (bf16[512,2048]{1,0:T(8,128)(2,1)S(1)}, bf16[512,2048]{1,0:T(8,128)(2,1)}, u32[]{:S(2)}, u32[]{:S(2)}) collective-permute-start(bf16[512,2048]{1,0:T(8,128)(2,1)S(1)} %constant_dynamic-update-slice_fusion.4.refs_0_.refs_2_), channel_id=1, source_target_pairs={{0,1},{1,0},{2,3},{3,2},{4,5},{5,4},{6,7},{7,6},{8,9},{9,8},{10,11... | collective-permute-start | bytes 6291464 | tf_op jit(solution)/shard_map/ppermute | solution.py:465
  138.3 26.1 %collective-permute-start.14 = (bf16[128,2048]{1,0:T(8,128)(2,1)}, bf16[128,2048]{1,0:T(8,128)(2,1)}, u32[]{:S(2)}, u32[]{:S(2)}) collective-permute-start(bf16[128,2048]{1,0:T(8,128)(2,1)} %get-tuple-element.163), channel_id=1, source_target_pairs={{0,2},{1,3},{2,0},{3,1},{4,6},{5,7},{6,4},{7,5},{8,10},{9,11},{10,... | collective-permute-start | bytes 1572872 | tf_op jit(solution)/shard_map/ppermute | solution.py:465
  139.9 25.2 %collective-permute-start.15 = (bf16[128,2048]{1,0:T(8,128)(2,1)}, bf16[128,2048]{1,0:T(8,128)(2,1)}, u32[]{:S(2)}, u32[]{:S(2)}) collective-permute-start(bf16[128,2048]{1,0:T(8,128)(2,1)} %get-tuple-element.164), channel_id=1, source_target_pairs={{0,4},{1,5},{2,6},{3,7},{4,0},{5,1},{6,2},{7,3},{8,12},{9,13},{10,... | collective-permute-start | bytes 1572872 | tf_op jit(solution)/shard_map/ppermute | solution.py:465
  140.3 24.8 %collective-permute-start.16 = (bf16[128,2048]{1,0:T(8,128)(2,1)}, bf16[128,2048]{1,0:T(8,128)(2,1)}, u32[]{:S(2)}, u32[]{:S(2)}) collective-permute-start(bf16[128,2048]{1,0:T(8,128)(2,1)} %get-tuple-element.165), channel_id=1, source_target_pairs={{0,6},{1,7},{2,4},{3,5},{4,2},{5,3},{6,0},{7,1},{8,14},{9,15},{10,... | collective-permute-start | bytes 1572872 | tf_op jit(solution)/shard_map/ppermute | solution.py:465
  171.9 26.9 %collective-permute-start.25 = (bf16[512,2048]{1,0:T(8,128)(2,1)}, bf16[512,2048]{1,0:T(8,128)(2,1)}, u32[]{:S(2)}, u32[]{:S(2)}) collective-permute-start(bf16[512,2048]{1,0:T(8,128)(2,1)} %mix.6), channel_id=1, source_target_pairs={{0,1},{1,0},{2,3},{3,2},{4,5},{5,4},{6,7},{7,6},{8,9},{9,8},{10,11... | collective-permute-start | bytes 6291464 | tf_op jit(solution)/shard_map/ppermute | solution.py:465
  171.9 16.1 %collective-permute-start.23 = (bf16[128,2048]{1,0:T(8,128)(2,1)}, bf16[128,2048]{1,0:T(8,128)(2,1)}, u32[]{:S(2)}, u32[]{:S(2)}) collective-permute-start(bf16[128,2048]{1,0:T(8,128)(2,1)} %add_convert_fusion.1), channel_id=1, source_target_pairs={{0,6},{1,7},{2,4},{3,5},{4,2},{5,3},{6,0},{7,1},{8,14},{9,15},{10,... | collective-permute-start | bytes 1572872 | tf_op jit(solution)/shard_map/ppermute | solution.py:465
  173.4 25.3 %collective-permute-start.22 = (bf16[128,2048]{1,0:T(8,128)(2,1)}, bf16[128,2048]{1,0:T(8,128)(2,1)}, u32[]{:S(2)}, u32[]{:S(2)}) collective-permute-start(bf16[128,2048]{1,0:T(8,128)(2,1)} %add_convert_fusion.1), channel_id=1, source_target_pairs={{0,4},{1,5},{2,6},{3,7},{4,0},{5,1},{6,2},{7,3},{8,12},{9,13},{10,... | collective-permute-start | bytes 1572872 | tf_op jit(solution)/shard_map/ppermute | solution.py:465
  174.9 24.0 %collective-permute-start.21 = (bf16[128,2048]{1,0:T(8,128)(2,1)}, bf16[128,2048]{1,0:T(8,128)(2,1)}, u32[]{:S(2)}, u32[]{:S(2)}) collective-permute-start(bf16[128,2048]{1,0:T(8,128)(2,1)} %add_convert_fusion.1), channel_id=1, source_target_pairs={{0,2},{1,3},{2,0},{3,1},{4,6},{5,7},{6,4},{7,5},{8,10},{9,11},{10,... | collective-permute-start | bytes 1572872 | tf_op jit(solution)/shard_map/ppermute | solution.py:465
  175.5 266.5 %reduce-scatter.4.cloned.1.call-start = ((), (), s32[]{:S(2)}) async-start(), calls=%async_computation.6 | async-start | bytes 5242880 | tf_op jit(solution)/shard_map/reduce_scatter | solution.py:662
  177.3 98.0 %collective-permute-start.33 = (bf16[512,2048]{1,0:T(8,128)(2,1)S(1)}, bf16[512,2048]{1,0:T(8,128)(2,1)}, u32[]{:S(2)}, u32[]{:S(2)}) collective-permute-start(bf16[512,2048]{1,0:T(8,128)(2,1)S(1)} %pad_maximum_fusion.refs_4_.x_ref.refs_3_), channel_id=1, source_target_pairs={{0,1},{1,0},{2,3},{3,2},{4,5},{5,4},{6,7},{7,6},{8,9},{9,8},{10,11... | collective-permute-start | bytes 6291464 | tf_op jit(solution)/shard_map/ppermute | solution.py:465
  205.7 15.1 %collective-permute-start.26 = (bf16[128,2048]{1,0:T(8,128)(2,1)}, bf16[128,2048]{1,0:T(8,128)(2,1)}, u32[]{:S(2)}, u32[]{:S(2)}) collective-permute-start(bf16[128,2048]{1,0:T(8,128)(2,1)} %get-tuple-element.186), channel_id=1, source_target_pairs={{0,2},{1,3},{2,0},{3,1},{4,6},{5,7},{6,4},{7,5},{8,10},{9,11},{10,... | collective-permute-start | bytes 1572872 | tf_op jit(solution)/shard_map/ppermute | solution.py:465
  207.1 25.1 %collective-permute-start.27 = (bf16[128,2048]{1,0:T(8,128)(2,1)}, bf16[128,2048]{1,0:T(8,128)(2,1)}, u32[]{:S(2)}, u32[]{:S(2)}) collective-permute-start(bf16[128,2048]{1,0:T(8,128)(2,1)} %get-tuple-element.187), channel_id=1, source_target_pairs={{0,4},{1,5},{2,6},{3,7},{4,0},{5,1},{6,2},{7,3},{8,12},{9,13},{10,... | collective-permute-start | bytes 1572872 | tf_op jit(solution)/shard_map/ppermute | solution.py:465
  207.7 24.5 %collective-permute-start.28 = (bf16[128,2048]{1,0:T(8,128)(2,1)}, bf16[128,2048]{1,0:T(8,128)(2,1)}, u32[]{:S(2)}, u32[]{:S(2)}) collective-permute-start(bf16[128,2048]{1,0:T(8,128)(2,1)} %get-tuple-element.188), channel_id=1, source_target_pairs={{0,6},{1,7},{2,4},{3,5},{4,2},{5,3},{6,0},{7,1},{8,14},{9,15},{10,... | collective-permute-start | bytes 1572872 | tf_op jit(solution)/shard_map/ppermute | solution.py:465
  214.9 32.9 %collective-permute-start.24 = (bf16[512,2048]{1,0:T(8,128)(2,1)}, bf16[512,2048]{1,0:T(8,128)(2,1)}, u32[]{:S(2)}, u32[]{:S(2)}) collective-permute-start(bf16[512,2048]{1,0:T(8,128)(2,1)} %constant_dynamic-update-slice_fusion.8.x_ref.refs_0_), channel_id=1, source_target_pairs={{0,1},{1,0},{2,3},{3,2},{4,5},{5,4},{6,7},{7,6},{8,9},{9,8},{10,11... | collective-permute-start | bytes 6291464 | tf_op jit(solution)/shard_map/ppermute | solution.py:465
  235.0 18.6 %collective-permute-start.31 = (bf16[128,2048]{1,0:T(8,128)(2,1)S(1)}, bf16[128,2048]{1,0:T(8,128)(2,1)S(1)}, u32[]{:S(2)}, u32[]{:S(2)}) collective-permute-start(bf16[128,2048]{1,0:T(8,128)(2,1)S(1)} %add_convert_fusion), channel_id=1, source_target_pairs={{0,6},{1,7},{2,4},{3,5},{4,2},{5,3},{6,0},{7,1},{8,14},{9,15},{10,... | collective-permute-start | bytes 1572872 | tf_op jit(solution)/shard_map/ppermute | solution.py:465
  236.6 23.4 %collective-permute-start.30 = (bf16[128,2048]{1,0:T(8,128)(2,1)S(1)}, bf16[128,2048]{1,0:T(8,128)(2,1)S(1)}, u32[]{:S(2)}, u32[]{:S(2)}) collective-permute-start(bf16[128,2048]{1,0:T(8,128)(2,1)S(1)} %add_convert_fusion), channel_id=1, source_target_pairs={{0,4},{1,5},{2,6},{3,7},{4,0},{5,1},{6,2},{7,3},{8,12},{9,13},{10,... | collective-permute-start | bytes 1572872 | tf_op jit(solution)/shard_map/ppermute | solution.py:465
  237.1 22.9 %collective-permute-start.29 = (bf16[128,2048]{1,0:T(8,128)(2,1)S(1)}, bf16[128,2048]{1,0:T(8,128)(2,1)S(1)}, u32[]{:S(2)}, u32[]{:S(2)}) collective-permute-start(bf16[128,2048]{1,0:T(8,128)(2,1)S(1)} %add_convert_fusion), channel_id=1, source_target_pairs={{0,2},{1,3},{2,0},{3,1},{4,6},{5,7},{6,4},{7,5},{8,10},{9,11},{10,... | collective-permute-start | bytes 1572872 | tf_op jit(solution)/shard_map/ppermute | solution.py:465
  261.2 14.2 %collective-permute-start.34 = (bf16[512,2048]{1,0:T(8,128)(2,1)S(1)}, bf16[512,2048]{1,0:T(8,128)(2,1)S(1)}, u32[]{:S(2)}, u32[]{:S(2)}) collective-permute-start(bf16[512,2048]{1,0:T(8,128)(2,1)S(1)} %constant_dynamic-update-slice_fusion.12.refs_6_.x_ref.refs_3_), channel_id=1, source_target_pairs={{0,1},{1,0},{2,3},{3,2},{4,5},{5,4},{6,7},{7,6},{8,9},{9,8},{10,11... | collective-permute-start | bytes 6291464 | tf_op jit(solution)/shard_map/ppermute | solution.py:465
  292.0 252.6 %reduce-scatter.6.cloned.1.call-start = ((), (), s32[]{:S(2)}) async-start(), calls=%async_computation.7 | async-start | bytes 5242880 | tf_op jit(solution)/shard_map/reduce_scatter | solution.py:731
  312.0 14.9 %collective-permute-start.36 = (bf16[128,2048]{1,0:T(8,128)(2,1)S(1)}, bf16[128,2048]{1,0:T(8,128)(2,1)S(1)}, u32[]{:S(2)}, u32[]{:S(2)}) collective-permute-start(bf16[128,2048]{1,0:T(8,128)(2,1)S(1)} %get-tuple-element.207), channel_id=1, source_target_pairs={{0,2},{1,3},{2,0},{3,1},{4,6},{5,7},{6,4},{7,5},{8,10},{9,11},{10,... | collective-permute-start | bytes 1572872 | tf_op jit(solution)/shard_map/ppermute | solution.py:465
  313.1 24.9 %collective-permute-start.37 = (bf16[128,2048]{1,0:T(8,128)(2,1)S(1)}, bf16[128,2048]{1,0:T(8,128)(2,1)S(1)}, u32[]{:S(2)}, u32[]{:S(2)}) collective-permute-start(bf16[128,2048]{1,0:T(8,128)(2,1)S(1)} %get-tuple-element.208), channel_id=1, source_target_pairs={{0,4},{1,5},{2,6},{3,7},{4,0},{5,1},{6,2},{7,3},{8,12},{9,13},{10,... | collective-permute-start | bytes 1572872 | tf_op jit(solution)/shard_map/ppermute | solution.py:465
  314.5 23.5 %collective-permute-start.38 = (bf16[128,2048]{1,0:T(8,128)(2,1)S(1)}, bf16[128,2048]{1,0:T(8,128)(2,1)S(1)}, u32[]{:S(2)}, u32[]{:S(2)}) collective-permute-start(bf16[128,2048]{1,0:T(8,128)(2,1)S(1)} %get-tuple-element.209), channel_id=1, source_target_pairs={{0,6},{1,7},{2,4},{3,5},{4,2},{5,3},{6,0},{7,1},{8,14},{9,15},{10,... | collective-permute-start | bytes 1572872 | tf_op jit(solution)/shard_map/ppermute | solution.py:465
  350.8 31.1 %collective-permute-start.42 = (bf16[256,2048]{1,0:T(8,128)(2,1)}, bf16[256,2048]{1,0:T(8,128)(2,1)}, u32[]{:S(2)}, u32[]{:S(2)}) collective-permute-start(bf16[256,2048]{1,0:T(8,128)(2,1)} %get-tuple-element.335), channel_id=1, source_target_pairs={{0,6},{1,7},{2,4},{3,5},{4,2},{5,3},{6,0},{7,1},{8,14},{9,15},{10,... | collective-permute-start | bytes 3145736 | tf_op jit(solution)/shard_map/ppermute | solution.py:465
  352.3 47.6 %collective-permute-start.40 = (bf16[256,2048]{1,0:T(8,128)(2,1)}, bf16[256,2048]{1,0:T(8,128)(2,1)}, u32[]{:S(2)}, u32[]{:S(2)}) collective-permute-start(bf16[256,2048]{1,0:T(8,128)(2,1)} %get-tuple-element.336), channel_id=1, source_target_pairs={{0,2},{1,3},{2,0},{3,1},{4,6},{5,7},{6,4},{7,5},{8,10},{9,11},{10,... | collective-permute-start | bytes 3145736 | tf_op jit(solution)/shard_map/ppermute | solution.py:465
  353.7 46.3 %collective-permute-start.41 = (bf16[256,2048]{1,0:T(8,128)(2,1)}, bf16[256,2048]{1,0:T(8,128)(2,1)}, u32[]{:S(2)}, u32[]{:S(2)}) collective-permute-start(bf16[256,2048]{1,0:T(8,128)(2,1)} %get-tuple-element.337), channel_id=1, source_target_pairs={{0,4},{1,5},{2,6},{3,7},{4,0},{5,1},{6,2},{7,3},{8,12},{9,13},{10,... | collective-permute-start | bytes 3145736 | tf_op jit(solution)/shard_map/ppermute | solution.py:465
  367.0 230.4 %reduce-scatter.8.cloned.1.call-start = ((), (), s32[]{:S(2)}) async-start(), calls=%async_computation.8 | async-start | bytes 5242880 | tf_op jit(solution)/shard_map/reduce_scatter | solution.py:799
  403.5 8.7 %collective-permute-start.43 = (bf16[512,2048]{1,0:T(8,128)(2,1)S(1)}, bf16[512,2048]{1,0:T(8,128)(2,1)S(1)}, u32[]{:S(2)}, u32[]{:S(2)}) collective-permute-start(bf16[512,2048]{1,0:T(8,128)(2,1)S(1)} %constant_dynamic-update-slice_fusion.20.refs_0_.refs_2_), channel_id=1, source_target_pairs={{0,1},{1,0},{2,3},{3,2},{4,5},{5,4},{6,7},{7,6},{8,9},{9,8},{10,11... | collective-permute-start | bytes 6291464 | tf_op jit(solution)/shard_map/ppermute | solution.py:465
  403.5 23.7 %collective-permute-start.44 = (bf16[512,2048]{1,0:T(8,128)(2,1)}, bf16[512,2048]{1,0:T(8,128)(2,1)}, u32[]{:S(2)}, u32[]{:S(2)}) collective-permute-start(bf16[512,2048]{1,0:T(8,128)(2,1)} %get-tuple-element.235), channel_id=1, source_target_pairs={{0,1},{1,0},{2,3},{3,2},{4,5},{5,4},{6,7},{7,6},{8,9},{9,8},{10,11... | collective-permute-start | bytes 6291464 | tf_op jit(solution)/shard_map/ppermute | solution.py:465
  404.0 32.0 %collective-permute-start.45 = (bf16[512,2048]{1,0:T(8,128)(2,1)}, bf16[512,2048]{1,0:T(8,128)(2,1)}, u32[]{:S(2)}, u32[]{:S(2)}) collective-permute-start(bf16[512,2048]{1,0:T(8,128)(2,1)} %get-tuple-element.238), channel_id=1, source_target_pairs={{0,1},{1,0},{2,3},{3,2},{4,5},{5,4},{6,7},{7,6},{8,9},{9,8},{10,11... | collective-permute-start | bytes 6291464 | tf_op jit(solution)/shard_map/ppermute | solution.py:465
  409.5 32.4 %collective-permute-start.51 = (bf16[128,2048]{1,0:T(8,128)(2,1)}, bf16[128,2048]{1,0:T(8,128)(2,1)}, u32[]{:S(2)}, u32[]{:S(2)}) collective-permute-start(bf16[128,2048]{1,0:T(8,128)(2,1)} %get-tuple-element.249), channel_id=1, source_target_pairs={{0,6},{1,7},{2,4},{3,5},{4,2},{5,3},{6,0},{7,1},{8,14},{9,15},{10,... | collective-permute-start | bytes 1572872 | tf_op jit(solution)/shard_map/ppermute | solution.py:465
  411.1 30.8 %collective-permute-start.50 = (bf16[128,2048]{1,0:T(8,128)(2,1)}, bf16[128,2048]{1,0:T(8,128)(2,1)}, u32[]{:S(2)}, u32[]{:S(2)}) collective-permute-start(bf16[128,2048]{1,0:T(8,128)(2,1)} %get-tuple-element.249), channel_id=1, source_target_pairs={{0,4},{1,5},{2,6},{3,7},{4,0},{5,1},{6,2},{7,3},{8,12},{9,13},{10,... | collective-permute-start | bytes 1572872 | tf_op jit(solution)/shard_map/ppermute | solution.py:465
  412.2 29.7 %collective-permute-start.49 = (bf16[128,2048]{1,0:T(8,128)(2,1)}, bf16[128,2048]{1,0:T(8,128)(2,1)}, u32[]{:S(2)}, u32[]{:S(2)}) collective-permute-start(bf16[128,2048]{1,0:T(8,128)(2,1)} %get-tuple-element.249), channel_id=1, source_target_pairs={{0,2},{1,3},{2,0},{3,1},{4,6},{5,7},{6,4},{7,5},{8,10},{9,11},{10,... | collective-permute-start | bytes 1572872 | tf_op jit(solution)/shard_map/ppermute | solution.py:465
  449.8 36.6 %collective-permute-start.48 = (bf16[256,2048]{1,0:T(8,128)(2,1)}, bf16[256,2048]{1,0:T(8,128)(2,1)}, u32[]{:S(2)}, u32[]{:S(2)}) collective-permute-start(bf16[256,2048]{1,0:T(8,128)(2,1)} %pad_maximum_fusion.9), channel_id=1, source_target_pairs={{0,6},{1,7},{2,4},{3,5},{4,2},{5,3},{6,0},{7,1},{8,14},{9,15},{10,... | collective-permute-start | bytes 3145736 | tf_op jit(solution)/shard_map/ppermute | solution.py:465
  451.4 47.6 %collective-permute-start.47 = (bf16[256,2048]{1,0:T(8,128)(2,1)}, bf16[256,2048]{1,0:T(8,128)(2,1)}, u32[]{:S(2)}, u32[]{:S(2)}) collective-permute-start(bf16[256,2048]{1,0:T(8,128)(2,1)} %pad_maximum_fusion.8), channel_id=1, source_target_pairs={{0,4},{1,5},{2,6},{3,7},{4,0},{5,1},{6,2},{7,3},{8,12},{9,13},{10,... | collective-permute-start | bytes 3145736 | tf_op jit(solution)/shard_map/ppermute | solution.py:465
  452.4 46.6 %collective-permute-start.46 = (bf16[256,2048]{1,0:T(8,128)(2,1)}, bf16[256,2048]{1,0:T(8,128)(2,1)}, u32[]{:S(2)}, u32[]{:S(2)}) collective-permute-start(bf16[256,2048]{1,0:T(8,128)(2,1)} %pad_maximum_fusion.7), channel_id=1, source_target_pairs={{0,2},{1,3},{2,0},{3,1},{4,6},{5,7},{6,4},{7,5},{8,10},{9,11},{10,... | collective-permute-start | bytes 3145736 | tf_op jit(solution)/shard_map/ppermute | solution.py:465
  508.6 20.4 %collective-permute-start.53 = (bf16[512,2048]{1,0:T(8,128)(2,1)}, bf16[512,2048]{1,0:T(8,128)(2,1)}, u32[]{:S(2)}, u32[]{:S(2)}) collective-permute-start(bf16[512,2048]{1,0:T(8,128)(2,1)} %unproject.4), channel_id=1, source_target_pairs={{0,1},{1,0},{2,3},{3,2},{4,5},{5,4},{6,7},{7,6},{8,9},{9,8},{10,11... | collective-permute-start | bytes 6291464 | tf_op jit(solution)/shard_map/ppermute | solution.py:465
  517.5 21.4 %collective-permute-start.55 = (bf16[128,2048]{1,0:T(8,128)(2,1)}, bf16[128,2048]{1,0:T(8,128)(2,1)}, u32[]{:S(2)}, u32[]{:S(2)}) collective-permute-start(bf16[128,2048]{1,0:T(8,128)(2,1)} %get-tuple-element.266), channel_id=1, source_target_pairs={{0,2},{1,3},{2,0},{3,1},{4,6},{5,7},{6,4},{7,5},{8,10},{9,11},{10,... | collective-permute-start | bytes 1572872 | tf_op jit(solution)/shard_map/ppermute | solution.py:465
  518.6 23.4 %collective-permute-start.56 = (bf16[128,2048]{1,0:T(8,128)(2,1)}, bf16[128,2048]{1,0:T(8,128)(2,1)}, u32[]{:S(2)}, u32[]{:S(2)}) collective-permute-start(bf16[128,2048]{1,0:T(8,128)(2,1)} %get-tuple-element.267), channel_id=1, source_target_pairs={{0,4},{1,5},{2,6},{3,7},{4,0},{5,1},{6,2},{7,3},{8,12},{9,13},{10,... | collective-permute-start | bytes 1572872 | tf_op jit(solution)/shard_map/ppermute | solution.py:465
  519.6 25.0 %collective-permute-start.57 = (bf16[128,2048]{1,0:T(8,128)(2,1)}, bf16[128,2048]{1,0:T(8,128)(2,1)}, u32[]{:S(2)}, u32[]{:S(2)}) collective-permute-start(bf16[128,2048]{1,0:T(8,128)(2,1)} %get-tuple-element.268), channel_id=1, source_target_pairs={{0,6},{1,7},{2,4},{3,5},{4,2},{5,3},{6,0},{7,1},{8,14},{9,15},{10,... | collective-permute-start | bytes 1572872 | tf_op jit(solution)/shard_map/ppermute | solution.py:465
  536.9 18.2 %collective-permute-start.58 = (bf16[128,2048]{1,0:T(8,128)(2,1)}, bf16[128,2048]{1,0:T(8,128)(2,1)S(1)}, u32[]{:S(2)}, u32[]{:S(2)}) collective-permute-start(bf16[128,2048]{1,0:T(8,128)(2,1)} %get-tuple-element.256), channel_id=1, source_target_pairs={{0,2},{1,3},{2,0},{3,1},{4,6},{5,7},{6,4},{7,5},{8,10},{9,11},{10,... | collective-permute-start | bytes 1572872 | tf_op jit(solution)/shard_map/ppermute | solution.py:465
  537.9 26.9 %collective-permute-start.59 = (bf16[128,2048]{1,0:T(8,128)(2,1)S(1)}, bf16[128,2048]{1,0:T(8,128)(2,1)S(1)}, u32[]{:S(2)}, u32[]{:S(2)}) collective-permute-start(bf16[128,2048]{1,0:T(8,128)(2,1)S(1)} %get-tuple-element.257), channel_id=1, source_target_pairs={{0,4},{1,5},{2,6},{3,7},{4,0},{5,1},{6,2},{7,3},{8,12},{9,13},{10,... | collective-permute-start | bytes 1572872 | tf_op jit(solution)/shard_map/ppermute | solution.py:465
  539.0 27.2 %collective-permute-start.60 = (bf16[128,2048]{1,0:T(8,128)(2,1)S(1)}, bf16[128,2048]{1,0:T(8,128)(2,1)S(1)}, u32[]{:S(2)}, u32[]{:S(2)}) collective-permute-start(bf16[128,2048]{1,0:T(8,128)(2,1)S(1)} %get-tuple-element.258), channel_id=1, source_target_pairs={{0,6},{1,7},{2,4},{3,5},{4,2},{5,3},{6,0},{7,1},{8,14},{9,15},{10,... | collective-permute-start | bytes 1572872 | tf_op jit(solution)/shard_map/ppermute | solution.py:465
  569.3 17.7 %collective-permute-start.61 = (f32[8,512]{1,0:T(8,128)S(1)}, f32[8,512]{1,0:T(8,128)S(1)}, u32[]{:S(2)}, u32[]{:S(2)}) collective-permute-start(f32[8,512]{1,0:T(8,128)S(1)} %get-tuple-element.339), channel_id=1, source_target_pairs={{0,8},{8,16},{16,24},{24,0},{1,9},{9,17},{17,25},{25,1},{2,10},{10... | collective-permute-start | bytes 49160 | tf_op jit(solution)/shard_map/ppermute | solution.py:522
  569.7 17.3 %collective-permute-start.62 = (f32[8,512]{1,0:T(8,128)S(1)}, f32[8,512]{1,0:T(8,128)S(1)}, u32[]{:S(2)}, u32[]{:S(2)}) collective-permute-start(f32[8,512]{1,0:T(8,128)S(1)} %get-tuple-element.340), channel_id=1, source_target_pairs={{0,16},{8,24},{16,0},{24,8},{1,17},{9,25},{17,1},{25,9},{2,18},{10... | collective-permute-start | bytes 49160 | tf_op jit(solution)/shard_map/ppermute | solution.py:522
  570.0 17.0 %collective-permute-start.63 = (f32[8,512]{1,0:T(8,128)S(1)}, f32[8,512]{1,0:T(8,128)S(1)}, u32[]{:S(2)}, u32[]{:S(2)}) collective-permute-start(f32[8,512]{1,0:T(8,128)S(1)} %get-tuple-element.341), channel_id=1, source_target_pairs={{0,24},{8,0},{16,8},{24,16},{1,25},{9,1},{17,9},{25,17},{2,26},{10... | collective-permute-start | bytes 49160 | tf_op jit(solution)/shard_map/ppermute | solution.py:522
  (156 other events, 1544.1 us)
Sparse Core Ops, SparseCore 0:
  19.3 78.9 all-gather.3
  99.8 79.2 all-gather.5
  180.7 79.2 all-gather.7
  292.2 74.0 reduce-scatter.3
  368.9 77.3 reduce-scatter.5
  509.2 75.1 reduce-scatter.7
